TPU v7x, 256 devices: a whole 4x4x8 slice. The times are simulated.
256 devices in a mesh: face: 8 (over z_hi, x), patch: 32 (over z_lo, y, core).
Axes of the slice: x: 4, y: 4, z: 8 (z_hi: 2, z_lo: 4; z = z_hi * 4 + z_lo), core: 2. Of those that a mesh axis runs over, the one named last changes fastest.
Arguments:
- features: bfloat16 [32, 8, 131072], P(None, 'face', 'patch'), may hold values from -6 to 6
- film_first: float32 [2, 32], replicated, may hold values from -3 to 3
- weight_first: bfloat16 [32, 288], replicated, may hold values from -0.375 to 0.375
- film_second: float32 [2, 32], replicated, may hold values from -3 to 3
- weight_second: bfloat16 [64, 288], replicated, may hold values from -0.375 to 0.375
- film_third: float32 [2, 64], replicated, may hold values from -3 to 3
- weight_third: bfloat16 [128, 576], replicated, may hold values from -0.25 to 0.25
- film_fourth: float32 [2, 128], replicated, may hold values from -3 to 3
- weight_fourth: bfloat16 [128, 1152], replicated, may hold values from -0.1875 to 0.1875
- film_fifth: float32 [2, 192], replicated, may hold values from -3 to 3
- weight_fifth: bfloat16 [64, 1728], replicated, may hold values from -0.15625 to 0.15625
- film_sixth: float32 [2, 96], replicated, may hold values from -3 to 3
- weight_sixth: bfloat16 [32, 864], replicated, may hold values from -0.21875 to 0.21875
- link_patch: int32 [8, 32, 8], replicated, may hold values from 0 to 31, as said below
- link_shift: int32 [8, 32, 8], replicated, may hold values from -1 to 1, as said below
- link_turn: int32 [8, 32, 8], replicated, may hold values from 0 to 3, as said below
Outputs:
- denoised: bfloat16 [32, 8, 131072], P(None, 'face', 'patch')
Inputs may be any that keep to these rules, and one draw needn't show every extreme that they name: `link_patch`: patch p of a face sits at row p // 8 and column p % 8 of a 4 x 8 grid of patches. For a direction that stays inside that grid the entry is the grid neighbour. For a direction that leaves it the entry is a patch on the outer row or column of the neighbouring face's grid such that every cell that padded reads from it lies on that face's outer border. `link_shift`: 0 for a direction that stays inside the face's grid of patches, -1 or +1 for one that leaves it. `link_turn`: 0 for a direction that stays inside the face's grid of patches.
All inputs are finite; a program needn't handle non-finite values.
Results may differ from a plain program's by a relative error of at most 0.009.
Values may be sent and summed in bfloat16 or wider, within the bound.
No kernel may reach another device: no remote copies, remote signals or barrier semaphores. Data moves between devices by JAX's collectives and lax.ppermute only.
A program may use at most 128 MiB of HBM per device.

v0:
```python
import functools

import jax
import jax.numpy as jnp
import numpy as np
from jax import lax
from jax.experimental import pallas as pl
from jax.experimental.pallas import tpu as pltpu
from jax.sharding import PartitionSpec as P

EPSILON = 1e-05
FLOOR_SQUARE = 0.5
F32 = jnp.float32
BF16 = jnp.bfloat16
TAPS = [(u, v) for u in (-1, 0, 1) for v in (-1, 0, 1)]
FILM_ROWS = {1: (0, 32), 2: (32, 64), 3: (64, 128), 4: (128, 256), 5: (256, 448), 6: (448, 544)}
TURN_EDGE = np.array([[0, 1, 2, 3], [3, 2, 0, 1], [1, 0, 3, 2], [2, 3, 1, 0]])
TURN_FLIP = np.array([[0, 0, 0, 0], [0, 0, 1, 1], [1, 1, 1, 1], [1, 1, 0, 0]])
READ_EDGE = np.array([1, 0, 3, 2, 1, 1, 0, 0])
READ_END = np.array([0, 0, 0, 0, 1, 0, 1, 0])
CORNERS = [(4, 0), (5, 1), (6, 2), (7, 3)]
BLOCKS = {
    64: [[(0, 0), (1, 64)], [(2, 0), (3, 64)], CORNERS],
    32: [[(0, 0), (1, 32), (2, 64), (3, 96)], CORNERS],
    16: [[(0, 0), (1, 16), (2, 32), (3, 48), (4, 64), (5, 65), (6, 66), (7, 67)]],
}


def dot(a, b):
    return jnp.dot(a, b, preferred_element_type=F32)


def lanes_of(width):
    return lax.broadcasted_iota(jnp.int32, (1, width), 1)


def halves(x):
    high = x.astype(BF16)
    return high, (x - high.astype(F32)).astype(BF16)


def activate(values, film):
    mean_square = jnp.mean(values * values, axis=0, keepdims=True)
    if values.shape[0] >= 64:
        inverse = lax.rsqrt(mean_square + EPSILON)
    else:
        inverse = lax.rsqrt(jnp.maximum(mean_square, FLOOR_SQUARE))
    shaped = values * inverse * (1.0 + film[:, 0:1]) + film[:, 1:2]
    return (shaped / (1.0 + jnp.exp(-shaped))).astype(BF16)


def film_of(ref, index):
    first, last = FILM_ROWS[index]
    return ref[first:last, :]


def by_chunks(x, matrix):
    channels = x.shape[0]
    run = matrix.shape[0]
    count = x.shape[1] // run
    stacked = jnp.concatenate([x[:, run * k : run * (k + 1)] for k in range(count)], axis=0)
    high, low = halves(stacked)
    result = dot(high, matrix) + dot(low, matrix)
    return jnp.concatenate([result[channels * k : channels * (k + 1)] for k in range(count)], axis=1)


def frame_64(a, west_east_t):
    cells = a.shape[1]
    upper = jnp.where(lanes_of(128) < 64, a[:, :128].astype(F32), a[:, cells - 128 :].astype(F32))
    return jnp.concatenate([upper, dot(a, west_east_t)], axis=0).astype(BF16)


def frame_16(a, low_t, high_t):
    half = a.shape[0] // 2
    return (dot(a[:half], low_t) + dot(a[half:], high_t)).astype(BF16)


def halo_of(own, down, up, first, channels, blocks):
    rows = slice(first, first + channels * blocks)
    packed = own[rows, :].astype(F32) + down[rows, :].astype(F32) + up[rows, :].astype(F32)
    return jnp.concatenate([packed[channels * k : channels * (k + 1)] for k in range(blocks)], axis=1)


def expand(z, matrix):
    high, low = halves(z)
    both = dot(jnp.concatenate([high, low], axis=0), matrix)
    return both[: z.shape[0]] + both[z.shape[0] :]


def border_sums(halo, weight, length):
    products = dot(weight, halo)
    out_channels = weight.shape[0] // 9
    width = halo.shape[1]

    def tap(u, v):
        t = 3 * (u + 1) + v + 1
        return products[t * out_channels : (t + 1) * out_channels]

    lane = lanes_of(width)
    part = lane // length
    place = lane % length

    def along(step):
        return jnp.where(
            part == 0,
            tap(-1, step),
            jnp.where(part == 1, tap(1, step), jnp.where(part == 2, tap(step, -1), tap(step, 1))),
        )

    end = 4 * length
    corner = jnp.where(lane == end, tap(-1, -1), 0.0)
    corner = jnp.where(lane == end + 1, tap(-1, 1), corner)
    corner = jnp.where(lane == end + 2, tap(1, -1), corner)
    corner = jnp.where(lane == end + 3, tap(1, 1), corner)
    edge = part < 4
    before = jnp.where(edge & (place != 0), pltpu.roll(along(-1), 1, 1), 0.0)
    after = jnp.where(edge & (place != length - 1), pltpu.roll(along(1), width - 1, 1), 0.0)
    return jnp.where(edge, along(0), corner) + before + after


def with_halo_64(base, halo, weight, west_east, corner_map):
    sums = border_sums(halo, weight, 64)
    rows = sums[:, :128] + expand(sums[:, 256:], corner_map)
    total = base + expand(sums[:, 128:256], west_east)
    cells = total.shape[1]
    low = lanes_of(128) < 64
    top = total[:, :128] + jnp.where(low, rows, 0.0)
    bottom = total[:, cells - 128 :] + jnp.where(low, 0.0, rows)
    return jnp.concatenate([top, total[:, 128 : cells - 128], bottom], axis=1)


def with_halo(base, halo, weight, length, matrix):
    return base + expand(border_sums(halo, weight, length), matrix)


def main_kernel(a_ref, w_ref, out_ref, products, *, length):
    products[...] = dot(w_ref[...], a_ref[...])
    out_channels, cells = out_ref.shape
    lane = lanes_of(cells)
    place = lane % length

    def tap(u, v):
        t = 3 * (u + 1) + v + 1
        return products[t * out_channels : (t + 1) * out_channels, :]

    def column(v):
        above = jnp.where(lane < length, 0.0, pltpu.roll(tap(-1, v), length, 1))
        below = jnp.where(lane >= cells - length, 0.0, pltpu.roll(tap(1, v), cells - length, 1))
        return tap(0, v) + above + below

    total = column(0)
    total += jnp.where(place == 0, 0.0, pltpu.roll(column(-1), 1, 1))
    total += jnp.where(place == length - 1, 0.0, pltpu.roll(column(1), cells - 1, 1))
    out_ref[...] = total


def main_conv(a, weight, length):
    taps_out = weight.shape[0]
    cells = a.shape[1]
    return pl.pallas_call(
        functools.partial(main_kernel, length=length),
        out_shape=jax.ShapeDtypeStruct((taps_out // 9, cells), F32),
        scratch_shapes=[pltpu.VMEM((taps_out, cells), F32)],
        cost_estimate=pl.CostEstimate(
            flops=2 * taps_out * weight.shape[1] * cells * 8, bytes_accessed=a.size * 2 + taps_out * cells, transcendentals=0
        ),
        name="main_conv",
    )(a, weight)


def pick_kernel(code_ref, gathered, own_ref, up_ref, down_ref, *, specs):
    for target, (out, wanted) in enumerate(((own_ref, 1), (up_ref, 0), (down_ref, 2))):
        codes = [code_ref[target * 8 + d] for d in range(8)]
        row_out = 0
        row_in = 0
        for channels, length in specs:
            rows_in = channels * length // 32

            def frame(code):
                rows = gathered[code & 31, row_in : row_in + rows_in, :]
                if length == 64:
                    return jnp.concatenate([rows[:channels], rows[channels:]], axis=1)
                if length == 16:
                    low = lanes_of(128) < 64
                    wide = rows.astype(F32)
                    split = [jnp.where(low, wide, 0.0), jnp.where(low, 0.0, wide)]
                    return jnp.concatenate(split, axis=0).astype(BF16)
                return rows

            depth = 256 if length == 64 else 128
            source = lax.broadcasted_iota(jnp.int32, (depth, 128), 0)
            if length == 16:
                source = source & 63
            lane = lanes_of(128)
            for block in BLOCKS[length]:
                total = None
                for d, base in block:
                    code = codes[d]
                    edge = (code >> 5) & 3
                    flip = (code >> 7) & 1
                    active = (code >> 8) == wanted
                    start = edge * length + flip * (length - 1)
                    if d < 4:
                        target_cell = start + (1 - 2 * flip) * (lane - base)
                        inside = (lane >= base) & (lane < base + length)
                    else:
                        target_cell = start + jnp.zeros_like(lane)
                        inside = lane == base
                    target_cell = jnp.where(inside & active, target_cell, -1)
                    chosen = jnp.where(source == target_cell, 1.0, 0.0).astype(BF16)
                    piece = dot(frame(code), chosen)
                    total = piece if total is None else total + piece
                out[row_out : row_out + channels, :] = total.astype(BF16)
                row_out += channels
            row_in += rows_in


def pick(codes, gathered, specs):
    rows = sum(channels * len(BLOCKS[length]) for channels, length in specs)
    shape = jax.ShapeDtypeStruct((rows, 128), BF16)
    return pl.pallas_call(
        functools.partial(pick_kernel, specs=specs),
        out_shape=(shape, shape, shape),
        in_specs=[pl.BlockSpec(memory_space=pltpu.SMEM), pl.BlockSpec(memory_space=pltpu.VMEM)],
        name="pick",
    )(codes, gathered)


def call(kernel, shapes, *args, name):
    return pl.pallas_call(
        kernel,
        out_shape=tuple(jax.ShapeDtypeStruct(s, t) for s, t in shapes),
        name=name,
    )(*args)


def start_kernel(x_ref, film_ref, wet_ref, a_ref, frame_ref):
    a = activate(x_ref[...].astype(F32), film_of(film_ref, 1))
    a_ref[...] = a
    frame_ref[...] = frame_64(a, wet_ref[...])


def finish_1(base, x, own, down, up, w, we, cm, wet, c64, x32t, film, skip_ref, a_ref, frame_ref, skip_frame_ref):
    halo = halo_of(own, down, up, 0, 32, 3).astype(BF16)
    first = x[...].astype(F32) + with_halo_64(base[...], halo, w[...], we[...], cm[...])
    skip = first.astype(BF16)
    skip_ref[...] = skip
    a = activate(by_chunks(first, c64[...]), film_of(film, 2))
    a_ref[...] = a
    frame_ref[...] = dot(a, x32t[...]).astype(BF16)
    skip_frame_ref[...] = frame_64(skip, wet[...])


def finish_2(base, own, down, up, w, x32, c32, x32t, low_t, high_t, film, skip_ref, a_ref, frame_ref, skip_frame_ref):
    halo = halo_of(own, down, up, 0, 32, 2).astype(BF16)
    second = with_halo(base[...], halo, w[...], 32, x32[...])
    skip = second.astype(BF16)
    skip_ref[...] = skip
    a = activate(by_chunks(second, c32[...]), film_of(film, 3))
    a_ref[...] = a
    frame_ref[...] = frame_16(a, low_t[...], high_t[...])
    skip_frame_ref[...] = dot(skip, x32t[...]).astype(BF16)


def finish_3(base, own, down, up, w, x16, low_t, high_t, film, third_ref, a_ref, frame_ref):
    halo = halo_of(own, down, up, 0, 64, 1).astype(BF16)
    third = with_halo(base[...], halo, w[...], 16, x16[...])
    third_ref[...] = third
    a = activate(third, film_of(film, 4))
    a_ref[...] = a
    frame_ref[...] = frame_16(a, low_t[...], high_t[...])


def finish_4(base, third, own, down, up, w, x16, low_t, high_t, r32, skip, skip_frame, film, a_ref, frame_ref):
    halo = halo_of(own, down, up, 0, 128, 1).astype(BF16)
    fourth = third[...] + with_halo(base[...], halo, w[...], 16, x16[...])
    frame_ref[0:64, :] = frame_16(fourth.astype(BF16), low_t[...], high_t[...])
    frame_ref[64:128, :] = skip_frame[...]
    joined = jnp.concatenate([by_chunks(fourth, r32[...]), skip[...].astype(F32)], axis=0)
    a_ref[...] = activate(joined, film_of(film, 5))


def finish_5(base, own, down, up, w, x32, x32t, double, r64, skip, skip_frame, film, a_ref, frame_ref):
    coarse = dot(halo_of(own, down, up, 0, 128, 1).astype(BF16), double[...])
    halo = activate(jnp.concatenate([coarse, halo_of(own, down, up, 128, 64, 2)], axis=0), film_of(film, 5))
    fifth = with_halo(base[...], halo, w[...], 32, x32[...])
    frame_ref[0:64, :] = dot(fifth.astype(BF16), x32t[...]).astype(BF16)
    frame_ref[64:128, :] = skip_frame[...]
    joined = jnp.concatenate([by_chunks(fifth, r64[...]), skip[...].astype(F32)], axis=0)
    a_ref[...] = activate(joined, film_of(film, 6))


def finish_6(base, own, down, up, w, we, cm, double, skip, film, out_ref):
    coarse = dot(halo_of(own, down, up, 0, 64, 2).astype(BF16), double[...])
    halo = activate(jnp.concatenate([coarse, halo_of(own, down, up, 128, 32, 3)], axis=0), film_of(film, 6))
    total = with_halo_64(base[...], halo, w[...], we[...], cm[...])
    out_ref[...] = (skip[...].astype(F32) + total).astype(BF16)


def one_hot(targets, width):
    return (jnp.asarray(targets, jnp.int32)[:, None] == lax.broadcasted_iota(jnp.int32, (1, width), 1)).astype(BF16)


def border_targets(length, width):
    cells = length * length
    k = np.arange(length)
    targets = np.full(width, -1)
    edges = [k, cells - length + k, k * length, k * length + length - 1]
    targets[: 4 * length] = np.concatenate(edges)
    targets[4 * length : 4 * length + 4] = [0, length - 1, cells - length, cells - 1]
    return targets


def chunk_targets(length):
    lane = np.arange(512)
    return (lane // length // 2) * (length // 2) + (lane % length) // 2


def double_targets(length, width):
    targets = np.full(width, -1)
    lane = np.arange(4 * length)
    targets[: 4 * length] = (lane // length) * (length // 2) + (lane % length) // 2
    targets[4 * length : 4 * length + 4] = 2 * length + np.arange(4)
    return targets


def tap_rows(weight):
    out_channels = weight.shape[0]
    channels = weight.shape[1] // 9
    return weight.reshape(out_channels, 9, channels).transpose(1, 0, 2).reshape(9 * out_channels, channels)


def far_patch(patch):
    return (patch + 16) % 32


def face_moves(by):
    moves = []
    for face in range(8):
        jump = face % 4 == (3 if by == 1 else 0)
        for patch in range(32):
            moves.append((face * 32 + patch, (face + by) % 8 * 32 + (far_patch(patch) if jump else patch)))
    return moves


def link_codes(link_patch, link_shift, link_turn):
    edge_table = TURN_EDGE[:, READ_EDGE]
    flip_table = TURN_FLIP[:, READ_EDGE] ^ READ_END[None, :]
    packed = edge_table * 32 + flip_table * 128
    extra = jnp.full(link_turn.shape, 0, jnp.int32)
    for turn in range(4):
        extra = jnp.where(link_turn == turn, jnp.asarray(packed[turn], jnp.int32), extra)
    codes = link_patch + extra + (link_shift + 1) * 256
    face = lax.axis_index("face")
    patch = lax.axis_index("patch")
    up_patch = jnp.where(face % 4 == 3, far_patch(patch), patch)
    down_patch = jnp.where(face % 4 == 0, far_patch(patch), patch)
    flat = codes.reshape(256, 8)
    rows = [face * 32 + patch, (face + 1) % 8 * 32 + up_patch, (face + 7) % 8 * 32 + down_patch]
    return jnp.concatenate([lax.dynamic_slice(flat, (row, 0), (1, 8)) for row in rows], axis=0).reshape(24)


def body(
    features,
    film_first,
    weight_first,
    film_second,
    weight_second,
    film_third,
    weight_third,
    film_fourth,
    weight_fourth,
    film_fifth,
    weight_fifth,
    film_sixth,
    weight_sixth,
    link_patch,
    link_shift,
    link_turn,
):
    x = features[:, 0, :]
    film = jnp.concatenate([film_first, film_second, film_third, film_fourth, film_fifth, film_sixth], axis=1).T
    codes = link_codes(link_patch, link_shift, link_turn)
    w1, w2, w3, w4, w5, w6 = [
        tap_rows(w) for w in (weight_first, weight_second, weight_third, weight_fourth, weight_fifth, weight_sixth)
    ]
    k = np.arange(64)
    we = one_hot(np.concatenate([k * 64, k * 64 + 63]), 4096)
    wet = we.T
    cm = one_hot(np.concatenate([[0, 63, 64, 127], np.full(124, -1)]), 128)
    x32 = one_hot(border_targets(32, 256), 1024)
    x32t = one_hot(border_targets(32, 256)[:128], 1024).T
    x16 = one_hot(border_targets(16, 128), 256)
    edges16 = border_targets(16, 128)[:64]
    none16 = np.full(64, -1)
    low_t = one_hot(np.concatenate([edges16, none16]), 256).T
    high_t = one_hot(np.concatenate([none16, edges16]), 256).T
    r64 = one_hot(chunk_targets(64), 128).T
    r32 = one_hot(chunk_targets(32), 128).T
    c64 = one_hot(chunk_targets(64), 128) * jnp.asarray(0.25, BF16)
    c32 = one_hot(chunk_targets(32), 128) * jnp.asarray(0.25, BF16)
    double32 = one_hot(double_targets(32, 256), 128).T
    double64 = one_hot(double_targets(64, 384), 256).T
    above = face_moves(1)
    below = face_moves(-1)

    def exchange(frame, specs):
        copies = jnp.broadcast_to(frame[None], (32, *frame.shape))
        gathered = lax.all_to_all(copies, "patch", split_axis=0, concat_axis=0, tiled=True)
        own, for_up, for_down = pick(codes, gathered, specs)
        from_down = lax.ppermute(for_up, ("face", "patch"), above)
        from_up = lax.ppermute(for_down, ("face", "patch"), below)
        return own, from_down, from_up

    a1, f1 = call(start_kernel, [((32, 4096), BF16), ((64, 128), BF16)], x, film, wet, name="start")
    h = exchange(f1, ((32, 64),))
    base = main_conv(a1, w1, 64)
    skip_fine, a2, f2, fine_frame = call(
        finish_1,
        [((32, 4096), BF16), ((32, 1024), BF16), ((32, 128), BF16), ((64, 128), BF16)],
        base, x, *h, w1, we, cm, wet, c64, x32t, film,
        name="finish_1",
    )
    h = exchange(f2, ((32, 32),))
    base = main_conv(a2, w2, 32)
    skip_middle, a3, f3, middle_frame = call(
        finish_2,
        [((64, 1024), BF16), ((64, 256), BF16), ((32, 128), BF16), ((64, 128), BF16)],
        base, *h, w2, x32, c32, x32t, low_t, high_t, film,
        name="finish_2",
    )
    h = exchange(f3, ((64, 16),))
    base = main_conv(a3, w3, 16)
    third, a4, f4 = call(
        finish_3,
        [((128, 256), F32), ((128, 256), BF16), ((64, 128), BF16)],
        base, *h, w3, x16, low_t, high_t, film,
        name="finish_3",
    )
    h = exchange(f4, ((128, 16),))
    base = main_conv(a4, w4, 16)
    a5, f5 = call(
        finish_4,
        [((192, 1024), BF16), ((128, 128), BF16)],
        base, third, *h, w4, x16, low_t, high_t, r32, skip_middle, middle_frame, film,
        name="finish_4",
    )
    h = exchange(f5, ((128, 16), (64, 32)))
    base = main_conv(a5, w5, 32)
    a6, f6 = call(
        finish_5,
        [((96, 4096), BF16), ((128, 128), BF16)],
        base, *h, w5, x32, x32t, double32, r64, skip_fine, fine_frame, film,
        name="finish_5",
    )
    h = exchange(f6, ((64, 32), (32, 64)))
    base = main_conv(a6, w6, 64)
    (result,) = call(
        finish_6,
        [((32, 4096), BF16)],
        base, *h, w6, we, cm, double64, skip_fine, film,
        name="finish_6",
    )
    return result[:, None, :]


def solution(mesh):
    in_specs = (P(None, "face", "patch"),) + (P(),) * 15
    out_specs = P(None, "face", "patch")
    return jax.shard_map(body, mesh=mesh, in_specs=in_specs, out_specs=out_specs, check_vma=False)
```

profile of v0, /device:TPU:39, one launch (start us, length us, event | category | flops | bytes accessed | tf_op | source)
XLA Modules:
  0.0 254.2 jit_solution(11790294411431014319)
XLA Ops:
  0.0 0.8 concatenate.6
  0.8 0.9 copy.63
  1.7 1.9 fusion.wet_ref.wet
  3.6 2.4 start.1
  6.1 1.7 broadcast_in_dim.31
  7.8 9.2 %all-to-all-start = ((bf16[32,64,128]{2,1,0:T(8,128)(2,1)}), bf16[32,64,128]{2,1,0:T(8,128)(2,1)S(1)}, u32[]{:S(2)}, u32[]{:S(2)}) async-start(bf16[32,64,128]{2,1,0:T(8,128)(2,1)} %broadcast_in_dim.31), calls=%async_computation | async-start | bytes 1048576 | tf_op jit(solution)/shard_map/all_to_all | solution.py:409
  17.3 0.8 fusion.3.x32t
  21.3 1.3 fusion.1.we
  22.6 10.1 %all-to-all-done.gathered = bf16[32,64,128]{2,1,0:T(8,128)(2,1)S(1)} async-done(((bf16[32,64,128]{2,1,0:T(8,128)(2,1)}), bf16[32,64,128]{2,1,0:T(8,128)(2,1)S(1)}, u32[]{:S(2)}, u32[]{:S(2)}) %all-to-all-start) | async-done | bytes 524320 | tf_op jit(solution)/shard_map/all_to_all | solution.py:409
  32.7 0.8 copy-done.2
  33.5 2.0 pick.6
  35.6 2.9 %collective-permute-start = (bf16[96,128]{1,0:T(8,128)(2,1)}, bf16[96,128]{1,0:T(8,128)(2,1)S(1)}, u32[]{:S(2)}, u32[]{:S(2)}) collective-permute-start(bf16[96,128]{1,0:T(8,128)(2,1)} %get-tuple-element.43), channel_id=1, source_target_pairs={{0,32},{1,33},{2,34},{3,35},{4,36},{5,37},{6,38},{7,39},{8,40},{9,... | collective-permute-start | bytes 73736 | tf_op jit(solution)/shard_map/ppermute | solution.py:411
  38.4 3.1 %main_conv.6.base = f32[32,4096]{1,0:T(8,128)} custom-call(bf16[32,4096]{1,0:T(8,128)(2,1)} %get-tuple-element.40.a_ref, bf16[288,32]{1,0:T(8,128)(2,1)} %bitcast.49), custom_call_target="tpu_custom_call" | custom-call | flops 603979776 | bytes 1441792 | tf_op jit(solution)/shard_map/main_conv/pallas_call | solution.py:160
  41.5 4.7 %collective-permute-done.1.up = bf16[96,128]{1,0:T(8,128)(2,1)S(1)} collective-permute-done((bf16[96,128]{1,0:T(8,128)(2,1)}, bf16[96,128]{1,0:T(8,128)(2,1)S(1)}, u32[]{:S(2)}, u32[]{:S(2)}) %collective-permute-start.1) | collective-permute-done | bytes 24608 | tf_op jit(solution)/shard_map/ppermute | solution.py:412
  46.9 3.8 %finish_1.1 = (bf16[32,4096]{1,0:T(8,128)(2,1)}, bf16[32,1024]{1,0:T(8,128)(2,1)}, bf16[32,128]{1,0:T(8,128)(2,1)}, bf16[64,128]{1,0:T(8,128)(2,1)}) custom-call(f32[32,4096]{1,0:T(8,128)} %main_conv.6.base, bf16[32,4096]{1,0:T(8,128)(2,1)} %bitcast.41, bf16[96,128]{1,0:T(8,128)(2,1)} %get-tuple-element.42.own, bf16[96,128]{1,0:T(8,128)(2,1)} %copy-done.20, ...), custom_call_target="tpu_custom_call" | custom-call | tf_op jit(solution)/shard_map/finish_1/pallas_call | solution.py:230
  50.7 1.5 broadcast_in_dim.32
  52.1 5.9 %all-to-all-start.1 = ((bf16[32,32,128]{2,1,0:T(8,128)(2,1)}), bf16[32,32,128]{2,1,0:T(8,128)(2,1)S(1)}, u32[]{:S(2)}, u32[]{:S(2)}) async-start(bf16[32,32,128]{2,1,0:T(8,128)(2,1)} %broadcast_in_dim.32), calls=%async_computation.1 | async-start | bytes 524288 | tf_op jit(solution)/shard_map/all_to_all | solution.py:409
  58.9 0.8 copy.69
  59.7 0.8 fusion.6.c32
  60.5 0.9 fusion.2.x32
  61.4 6.8 %all-to-all-done.1.gathered = bf16[32,32,128]{2,1,0:T(8,128)(2,1)S(1)} async-done(((bf16[32,32,128]{2,1,0:T(8,128)(2,1)}), bf16[32,32,128]{2,1,0:T(8,128)(2,1)S(1)}, u32[]{:S(2)}, u32[]{:S(2)}) %all-to-all-start.1) | async-done | bytes 262176 | tf_op jit(solution)/shard_map/all_to_all | solution.py:409
  68.9 1.9 pick.7
  71.5 0.8 collective-permute-start.3
  72.3 2.4 main_conv.7.base
  74.7 3.9 %collective-permute-done.3.up = bf16[64,128]{1,0:T(8,128)(2,1)S(1)} collective-permute-done((bf16[64,128]{1,0:T(8,128)(2,1)}, bf16[64,128]{1,0:T(8,128)(2,1)S(1)}, u32[]{:S(2)}, u32[]{:S(2)}) %collective-permute-start.3) | collective-permute-done | bytes 16416 | tf_op jit(solution)/shard_map/ppermute | solution.py:412
  79.1 3.1 %finish_2.1 = (bf16[64,1024]{1,0:T(8,128)(2,1)}, bf16[64,256]{1,0:T(8,128)(2,1)}, bf16[32,128]{1,0:T(8,128)(2,1)}, bf16[64,128]{1,0:T(8,128)(2,1)}) custom-call(f32[64,1024]{1,0:T(8,128)} %main_conv.7.base, bf16[64,128]{1,0:T(8,128)(2,1)} %get-tuple-element.47.own, bf16[64,128]{1,0:T(8,128)(2,1)} %copy-done.23, bf16[64,128]{1,0:T(8,128)(2,1)} %copy-done.24, ...), custom_call_target="tpu_custom_call" | custom-call | tf_op jit(solution)/shard_map/finish_2/pallas_call | solution.py:230
  82.2 1.4 broadcast_in_dim.33
  83.7 6.4 %all-to-all-start.2 = ((bf16[32,32,128]{2,1,0:T(8,128)(2,1)}), bf16[32,32,128]{2,1,0:T(8,128)(2,1)S(1)}, u32[]{:S(2)}, u32[]{:S(2)}) async-start(bf16[32,32,128]{2,1,0:T(8,128)(2,1)} %broadcast_in_dim.33), calls=%async_computation.2 | async-start | bytes 524288 | tf_op jit(solution)/shard_map/all_to_all | solution.py:409
  90.1 0.9 copy.70
  91.7 8.6 %all-to-all-done.2.gathered = bf16[32,32,128]{2,1,0:T(8,128)(2,1)S(1)} async-done(((bf16[32,32,128]{2,1,0:T(8,128)(2,1)}), bf16[32,32,128]{2,1,0:T(8,128)(2,1)S(1)}, u32[]{:S(2)}, u32[]{:S(2)}) %all-to-all-start.2) | async-done | bytes 262176 | tf_op jit(solution)/shard_map/all_to_all | solution.py:409
  101.0 1.9 pick.8
  102.9 1.5 collective-permute-start.5
  104.4 2.1 main_conv.8.base
  106.5 3.4 %collective-permute-done.5.up = bf16[64,128]{1,0:T(8,128)(2,1)S(1)} collective-permute-done((bf16[64,128]{1,0:T(8,128)(2,1)}, bf16[64,128]{1,0:T(8,128)(2,1)S(1)}, u32[]{:S(2)}, u32[]{:S(2)}) %collective-permute-start.5) | collective-permute-done | bytes 16416 | tf_op jit(solution)/shard_map/ppermute | solution.py:412
  110.5 2.6 %finish_3.1 = (f32[128,256]{1,0:T(8,128)}, bf16[128,256]{1,0:T(8,128)(2,1)}, bf16[64,128]{1,0:T(8,128)(2,1)}) custom-call(f32[128,256]{1,0:T(8,128)} %main_conv.8.base, bf16[64,128]{1,0:T(8,128)(2,1)} %get-tuple-element.52.own, bf16[64,128]{1,0:T(8,128)(2,1)} %copy-done.25, bf16[64,128]{1,0:T(8,128)(2,1)} %copy-done.26, bf16[1152,64]{1,0:T(8,128)(2,1)} %bitcast.39, ...), custom_call_target="tpu_custom_call" | custom-call | tf_op jit(solution)/shard_map/finish_3/pallas_call | solution.py:230
  113.1 1.6 broadcast_in_dim.34
  114.8 6.4 %all-to-all-start.3 = ((bf16[32,64,128]{2,1,0:T(8,128)(2,1)}), bf16[32,64,128]{2,1,0:T(8,128)(2,1)S(1)}, u32[]{:S(2)}, u32[]{:S(2)}) async-start(bf16[32,64,128]{2,1,0:T(8,128)(2,1)} %broadcast_in_dim.34), calls=%async_computation.3 | async-start | bytes 1048576 | tf_op jit(solution)/shard_map/all_to_all | solution.py:409
  121.4 0.9 copy.72
  123.0 13.9 %all-to-all-done.3.gathered = bf16[32,64,128]{2,1,0:T(8,128)(2,1)S(1)} async-done(((bf16[32,64,128]{2,1,0:T(8,128)(2,1)}), bf16[32,64,128]{2,1,0:T(8,128)(2,1)S(1)}, u32[]{:S(2)}, u32[]{:S(2)}) %all-to-all-start.3) | async-done | bytes 524320 | tf_op jit(solution)/shard_map/all_to_all | solution.py:409
  136.9 0.8 copy-done.3
  137.7 2.1 pick.9
  139.7 1.5 collective-permute-start.7
  141.2 2.2 main_conv.9.base
  143.4 3.5 %collective-permute-done.7.up = bf16[128,128]{1,0:T(8,128)(2,1)S(1)} collective-permute-done((bf16[128,128]{1,0:T(8,128)(2,1)}, bf16[128,128]{1,0:T(8,128)(2,1)S(1)}, u32[]{:S(2)}, u32[]{:S(2)}) %collective-permute-start.7) | collective-permute-done | bytes 32800 | tf_op jit(solution)/shard_map/ppermute | solution.py:412
  147.5 3.2 %finish_4.1 = (bf16[192,1024]{1,0:T(8,128)(2,1)}, bf16[128,128]{1,0:T(8,128)(2,1)}) custom-call(f32[128,256]{1,0:T(8,128)} %main_conv.9.base, f32[128,256]{1,0:T(8,128)} %get-tuple-element.56.third, bf16[128,128]{1,0:T(8,128)(2,1)} %get-tuple-element.58.own, bf16[128,128]{1,0:T(8,128)(2,1)} %copy-done.15, bf16[128,128]{1,0:T(8,128)(2,1)} %copy-done.16, ...), custom_call_target="tpu_custom_call" | custom-call | tf_op jit(solution)/shard_map/finish_4/pallas_call | solution.py:230
  150.7 2.0 broadcast_in_dim.35
  152.7 6.4 %all-to-all-start.4 = ((bf16[32,128,128]{2,1,0:T(8,128)(2,1)}), bf16[32,128,128]{2,1,0:T(8,128)(2,1)S(1)}, u32[]{:S(2)}, u32[]{:S(2)}) async-start(bf16[32,128,128]{2,1,0:T(8,128)(2,1)} %broadcast_in_dim.35), calls=%async_computation.4 | async-start | bytes 2097152 | tf_op jit(solution)/shard_map/all_to_all | solution.py:409
  159.5 0.8 copy.73
  161.7 24.2 %all-to-all-done.4.gathered = bf16[32,128,128]{2,1,0:T(8,128)(2,1)S(1)} async-done(((bf16[32,128,128]{2,1,0:T(8,128)(2,1)}), bf16[32,128,128]{2,1,0:T(8,128)(2,1)S(1)}, u32[]{:S(2)}, u32[]{:S(2)}) %all-to-all-start.4) | async-done | bytes 1048608 | tf_op jit(solution)/shard_map/all_to_all | solution.py:409
  185.9 1.0 copy-done
  186.9 2.4 pick.10
  189.3 1.5 collective-permute-start.9
  190.8 2.6 %main_conv.10.base = f32[64,1024]{1,0:T(8,128)} custom-call(bf16[192,1024]{1,0:T(8,128)(2,1)} %get-tuple-element.63.a_ref, bf16[576,192]{1,0:T(8,128)(2,1)} %bitcast.33), custom_call_target="tpu_custom_call" | custom-call | flops 1811939328 | bytes 983040 | tf_op jit(solution)/shard_map/main_conv/pallas_call | solution.py:160
  193.3 5.4 %collective-permute-done.9.up = bf16[256,128]{1,0:T(8,128)(2,1)S(1)} collective-permute-done((bf16[256,128]{1,0:T(8,128)(2,1)}, bf16[256,128]{1,0:T(8,128)(2,1)S(1)}, u32[]{:S(2)}, u32[]{:S(2)}) %collective-permute-start.9) | collective-permute-done | bytes 65568 | tf_op jit(solution)/shard_map/ppermute | solution.py:412
  199.4 4.3 %finish_5.1 = (bf16[96,4096]{1,0:T(8,128)(2,1)}, bf16[128,128]{1,0:T(8,128)(2,1)}) custom-call(f32[64,1024]{1,0:T(8,128)} %main_conv.10.base, bf16[256,128]{1,0:T(8,128)(2,1)} %get-tuple-element.65.own, bf16[256,128]{1,0:T(8,128)(2,1)} %copy-done.9, bf16[256,128]{1,0:T(8,128)(2,1)} %copy-done.10, bf16[576,192]{1,0:T(8,128)(2,1)} %bitcast.34, ...), custom_call_target="tpu_custom_call" | custom-call | tf_op jit(solution)/shard_map/finish_5/pallas_call | solution.py:230
  203.7 2.0 broadcast_in_dim.36
  205.6 5.3 %all-to-all-start.5 = ((bf16[32,128,128]{2,1,0:T(8,128)(2,1)}), bf16[32,128,128]{2,1,0:T(8,128)(2,1)S(1)}, u32[]{:S(2)}, u32[]{:S(2)}) async-start(bf16[32,128,128]{2,1,0:T(8,128)(2,1)} %broadcast_in_dim.36), calls=%async_computation.5 | async-start | bytes 2097152 | tf_op jit(solution)/shard_map/all_to_all | solution.py:409
  212.5 25.3 %all-to-all-done.5.gathered = bf16[32,128,128]{2,1,0:T(8,128)(2,1)S(1)} async-done(((bf16[32,128,128]{2,1,0:T(8,128)(2,1)}), bf16[32,128,128]{2,1,0:T(8,128)(2,1)S(1)}, u32[]{:S(2)}, u32[]{:S(2)}) %all-to-all-start.5) | async-done | bytes 1048608 | tf_op jit(solution)/shard_map/all_to_all | solution.py:409
  237.8 1.0 copy-done.1
  238.7 2.5 pick.11
  241.2 1.5 collective-permute-start.11
  242.7 3.3 %main_conv.11.base = f32[32,4096]{1,0:T(8,128)} custom-call(bf16[96,4096]{1,0:T(8,128)(2,1)} %get-tuple-element.70.a_ref, bf16[288,96]{1,0:T(8,128)(2,1)} %bitcast.45), custom_call_target="tpu_custom_call" | custom-call | flops 1811939328 | bytes 1966080 | tf_op jit(solution)/shard_map/main_conv/pallas_call | solution.py:160
  246.0 4.3 %collective-permute-done.11.up = bf16[224,128]{1,0:T(8,128)(2,1)S(1)} collective-permute-done((bf16[224,128]{1,0:T(8,128)(2,1)}, bf16[224,128]{1,0:T(8,128)(2,1)S(1)}, u32[]{:S(2)}, u32[]{:S(2)}) %collective-permute-start.11) | collective-permute-done | bytes 57376 | tf_op jit(solution)/shard_map/ppermute | solution.py:412
  251.0 3.2 %finish_6.1 = bf16[32,4096]{1,0:T(8,128)(2,1)} custom-call(f32[32,4096]{1,0:T(8,128)} %main_conv.11.base, bf16[224,128]{1,0:T(8,128)(2,1)} %get-tuple-element.72.own, bf16[224,128]{1,0:T(8,128)(2,1)} %copy-done.12, bf16[224,128]{1,0:T(8,128)(2,1)} %copy-done.13, bf16[288,96]{1,0:T(8,128)(2,1)} %bitcast.46, bf16[128,4096]{1,0:T(8,128)(2,1)} %fusion.1.we, ...), custom_call_target="tpu_custom_call" | custom-call | tf_op jit(solution)/shard_map/finish_6/pallas_call | solution.py:230
  (114 shorter events, 14.8 us)
Async XLA Ops:
  6.0 11.1 %copy-start.17 = (s32[8,32,8]{1,2,0:T(8,128)S(1)}, s32[8,32,8]{1,2,0:T(8,128)}, u32[]{:S(2)}) copy-start(s32[8,32,8]{1,2,0:T(8,128)} %param.47) | copy-start | bytes 24580
  6.0 11.1 %copy-start.18 = (s32[8,32,8]{1,2,0:T(8,128)S(1)}, s32[8,32,8]{1,2,0:T(8,128)}, u32[]{:S(2)}) copy-start(s32[8,32,8]{1,2,0:T(8,128)} %param.46) | copy-start | bytes 24580
  6.0 11.1 %copy-start.19 = (s32[8,32,8]{1,2,0:T(8,128)S(1)}, s32[8,32,8]{1,2,0:T(8,128)}, u32[]{:S(2)}) copy-start(s32[8,32,8]{1,2,0:T(8,128)} %param.48) | copy-start | bytes 24580
  6.0 11.1 %copy-start.38 = (s32[8]{0:T(128)S(1)}, s32[8]{0:T(128)}, u32[]{:S(2)}) copy-start(s32[8]{0:T(128)} %constant.100.clone) | copy-start | bytes 100
  6.0 11.1 %copy-start.39 = (s32[8]{0:T(128)S(1)}, s32[8]{0:T(128)}, u32[]{:S(2)}) copy-start(s32[8]{0:T(128)} %constant.101.clone) | copy-start | bytes 100
  6.0 11.1 %copy-start.40 = (s32[8]{0:T(128)S(1)}, s32[8]{0:T(128)}, u32[]{:S(2)}) copy-start(s32[8]{0:T(128)} %constant.102.clone) | copy-start | bytes 100
  6.0 11.1 %copy-start.41 = (s32[8]{0:T(128)S(1)}, s32[8]{0:T(128)}, u32[]{:S(2)}) copy-start(s32[8]{0:T(128)} %constant.103.clone) | copy-start | bytes 100
  6.1 11.3 %copy-start.37 = (s32[128]{0:T(128)S(1)}, s32[128]{0:T(128)}, u32[]{:S(2)}) copy-start(s32[128]{0:T(128)} %constant.107.clone) | copy-start | bytes 1540
  6.1 12.1 %copy-start.36 = (s32[128]{0:T(128)S(1)}, s32[128]{0:T(128)}, u32[]{:S(2)}) copy-start(s32[128]{0:T(128)} %constant.105.clone) | copy-start | bytes 1540
  6.1 12.8 %copy-start.27 = (s32[512]{0:T(512)S(1)}, s32[512]{0:T(512)}, u32[]{:S(2)}) copy-start(s32[512]{0:T(512)} %constant.111.clone) | copy-start | bytes 6148
  7.8 12.7 %copy-start.22 = (bf16[32,288]{1,0:T(8,128)(2,1)S(1)}, bf16[32,288]{1,0:T(8,128)(2,1)}, u32[]{:S(2)}) copy-start(bf16[32,288]{1,0:T(8,128)(2,1)} %param.35) | copy-start | bytes 55300
  7.8 13.5 %copy-start.30 = (s32[128]{0:T(128)S(1)}, s32[128]{0:T(128)}, u32[]{:S(2)}) copy-start(s32[128]{0:T(128)} %constant.104.clone) | copy-start | bytes 1540
  7.8 24.9 %all-to-all-start = ((bf16[32,64,128]{2,1,0:T(8,128)(2,1)}), bf16[32,64,128]{2,1,0:T(8,128)(2,1)S(1)}, u32[]{:S(2)}, u32[]{:S(2)}) async-start(bf16[32,64,128]{2,1,0:T(8,128)(2,1)} %broadcast_in_dim.31), calls=%async_computation | async-start | bytes 1048576 | tf_op jit(solution)/shard_map/all_to_all | solution.py:409
  32.7 0.8 copy-start.2
  35.6 6.0 %collective-permute-start = (bf16[96,128]{1,0:T(8,128)(2,1)}, bf16[96,128]{1,0:T(8,128)(2,1)S(1)}, u32[]{:S(2)}, u32[]{:S(2)}) collective-permute-start(bf16[96,128]{1,0:T(8,128)(2,1)} %get-tuple-element.43), channel_id=1, source_target_pairs={{0,32},{1,33},{2,34},{3,35},{4,36},{5,37},{6,38},{7,39},{8,40},{9,... | collective-permute-start | bytes 73736 | tf_op jit(solution)/shard_map/ppermute | solution.py:411
  38.4 7.8 %collective-permute-start.1 = (bf16[96,128]{1,0:T(8,128)(2,1)}, bf16[96,128]{1,0:T(8,128)(2,1)S(1)}, u32[]{:S(2)}, u32[]{:S(2)}) collective-permute-start(bf16[96,128]{1,0:T(8,128)(2,1)} %get-tuple-element.44), channel_id=1, source_target_pairs={{0,240},{1,241},{2,242},{3,243},{4,244},{5,245},{6,246},{7,247},{8... | collective-permute-start | bytes 73736 | tf_op jit(solution)/shard_map/ppermute | solution.py:412
  41.5 4.7 %copy-start.20 = (bf16[96,128]{1,0:T(8,128)(2,1)}, bf16[96,128]{1,0:T(8,128)(2,1)S(1)}, u32[]{:S(2)}) copy-start(bf16[96,128]{1,0:T(8,128)(2,1)S(1)} %collective-permute-done.down) | copy-start | bytes 73732
  46.3 0.6 copy-start.21
  46.9 11.2 %copy-start.34 = (s32[128]{0:T(128)S(1)}, s32[128]{0:T(128)}, u32[]{:S(2)}) copy-start(s32[128]{0:T(128)} %constant.109.clone) | copy-start | bytes 1540
  46.9 11.2 %copy-start.35 = (s32[128]{0:T(128)S(1)}, s32[128]{0:T(128)}, u32[]{:S(2)}) copy-start(s32[128]{0:T(128)} %constant.110.clone) | copy-start | bytes 1540
  46.9 11.9 %copy-start.14 = (bf16[64,288]{1,0:T(8,128)(2,1)S(1)}, bf16[64,288]{1,0:T(8,128)(2,1)}, u32[]{:S(2)}) copy-start(bf16[64,288]{1,0:T(8,128)(2,1)} %param.37) | copy-start | bytes 110596
  50.7 9.0 %copy-start.28 = (s32[512]{0:T(512)S(1)}, s32[512]{0:T(512)}, u32[]{:S(2)}) copy-start(s32[512]{0:T(512)} %constant.112.clone) | copy-start | bytes 6148
  50.7 9.8 %copy-start.32 = (s32[256]{0:T(256)S(1)}, s32[256]{0:T(256)}, u32[]{:S(2)}) copy-start(s32[256]{0:T(256)} %constant.106.clone) | copy-start | bytes 3076
  52.1 16.1 %all-to-all-start.1 = ((bf16[32,32,128]{2,1,0:T(8,128)(2,1)}), bf16[32,32,128]{2,1,0:T(8,128)(2,1)S(1)}, u32[]{:S(2)}, u32[]{:S(2)}) async-start(bf16[32,32,128]{2,1,0:T(8,128)(2,1)} %broadcast_in_dim.32), calls=%async_computation.1 | async-start | bytes 524288 | tf_op jit(solution)/shard_map/all_to_all | solution.py:409
  68.2 0.7 copy-start.4
  70.8 3.9 %collective-permute-start.2 = (bf16[64,128]{1,0:T(8,128)(2,1)}, bf16[64,128]{1,0:T(8,128)(2,1)S(1)}, u32[]{:S(2)}, u32[]{:S(2)}) collective-permute-start(bf16[64,128]{1,0:T(8,128)(2,1)} %get-tuple-element.48), channel_id=1, source_target_pairs={{0,32},{1,33},{2,34},{3,35},{4,36},{5,37},{6,38},{7,39},{8,40},{9,... | collective-permute-start | bytes 49160 | tf_op jit(solution)/shard_map/ppermute | solution.py:411
  71.5 7.0 %collective-permute-start.3 = (bf16[64,128]{1,0:T(8,128)(2,1)}, bf16[64,128]{1,0:T(8,128)(2,1)S(1)}, u32[]{:S(2)}, u32[]{:S(2)}) collective-permute-start(bf16[64,128]{1,0:T(8,128)(2,1)} %get-tuple-element.49), channel_id=1, source_target_pairs={{0,240},{1,241},{2,242},{3,243},{4,244},{5,245},{6,246},{7,247},{8... | collective-permute-start | bytes 49160 | tf_op jit(solution)/shard_map/ppermute | solution.py:412
  74.7 3.9 %copy-start.23 = (bf16[64,128]{1,0:T(8,128)(2,1)}, bf16[64,128]{1,0:T(8,128)(2,1)S(1)}, u32[]{:S(2)}) copy-start(bf16[64,128]{1,0:T(8,128)(2,1)S(1)} %collective-permute-done.2.down) | copy-start | bytes 49156
  78.5 0.6 copy-start.24
  79.1 10.9 %copy-start.8 = (bf16[128,576]{0,1:T(8,128)(2,1)S(1)}, bf16[128,576]{0,1:T(8,128)(2,1)}, u32[]{:S(2)}) copy-start(bf16[128,576]{0,1:T(8,128)(2,1)} %param.39) | copy-start | bytes 442372
  82.2 8.8 %copy-start.33 = (s32[128]{0:T(128)S(1)}, s32[128]{0:T(128)}, u32[]{:S(2)}) copy-start(s32[128]{0:T(128)} %constant.108.clone) | copy-start | bytes 1540
  83.7 16.6 %all-to-all-start.2 = ((bf16[32,32,128]{2,1,0:T(8,128)(2,1)}), bf16[32,32,128]{2,1,0:T(8,128)(2,1)S(1)}, u32[]{:S(2)}, u32[]{:S(2)}) async-start(bf16[32,32,128]{2,1,0:T(8,128)(2,1)} %broadcast_in_dim.33), calls=%async_computation.2 | async-start | bytes 524288 | tf_op jit(solution)/shard_map/all_to_all | solution.py:409
  100.3 0.7 copy-start.5
  102.9 3.6 %collective-permute-start.4 = (bf16[64,128]{1,0:T(8,128)(2,1)}, bf16[64,128]{1,0:T(8,128)(2,1)S(1)}, u32[]{:S(2)}, u32[]{:S(2)}) collective-permute-start(bf16[64,128]{1,0:T(8,128)(2,1)} %get-tuple-element.53), channel_id=1, source_target_pairs={{0,32},{1,33},{2,34},{3,35},{4,36},{5,37},{6,38},{7,39},{8,40},{9,... | collective-permute-start | bytes 49160 | tf_op jit(solution)/shard_map/ppermute | solution.py:411
  102.9 7.0 %collective-permute-start.5 = (bf16[64,128]{1,0:T(8,128)(2,1)}, bf16[64,128]{1,0:T(8,128)(2,1)S(1)}, u32[]{:S(2)}, u32[]{:S(2)}) collective-permute-start(bf16[64,128]{1,0:T(8,128)(2,1)} %get-tuple-element.54), channel_id=1, source_target_pairs={{0,240},{1,241},{2,242},{3,243},{4,244},{5,245},{6,246},{7,247},{8... | collective-permute-start | bytes 49160 | tf_op jit(solution)/shard_map/ppermute | solution.py:412
  106.5 3.4 %copy-start.25 = (bf16[64,128]{1,0:T(8,128)(2,1)}, bf16[64,128]{1,0:T(8,128)(2,1)S(1)}, u32[]{:S(2)}) copy-start(bf16[64,128]{1,0:T(8,128)(2,1)S(1)} %collective-permute-done.4.down) | copy-start | bytes 49156
  109.9 0.6 copy-start.26
  110.5 10.6 %copy-start.6 = (bf16[128,1152]{1,0:T(8,128)(2,1)S(1)}, bf16[128,1152]{1,0:T(8,128)(2,1)}, u32[]{:S(2)}) copy-start(bf16[128,1152]{1,0:T(8,128)(2,1)} %param.41) | copy-start | bytes 884740
  114.8 22.1 %all-to-all-start.3 = ((bf16[32,64,128]{2,1,0:T(8,128)(2,1)}), bf16[32,64,128]{2,1,0:T(8,128)(2,1)S(1)}, u32[]{:S(2)}, u32[]{:S(2)}) async-start(bf16[32,64,128]{2,1,0:T(8,128)(2,1)} %broadcast_in_dim.34), calls=%async_computation.3 | async-start | bytes 1048576 | tf_op jit(solution)/shard_map/all_to_all | solution.py:409
  136.9 0.8 copy-start.3
  139.7 3.6 %collective-permute-start.6 = (bf16[128,128]{1,0:T(8,128)(2,1)}, bf16[128,128]{1,0:T(8,128)(2,1)S(1)}, u32[]{:S(2)}, u32[]{:S(2)}) collective-permute-start(bf16[128,128]{1,0:T(8,128)(2,1)} %get-tuple-element.59), channel_id=1, source_target_pairs={{0,32},{1,33},{2,34},{3,35},{4,36},{5,37},{6,38},{7,39},{8,40},{9,... | collective-permute-start | bytes 98312 | tf_op jit(solution)/shard_map/ppermute | solution.py:411
  139.7 7.2 %collective-permute-start.7 = (bf16[128,128]{1,0:T(8,128)(2,1)}, bf16[128,128]{1,0:T(8,128)(2,1)S(1)}, u32[]{:S(2)}, u32[]{:S(2)}) collective-permute-start(bf16[128,128]{1,0:T(8,128)(2,1)} %get-tuple-element.60), channel_id=1, source_target_pairs={{0,240},{1,241},{2,242},{3,243},{4,244},{5,245},{6,246},{7,247},{8... | collective-permute-start | bytes 98312 | tf_op jit(solution)/shard_map/ppermute | solution.py:412
  143.4 3.6 %copy-start.15 = (bf16[128,128]{1,0:T(8,128)(2,1)}, bf16[128,128]{1,0:T(8,128)(2,1)S(1)}, u32[]{:S(2)}) copy-start(bf16[128,128]{1,0:T(8,128)(2,1)S(1)} %collective-permute-done.6.down) | copy-start | bytes 98308
  146.9 0.6 copy-start.16
  152.7 6.5 %copy-start.7 = (bf16[64,1728]{1,0:T(8,128)(2,1)S(1)}, bf16[64,1728]{1,0:T(8,128)(2,1)}, u32[]{:S(2)}) copy-start(bf16[64,1728]{1,0:T(8,128)(2,1)} %param.43) | copy-start | bytes 663556
  152.7 33.2 %all-to-all-start.4 = ((bf16[32,128,128]{2,1,0:T(8,128)(2,1)}), bf16[32,128,128]{2,1,0:T(8,128)(2,1)S(1)}, u32[]{:S(2)}, u32[]{:S(2)}) async-start(bf16[32,128,128]{2,1,0:T(8,128)(2,1)} %broadcast_in_dim.35), calls=%async_computation.4 | async-start | bytes 2097152 | tf_op jit(solution)/shard_map/all_to_all | solution.py:409
  159.1 1.2 copy-start.31
  185.9 1.0 copy-start
  189.3 4.0 %collective-permute-start.8 = (bf16[256,128]{1,0:T(8,128)(2,1)}, bf16[256,128]{1,0:T(8,128)(2,1)S(1)}, u32[]{:S(2)}, u32[]{:S(2)}) collective-permute-start(bf16[256,128]{1,0:T(8,128)(2,1)} %get-tuple-element.66), channel_id=1, source_target_pairs={{0,32},{1,33},{2,34},{3,35},{4,36},{5,37},{6,38},{7,39},{8,40},{9,... | collective-permute-start | bytes 196616 | tf_op jit(solution)/shard_map/ppermute | solution.py:411
  189.3 9.5 %collective-permute-start.9 = (bf16[256,128]{1,0:T(8,128)(2,1)}, bf16[256,128]{1,0:T(8,128)(2,1)S(1)}, u32[]{:S(2)}, u32[]{:S(2)}) collective-permute-start(bf16[256,128]{1,0:T(8,128)(2,1)} %get-tuple-element.67), channel_id=1, source_target_pairs={{0,240},{1,241},{2,242},{3,243},{4,244},{5,245},{6,246},{7,247},{8... | collective-permute-start | bytes 196616 | tf_op jit(solution)/shard_map/ppermute | solution.py:412
  193.3 5.5 %copy-start.9 = (bf16[256,128]{1,0:T(8,128)(2,1)}, bf16[256,128]{1,0:T(8,128)(2,1)S(1)}, u32[]{:S(2)}) copy-start(bf16[256,128]{1,0:T(8,128)(2,1)S(1)} %collective-permute-done.8.down) | copy-start | bytes 196612
  198.8 0.6 copy-start.10
  205.6 5.4 %copy-start.11 = (bf16[32,864]{1,0:T(8,128)(2,1)S(1)}, bf16[32,864]{1,0:T(8,128)(2,1)}, u32[]{:S(2)}) copy-start(bf16[32,864]{1,0:T(8,128)(2,1)} %param.45) | copy-start | bytes 165892
  205.6 6.1 %copy-start.29 = (s32[384]{0:T(512)S(1)}, s32[384]{0:T(512)}, u32[]{:S(2)}) copy-start(s32[384]{0:T(512)} %constant.114.clone) | copy-start | bytes 4612
  205.6 32.1 %all-to-all-start.5 = ((bf16[32,128,128]{2,1,0:T(8,128)(2,1)}), bf16[32,128,128]{2,1,0:T(8,128)(2,1)S(1)}, u32[]{:S(2)}, u32[]{:S(2)}) async-start(bf16[32,128,128]{2,1,0:T(8,128)(2,1)} %broadcast_in_dim.36), calls=%async_computation.5 | async-start | bytes 2097152 | tf_op jit(solution)/shard_map/all_to_all | solution.py:409
  237.8 1.0 copy-start.1
  241.2 4.8 %collective-permute-start.10 = (bf16[224,128]{1,0:T(8,128)(2,1)}, bf16[224,128]{1,0:T(8,128)(2,1)S(1)}, u32[]{:S(2)}, u32[]{:S(2)}) collective-permute-start(bf16[224,128]{1,0:T(8,128)(2,1)} %get-tuple-element.73), channel_id=1, source_target_pairs={{0,32},{1,33},{2,34},{3,35},{4,36},{5,37},{6,38},{7,39},{8,40},{9,... | collective-permute-start | bytes 172040 | tf_op jit(solution)/shard_map/ppermute | solution.py:411
  241.2 9.1 %collective-permute-start.11 = (bf16[224,128]{1,0:T(8,128)(2,1)}, bf16[224,128]{1,0:T(8,128)(2,1)S(1)}, u32[]{:S(2)}, u32[]{:S(2)}) collective-permute-start(bf16[224,128]{1,0:T(8,128)(2,1)} %get-tuple-element.74), channel_id=1, source_target_pairs={{0,240},{1,241},{2,242},{3,243},{4,244},{5,245},{6,246},{7,247},{8... | collective-permute-start | bytes 172040 | tf_op jit(solution)/shard_map/ppermute | solution.py:412
  246.0 4.4 %copy-start.12 = (bf16[224,128]{1,0:T(8,128)(2,1)}, bf16[224,128]{1,0:T(8,128)(2,1)S(1)}, u32[]{:S(2)}) copy-start(bf16[224,128]{1,0:T(8,128)(2,1)S(1)} %collective-permute-done.10.down) | copy-start | bytes 172036
  250.4 0.6 copy-start.13
where the time goes:
time: 256 us; the launch traced here: 254 us
  waiting for transfers between devices  114 us (45%)
  Pallas kernels  51 us (20%)
  starting transfers between devices  49.9 us (19%)
  local copies, waits for them, and re-layouts  27.2 us (11%)
  other arithmetic  11.4 us (4%)
    all_to_all x6, waiting for transfers between devices, exchange(): lax.all_to_all(copies, 'patch', split_axis=0, concat_axis=0, tiled=True)  88.9 us
    all_to_all x6, starting transfers between devices, exchange(): lax.all_to_all(copies, 'patch', split_axis=0, concat_axis=0, tiled=True)  39.7 us
    ppermute x6, waiting for transfers between devices, exchange(): from_up = lax.ppermute(for_down, ('face', 'patch'), below)  25.3 us
    pallas_call x7, Pallas kernels, call(): pl.pallas_call(kernel, out_shape=tuple((jax.ShapeDtypeStruct(s, t) for s,...  22.4 us
    pallas_call x6, Pallas kernels, main_conv(): pl.pallas_call(functools.partial(main_kernel, length=length), out_shape=j...  15.7 us
    pallas_call x6, Pallas kernels, pick(): pl.pallas_call(functools.partial(pick_kernel, specs=specs), out_shape=(sh...  12.8 us
    broadcast_in_dim x6, local copies, waits for them, and re-layouts, exchange(): copies = jnp.broadcast_to(frame[None], (32, *frame.shape))  10.2 us
    convert_element_type x11, other arithmetic, one_hot(): (jnp.asarray(targets, jnp.int32)[:, None] == lax.broadcasted_iota(jnp.int...  9.73 us
  transfers between devices with their start and end apart: 18, of which 12 were waited for; matrix products, arithmetic and copies ran while one was open for 6% of the time, Pallas kernels for 6%

commit v1 on v0

--- a/solution.py
+++ b/solution.py
@@ -12,7 +12,7 @@
 FLOOR_SQUARE = 0.5
 F32 = jnp.float32
 BF16 = jnp.bfloat16
-TAPS = [(u, v) for u in (-1, 0, 1) for v in (-1, 0, 1)]
+LIMIT = pltpu.CompilerParams(vmem_limit_bytes=24 * 1024 * 1024)
 FILM_ROWS = {1: (0, 32), 2: (32, 64), 3: (64, 128), 4: (128, 256), 5: (256, 448), 6: (448, 544)}
 TURN_EDGE = np.array([[0, 1, 2, 3], [3, 2, 0, 1], [1, 0, 3, 2], [2, 3, 1, 0]])
 TURN_FLIP = np.array([[0, 0, 0, 0], [0, 0, 1, 1], [1, 1, 1, 1], [1, 1, 0, 0]])
@@ -30,6 +30,10 @@
     return jnp.dot(a, b, preferred_element_type=F32)
 
 
+def in_vmem(x):
+    return pltpu.with_memory_space_constraint(x, pltpu.VMEM)
+
+
 def lanes_of(width):
     return lax.broadcasted_iota(jnp.int32, (1, width), 1)
 
@@ -67,12 +71,43 @@
 def frame_64(a, west_east_t):
     cells = a.shape[1]
     upper = jnp.where(lanes_of(128) < 64, a[:, :128].astype(F32), a[:, cells - 128 :].astype(F32))
-    return jnp.concatenate([upper, dot(a, west_east_t)], axis=0).astype(BF16)
-
-
-def frame_16(a, low_t, high_t):
-    half = a.shape[0] // 2
-    return (dot(a[:half], low_t) + dot(a[half:], high_t)).astype(BF16)
+    return jnp.concatenate([upper, dot(a, west_east_t)], axis=1).astype(BF16)
+
+
+def put_slots(stage, first, frame, length):
+    groups = 64 // length
+    rows = frame.shape[0] // groups
+    patch = lax.axis_index("patch")
+    row, column = patch // 8, patch % 8
+    outer = jnp.where(row == 0, 0, jnp.where(row == 3, 1, jnp.where(column == 0, 2, 3)))
+    source = lax.broadcasted_iota(jnp.int32, (frame.shape[1], 128), 0)
+
+    def placed(edge, half):
+        total = None
+        for group in range(groups):
+            place = lanes_of(128) - (2 * group + half) * length
+            wanted = jnp.where((place >= 0) & (place < length), edge * length + place, -1)
+            chosen = jnp.where(source == wanted, 1.0, 0.0).astype(BF16)
+            piece = dot(frame[group * rows : (group + 1) * rows], chosen)
+            total = piece if total is None else total + piece
+        return total
+
+    shared = placed(outer, 0)
+    for edge in range(4):
+        stage[edge, first : first + rows, :] = (shared + placed(edge, 1)).astype(BF16)
+
+
+def send_slots(stage, out):
+    patch = lax.axis_index("patch")
+    row, column = patch // 8, patch % 8
+    second = jnp.where(column == 0, 2, 3)
+    for target in range(32):
+        down = target // 8 - row
+        right = target % 8 - column
+        near = (down >= -1) & (down <= 1) & (right >= -1) & (right <= 1) & (target != patch)
+        across = jnp.where(right > 0, 3, 2)
+        inner = jnp.where(down > 0, 1, jnp.where(down < 0, 0, across))
+        out[target] = stage[jnp.where(near, inner, second)]
 
 
 def halo_of(own, down, up, first, channels, blocks):
@@ -164,50 +199,46 @@
         cost_estimate=pl.CostEstimate(
             flops=2 * taps_out * weight.shape[1] * cells * 8, bytes_accessed=a.size * 2 + taps_out * cells, transcendentals=0
         ),
+        compiler_params=LIMIT,
         name="main_conv",
-    )(a, weight)
-
-
-def pick_kernel(code_ref, gathered, own_ref, up_ref, down_ref, *, specs):
-    for target, (out, wanted) in enumerate(((own_ref, 1), (up_ref, 0), (down_ref, 2))):
+    )(in_vmem(a), in_vmem(weight))
+
+
+def pick_kernel(code_ref, gathered, *outs, specs):
+    for target, out in enumerate(outs):
         codes = [code_ref[target * 8 + d] for d in range(8)]
         row_out = 0
         row_in = 0
         for channels, length in specs:
-            rows_in = channels * length // 32
+            groups = 64 // length
+            rows_in = channels // groups
+            lane = lanes_of(128)
+            source = lax.broadcasted_iota(jnp.int32, (128, 128), 0) & (2 * length - 1)
 
             def frame(code):
                 rows = gathered[code & 31, row_in : row_in + rows_in, :]
-                if length == 64:
-                    return jnp.concatenate([rows[:channels], rows[channels:]], axis=1)
-                if length == 16:
-                    low = lanes_of(128) < 64
-                    wide = rows.astype(F32)
-                    split = [jnp.where(low, wide, 0.0), jnp.where(low, 0.0, wide)]
-                    return jnp.concatenate(split, axis=0).astype(BF16)
-                return rows
-
-            depth = 256 if length == 64 else 128
-            source = lax.broadcasted_iota(jnp.int32, (depth, 128), 0)
-            if length == 16:
-                source = source & 63
-            lane = lanes_of(128)
+                if groups == 1:
+                    return rows
+                wide = rows.astype(F32)
+                split = [jnp.where(lane // (2 * length) == group, wide, 0.0) for group in range(groups)]
+                return jnp.concatenate(split, axis=0).astype(BF16)
+
             for block in BLOCKS[length]:
                 total = None
                 for d, base in block:
                     code = codes[d]
-                    edge = (code >> 5) & 3
-                    flip = (code >> 7) & 1
-                    active = (code >> 8) == wanted
-                    start = edge * length + flip * (length - 1)
+                    half = (code >> 5) & 1
+                    flip = (code >> 6) & 1
+                    active = (code >> 7) == 1
+                    start = half * length + flip * (length - 1)
                     if d < 4:
-                        target_cell = start + (1 - 2 * flip) * (lane - base)
+                        cell = start + (1 - 2 * flip) * (lane - base)
                         inside = (lane >= base) & (lane < base + length)
                     else:
-                        target_cell = start + jnp.zeros_like(lane)
+                        cell = start + jnp.zeros_like(lane)
                         inside = lane == base
-                    target_cell = jnp.where(inside & active, target_cell, -1)
-                    chosen = jnp.where(source == target_cell, 1.0, 0.0).astype(BF16)
+                    cell = jnp.where(inside & active, cell, -1)
+                    chosen = jnp.where(source == cell, 1.0, 0.0).astype(BF16)
                     piece = dot(frame(code), chosen)
                     total = piece if total is None else total + piece
                 out[row_out : row_out + channels, :] = total.astype(BF16)
@@ -215,77 +246,92 @@
             row_in += rows_in
 
 
-def pick(codes, gathered, specs):
+def pick(codes, gathered, specs, targets):
     rows = sum(channels * len(BLOCKS[length]) for channels, length in specs)
     shape = jax.ShapeDtypeStruct((rows, 128), BF16)
     return pl.pallas_call(
         functools.partial(pick_kernel, specs=specs),
-        out_shape=(shape, shape, shape),
+        out_shape=(shape,) * targets,
         in_specs=[pl.BlockSpec(memory_space=pltpu.SMEM), pl.BlockSpec(memory_space=pltpu.VMEM)],
+        compiler_params=LIMIT,
         name="pick",
     )(codes, gathered)
 
 
-def call(kernel, shapes, *args, name):
+def call(kernel, shapes, *args, stage=0):
     return pl.pallas_call(
         kernel,
         out_shape=tuple(jax.ShapeDtypeStruct(s, t) for s, t in shapes),
-        name=name,
-    )(*args)
-
-
-def start_kernel(x_ref, film_ref, wet_ref, a_ref, frame_ref):
-    a = activate(x_ref[...].astype(F32), film_of(film_ref, 1))
+        scratch_shapes=[pltpu.VMEM((4, stage, 128), BF16)] if stage else [],
+        compiler_params=LIMIT,
+    )(*[in_vmem(x) for x in args])
+
+
+def start_kernel(x_ref, film_ref, a_ref, slots, stage):
+    square = [lax.broadcasted_iota(jnp.int32, (32, 32), dim) for dim in (0, 1)]
+    columns = [
+        jnp.sum(jnp.where(square[0] == square[1], film_ref[k : k + 1, :], 0.0), axis=1, keepdims=True) for k in (0, 1)
+    ]
+    a = activate(x_ref[...].astype(F32), jnp.concatenate(columns, axis=1))
     a_ref[...] = a
-    frame_ref[...] = frame_64(a, wet_ref[...])
-
-
-def finish_1(base, x, own, down, up, w, we, cm, wet, c64, x32t, film, skip_ref, a_ref, frame_ref, skip_frame_ref):
+    cell = lax.broadcasted_iota(jnp.int32, (4096, 128), 0)
+    lane = lanes_of(128)
+    wanted = jnp.where(lane < 64, lane * 64, (lane - 64) * 64 + 63)
+    put_slots(stage, 0, frame_64(a, jnp.where(cell == wanted, 1.0, 0.0).astype(BF16)), 64)
+    send_slots(stage, slots)
+
+
+def finish_1(base, x, own, down, up, w, we, cm, wet, c64, x32t, film, skip_ref, a_ref, slots, skip_frame_ref, stage):
     halo = halo_of(own, down, up, 0, 32, 3).astype(BF16)
     first = x[...].astype(F32) + with_halo_64(base[...], halo, w[...], we[...], cm[...])
     skip = first.astype(BF16)
     skip_ref[...] = skip
     a = activate(by_chunks(first, c64[...]), film_of(film, 2))
     a_ref[...] = a
-    frame_ref[...] = dot(a, x32t[...]).astype(BF16)
+    put_slots(stage, 0, dot(a, x32t[...]).astype(BF16), 32)
+    send_slots(stage, slots)
     skip_frame_ref[...] = frame_64(skip, wet[...])
 
 
-def finish_2(base, own, down, up, w, x32, c32, x32t, low_t, high_t, film, skip_ref, a_ref, frame_ref, skip_frame_ref):
+def finish_2(base, own, down, up, w, x32, c32, x32t, x16t, film, skip_ref, a_ref, slots, skip_frame_ref, stage):
     halo = halo_of(own, down, up, 0, 32, 2).astype(BF16)
     second = with_halo(base[...], halo, w[...], 32, x32[...])
     skip = second.astype(BF16)
     skip_ref[...] = skip
     a = activate(by_chunks(second, c32[...]), film_of(film, 3))
     a_ref[...] = a
-    frame_ref[...] = frame_16(a, low_t[...], high_t[...])
+    put_slots(stage, 0, dot(a, x16t[...]).astype(BF16), 16)
+    send_slots(stage, slots)
     skip_frame_ref[...] = dot(skip, x32t[...]).astype(BF16)
 
 
-def finish_3(base, own, down, up, w, x16, low_t, high_t, film, third_ref, a_ref, frame_ref):
+def finish_3(base, own, down, up, w, x16, x16t, film, third_ref, a_ref, slots, stage):
     halo = halo_of(own, down, up, 0, 64, 1).astype(BF16)
     third = with_halo(base[...], halo, w[...], 16, x16[...])
     third_ref[...] = third
     a = activate(third, film_of(film, 4))
     a_ref[...] = a
-    frame_ref[...] = frame_16(a, low_t[...], high_t[...])
-
-
-def finish_4(base, third, own, down, up, w, x16, low_t, high_t, r32, skip, skip_frame, film, a_ref, frame_ref):
+    put_slots(stage, 0, dot(a, x16t[...]).astype(BF16), 16)
+    send_slots(stage, slots)
+
+
+def finish_4(base, third, own, down, up, w, x16, x16t, r32, skip, skip_frame, film, a_ref, slots, stage):
     halo = halo_of(own, down, up, 0, 128, 1).astype(BF16)
     fourth = third[...] + with_halo(base[...], halo, w[...], 16, x16[...])
-    frame_ref[0:64, :] = frame_16(fourth.astype(BF16), low_t[...], high_t[...])
-    frame_ref[64:128, :] = skip_frame[...]
+    put_slots(stage, 0, dot(fourth.astype(BF16), x16t[...]).astype(BF16), 16)
+    put_slots(stage, 32, skip_frame[...], 32)
+    send_slots(stage, slots)
     joined = jnp.concatenate([by_chunks(fourth, r32[...]), skip[...].astype(F32)], axis=0)
     a_ref[...] = activate(joined, film_of(film, 5))
 
 
-def finish_5(base, own, down, up, w, x32, x32t, double, r64, skip, skip_frame, film, a_ref, frame_ref):
+def finish_5(base, own, down, up, w, x32, x32t, double, r64, skip, skip_frame, film, a_ref, slots, stage):
     coarse = dot(halo_of(own, down, up, 0, 128, 1).astype(BF16), double[...])
     halo = activate(jnp.concatenate([coarse, halo_of(own, down, up, 128, 64, 2)], axis=0), film_of(film, 5))
     fifth = with_halo(base[...], halo, w[...], 32, x32[...])
-    frame_ref[0:64, :] = dot(fifth.astype(BF16), x32t[...]).astype(BF16)
-    frame_ref[64:128, :] = skip_frame[...]
+    put_slots(stage, 0, dot(fifth.astype(BF16), x32t[...]).astype(BF16), 32)
+    put_slots(stage, 32, skip_frame[...], 64)
+    send_slots(stage, slots)
     joined = jnp.concatenate([by_chunks(fifth, r64[...]), skip[...].astype(F32)], axis=0)
     a_ref[...] = activate(joined, film_of(film, 6))
 
@@ -330,34 +376,68 @@
     return weight.reshape(out_channels, 9, channels).transpose(1, 0, 2).reshape(9 * out_channels, channels)
 
 
-def far_patch(patch):
-    return (patch + 16) % 32
-
-
-def face_moves(by):
+NEAR_RELAY = {p: p for p in (0, 3, 4, 7, 24, 27, 28, 31)}
+NEAR_RELAY |= {1: 2, 2: 10, 8: 11, 6: 5, 5: 13, 15: 12, 25: 26, 26: 18, 16: 19, 30: 29, 29: 21, 23: 20}
+FAR_RELAY = {0: 26, 1: 27, 2: 18, 3: 19, 8: 24, 16: 0, 24: 2, 25: 3, 26: 10, 27: 11}
+FAR_RELAY |= {7: 29, 6: 28, 5: 21, 4: 20, 15: 31, 23: 7, 31: 5, 30: 4, 29: 13, 28: 12}
+
+
+def other_face(face, kind):
+    return face ^ 1 if kind == 0 else (face + 1 if face % 2 else face - 1) % 8
+
+
+def face_moves(kind):
     moves = []
     for face in range(8):
-        jump = face % 4 == (3 if by == 1 else 0)
-        for patch in range(32):
-            moves.append((face * 32 + patch, (face + by) % 8 * 32 + (far_patch(patch) if jump else patch)))
+        far = kind == 1 and face % 4 in (0, 3)
+        for target, relay in (FAR_RELAY if far else NEAR_RELAY).items():
+            moves.append((face * 32 + relay, other_face(face, kind) * 32 + target))
     return moves
 
 
+def inverse(relays):
+    targets = np.full(32, -1)
+    for target, relay in relays.items():
+        targets[relay] = target
+    return targets
+
+
 def link_codes(link_patch, link_shift, link_turn):
-    edge_table = TURN_EDGE[:, READ_EDGE]
-    flip_table = TURN_FLIP[:, READ_EDGE] ^ READ_END[None, :]
-    packed = edge_table * 32 + flip_table * 128
-    extra = jnp.full(link_turn.shape, 0, jnp.int32)
+    packed = TURN_EDGE[:, READ_EDGE] * 2 + (TURN_FLIP[:, READ_EDGE] ^ READ_END[None, :])
+    choice = jnp.zeros(link_turn.shape, jnp.int32)
     for turn in range(4):
-        extra = jnp.where(link_turn == turn, jnp.asarray(packed[turn], jnp.int32), extra)
-    codes = link_patch + extra + (link_shift + 1) * 256
+        choice = jnp.where(link_turn == turn, jnp.asarray(packed[turn], jnp.int32), choice)
+    edge, flip = choice // 2, choice % 2
+    row, column = link_patch // 8, link_patch % 8
+    outer = jnp.where(row == 0, 0, jnp.where(row == 3, 1, jnp.where(column == 0, 2, 3)))
+    cell_row = jnp.where(edge < 2, edge, flip)
+    cell_column = jnp.where(edge < 2, flip, edge - 2)
+    in_first = jnp.where(outer < 2, cell_row == outer, cell_column == outer - 2)
+    is_corner = jnp.asarray(np.arange(8) >= 4)
+    half = jnp.where(is_corner, jnp.where(in_first, 0, 1), jnp.where(edge == outer, 0, 1))
+    corner_flip = jnp.where(in_first & (outer < 2), cell_column, cell_row)
+    inside = link_shift == 0
+    half = jnp.where(inside, 1, half)
+    flip = jnp.where(is_corner, jnp.where(inside, cell_column, corner_flip), flip)
+    flat = (link_patch + half * 32 + flip * 64 + (link_shift + 1) * 128).reshape(256, 8)
     face = lax.axis_index("face")
     patch = lax.axis_index("patch")
-    up_patch = jnp.where(face % 4 == 3, far_patch(patch), patch)
-    down_patch = jnp.where(face % 4 == 0, far_patch(patch), patch)
-    flat = codes.reshape(256, 8)
-    rows = [face * 32 + patch, (face + 1) % 8 * 32 + up_patch, (face + 7) % 8 * 32 + down_patch]
-    return jnp.concatenate([lax.dynamic_slice(flat, (row, 0), (1, 8)) for row in rows], axis=0).reshape(24)
+    odd = face % 2
+    this = np.arange(32) == patch
+    near = jnp.sum(jnp.where(this, jnp.asarray(inverse(NEAR_RELAY), jnp.int32), 0))
+    far = jnp.sum(jnp.where(this, jnp.asarray(inverse(FAR_RELAY), jnp.int32), 0))
+    far = jnp.where((face % 4 == 0) | (face % 4 == 3), far, near)
+    places = [
+        (face, patch, 1),
+        (face + 1 - 2 * odd, near, 2 * odd),
+        ((face + 7 + 2 * odd) % 8, far, 2 - 2 * odd),
+    ]
+    rows = []
+    for of_face, of_patch, shift in places:
+        chosen = lax.dynamic_slice(flat, (of_face * 32 + jnp.maximum(of_patch, 0), 0), (1, 8))
+        active = (chosen // 128 == shift) & (of_patch >= 0)
+        rows.append(chosen % 128 + jnp.where(active, 128, 0))
+    return jnp.concatenate(rows, axis=0).reshape(24)
 
 
 def body(
@@ -391,67 +471,65 @@
     x32 = one_hot(border_targets(32, 256), 1024)
     x32t = one_hot(border_targets(32, 256)[:128], 1024).T
     x16 = one_hot(border_targets(16, 128), 256)
-    edges16 = border_targets(16, 128)[:64]
-    none16 = np.full(64, -1)
-    low_t = one_hot(np.concatenate([edges16, none16]), 256).T
-    high_t = one_hot(np.concatenate([none16, edges16]), 256).T
+    x16t = one_hot(np.where(np.arange(128) < 64, border_targets(16, 128), -1), 256).T
     r64 = one_hot(chunk_targets(64), 128).T
     r32 = one_hot(chunk_targets(32), 128).T
     c64 = one_hot(chunk_targets(64), 128) * jnp.asarray(0.25, BF16)
     c32 = one_hot(chunk_targets(32), 128) * jnp.asarray(0.25, BF16)
     double32 = one_hot(double_targets(32, 256), 128).T
     double64 = one_hot(double_targets(64, 384), 256).T
-    above = face_moves(1)
-    below = face_moves(-1)
-
-    def exchange(frame, specs):
-        copies = jnp.broadcast_to(frame[None], (32, *frame.shape))
-        gathered = lax.all_to_all(copies, "patch", split_axis=0, concat_axis=0, tiled=True)
-        own, for_up, for_down = pick(codes, gathered, specs)
-        from_down = lax.ppermute(for_up, ("face", "patch"), above)
-        from_up = lax.ppermute(for_down, ("face", "patch"), below)
-        return own, from_down, from_up
-
-    a1, f1 = call(start_kernel, [((32, 4096), BF16), ((64, 128), BF16)], x, film, wet, name="start")
+    near_moves = face_moves(0)
+    far_moves = face_moves(1)
+
+    def exchange(slots, specs):
+        gathered = lax.all_to_all(slots, "patch", split_axis=0, concat_axis=0, tiled=True)
+        gathered = in_vmem(gathered)
+        for_near, for_far = pick(codes[8:], gathered, specs, 2)
+        from_far = lax.ppermute(for_far, ("face", "patch"), far_moves)
+        from_near = lax.ppermute(for_near, ("face", "patch"), near_moves)
+        (own,) = pick(codes[:8], gathered, specs, 1)
+        return own, from_near, from_far
+
+    a1, f1 = call(start_kernel, [((32, 4096), BF16), ((32, 32, 128), BF16)], x, film_first, stage=32)
     h = exchange(f1, ((32, 64),))
     base = main_conv(a1, w1, 64)
     skip_fine, a2, f2, fine_frame = call(
         finish_1,
-        [((32, 4096), BF16), ((32, 1024), BF16), ((32, 128), BF16), ((64, 128), BF16)],
+        [((32, 4096), BF16), ((32, 1024), BF16), ((32, 16, 128), BF16), ((32, 256), BF16)],
         base, x, *h, w1, we, cm, wet, c64, x32t, film,
-        name="finish_1",
+        stage=16,
     )
     h = exchange(f2, ((32, 32),))
     base = main_conv(a2, w2, 32)
     skip_middle, a3, f3, middle_frame = call(
         finish_2,
-        [((64, 1024), BF16), ((64, 256), BF16), ((32, 128), BF16), ((64, 128), BF16)],
-        base, *h, w2, x32, c32, x32t, low_t, high_t, film,
-        name="finish_2",
+        [((64, 1024), BF16), ((64, 256), BF16), ((32, 16, 128), BF16), ((64, 128), BF16)],
+        base, *h, w2, x32, c32, x32t, x16t, film,
+        stage=16,
     )
     h = exchange(f3, ((64, 16),))
     base = main_conv(a3, w3, 16)
     third, a4, f4 = call(
         finish_3,
-        [((128, 256), F32), ((128, 256), BF16), ((64, 128), BF16)],
-        base, *h, w3, x16, low_t, high_t, film,
-        name="finish_3",
+        [((128, 256), F32), ((128, 256), BF16), ((32, 32, 128), BF16)],
+        base, *h, w3, x16, x16t, film,
+        stage=32,
     )
     h = exchange(f4, ((128, 16),))
     base = main_conv(a4, w4, 16)
     a5, f5 = call(
         finish_4,
-        [((192, 1024), BF16), ((128, 128), BF16)],
-        base, third, *h, w4, x16, low_t, high_t, r32, skip_middle, middle_frame, film,
-        name="finish_4",
+        [((192, 1024), BF16), ((32, 64, 128), BF16)],
+        base, third, *h, w4, x16, x16t, r32, skip_middle, middle_frame, film,
+        stage=64,
     )
     h = exchange(f5, ((128, 16), (64, 32)))
     base = main_conv(a5, w5, 32)
     a6, f6 = call(
         finish_5,
-        [((96, 4096), BF16), ((128, 128), BF16)],
+        [((96, 4096), BF16), ((32, 64, 128), BF16)],
         base, *h, w5, x32, x32t, double32, r64, skip_fine, fine_frame, film,
-        name="finish_5",
+        stage=64,
     )
     h = exchange(f6, ((64, 32), (32, 64)))
     base = main_conv(a6, w6, 64)
@@ -459,7 +537,6 @@
         finish_6,
         [((32, 4096), BF16)],
         base, *h, w6, we, cm, double64, skip_fine, film,
-        name="finish_6",
     )
     return result[:, None, :]
 

time: 256 us -> 203 us (0.79)
  the two profiles are of different devices: /device:TPU:39 before, /device:TPU:1 now
where the time goes in v1:
time: 203 us; the launch traced here: 201 us
  waiting for transfers between devices  89.5 us (44%)
  starting transfers between devices  57.9 us (29%)
  Pallas kernels  28.5 us (14%)
  local copies, waits for them, and re-layouts  17 us (8%)
  other arithmetic  5.07 us (2%)
  between operations  3.39 us (2%)
    all_to_all x6, waiting for transfers between devices, exchange(): lax.all_to_all(slots, 'patch', split_axis=0, concat_axis=0, tiled=True)  56.9 us
    all_to_all x6, starting transfers between devices, exchange(): lax.all_to_all(slots, 'patch', split_axis=0, concat_axis=0, tiled=True)  42.2 us
    ppermute x6, waiting for transfers between devices, exchange(): from_far = lax.ppermute(for_far, ('face', 'patch'), far_moves)  23.8 us
    pallas_call x7, Pallas kernels, call(): pl.pallas_call(kernel, out_shape=tuple((jax.ShapeDtypeStruct(s, t) for s,...  12.8 us
    unnamed x93, local copies, waits for them, and re-layouts  12.3 us
    pallas_call x12, Pallas kernels, pick(): pl.pallas_call(functools.partial(pick_kernel, specs=specs), out_shape=(sh...  10.4 us
    ppermute x6, waiting for transfers between devices, exchange(): from_near = lax.ppermute(for_near, ('face', 'patch'), near_moves)  8.88 us
    ppermute x6, starting transfers between devices, exchange(): from_far = lax.ppermute(for_far, ('face', 'patch'), far_moves)  7.93 us
  transfers between devices with their start and end apart: 18, of which 18 were waited for; matrix products, arithmetic and copies ran while one was open for 6% of the time, Pallas kernels for 5%

profile of v1, /device:TPU:1, one launch (start us, length us, event | category | flops | bytes accessed | tf_op | source)
XLA Modules:
  0.0 201.4 jit_solution(16488692674632867011)
XLA Ops:
  0.0 1.0 copy-done
  1.6 1.6 shard_map.334
  3.2 10.2 %all-to-all-start = ((bf16[32,32,128]{2,1,0:T(8,128)(2,1)}), bf16[32,32,128]{2,1,0:T(8,128)(2,1)S(1)}, u32[]{:S(2)}, u32[]{:S(2)}) async-start(bf16[32,32,128]{2,1,0:T(8,128)(2,1)} %get-tuple-element.35), calls=%async_computation | async-start | bytes 524288 | tf_op jit(solution)/shard_map/all_to_all | solution.py:485
  13.4 1.3 fusion.32
  17.4 0.9 fusion.we
  20.2 4.3 %all-to-all-done.gathered = bf16[32,32,128]{2,1,0:T(8,128)(2,1)S(1)} async-done(((bf16[32,32,128]{2,1,0:T(8,128)(2,1)}), bf16[32,32,128]{2,1,0:T(8,128)(2,1)S(1)}, u32[]{:S(2)}, u32[]{:S(2)}) %all-to-all-start) | async-done | bytes 262176 | tf_op jit(solution)/shard_map/all_to_all | solution.py:485
  24.5 1.4 pick.13
  25.9 1.3 collective-permute-start
  27.2 1.3 collective-permute-start.1
  28.6 1.3 main_conv.6.base
  29.9 0.8 copy-done.2
  32.2 4.0 %collective-permute-done.1.up = bf16[96,128]{1,0:T(8,128)(2,1)} collective-permute-done((bf16[96,128]{1,0:T(8,128)(2,1)}, bf16[96,128]{1,0:T(8,128)(2,1)}, u32[]{:S(2)}, u32[]{:S(2)}) %collective-permute-start.1) | collective-permute-done | bytes 24608 | tf_op jit(solution)/shard_map/ppermute | solution.py:488
  36.3 1.0 copy-done.3
  37.3 2.0 %shard_map.335 = (bf16[32,4096]{1,0:T(8,128)(2,1)S(1)}, bf16[32,1024]{1,0:T(8,128)(2,1)S(1)}, bf16[32,16,128]{2,1,0:T(8,128)(2,1)S(1)}, bf16[32,256]{1,0:T(8,128)(2,1)S(1)}) custom-call(f32[32,4096]{1,0:T(8,128)S(1)} %copy-done.3, bf16[32,4096]{1,0:T(8,128)(2,1)S(1)} %bitcast.38, bf16[96,128]{1,0:T(8,128)(2,1)S(1)} %pick.12.own, ...), custom_call_target="tpu_custom_call" | custom-call | tf_op jit(solution)/shard_map/pallas_call | solution.py:262
  40.6 8.0 %all-to-all-start.1 = ((bf16[32,16,128]{2,1,0:T(8,128)(2,1)}), bf16[32,16,128]{2,1,0:T(8,128)(2,1)S(1)}, u32[]{:S(2)}, u32[]{:S(2)}) async-start(bf16[32,16,128]{2,1,0:T(8,128)(2,1)} %copy-done.5), calls=%async_computation.1 | async-start | bytes 262144 | tf_op jit(solution)/shard_map/all_to_all | solution.py:485
  49.3 0.9 copy.89
  50.4 0.8 fusion.2.x32
  51.2 5.9 %all-to-all-done.1.gathered = bf16[32,16,128]{2,1,0:T(8,128)(2,1)S(1)} async-done(((bf16[32,16,128]{2,1,0:T(8,128)(2,1)}), bf16[32,16,128]{2,1,0:T(8,128)(2,1)S(1)}, u32[]{:S(2)}, u32[]{:S(2)}) %all-to-all-start.1) | async-done | bytes 131104 | tf_op jit(solution)/shard_map/all_to_all | solution.py:485
  57.9 1.3 collective-permute-start.2
  59.2 1.3 collective-permute-start.3
  62.1 1.8 collective-permute-done.2.down
  63.9 4.0 %collective-permute-done.3.up = bf16[64,128]{1,0:T(8,128)(2,1)S(1)} collective-permute-done((bf16[64,128]{1,0:T(8,128)(2,1)S(1)}, bf16[64,128]{1,0:T(8,128)(2,1)S(1)}, u32[]{:S(2)}, u32[]{:S(2)}) %collective-permute-start.3) | collective-permute-done | bytes 16416 | tf_op jit(solution)/shard_map/ppermute | solution.py:488
  67.9 1.8 shard_map.336
  69.8 5.8 %all-to-all-start.2 = ((bf16[32,16,128]{2,1,0:T(8,128)(2,1)}), bf16[32,16,128]{2,1,0:T(8,128)(2,1)S(1)}, u32[]{:S(2)}, u32[]{:S(2)}) async-start(bf16[32,16,128]{2,1,0:T(8,128)(2,1)} %get-tuple-element.43), calls=%async_computation.2 | async-start | bytes 262144 | tf_op jit(solution)/shard_map/all_to_all | solution.py:485
  75.9 8.3 %all-to-all-done.2.gathered = bf16[32,16,128]{2,1,0:T(8,128)(2,1)S(1)} async-done(((bf16[32,16,128]{2,1,0:T(8,128)(2,1)}), bf16[32,16,128]{2,1,0:T(8,128)(2,1)S(1)}, u32[]{:S(2)}, u32[]{:S(2)}) %all-to-all-start.2) | async-done | bytes 131104 | tf_op jit(solution)/shard_map/all_to_all | solution.py:485
  85.0 1.3 collective-permute-start.4
  86.3 1.3 collective-permute-start.5
  88.9 2.1 %collective-permute-done.4.down = bf16[64,128]{1,0:T(8,128)(2,1)S(1)} collective-permute-done((bf16[64,128]{1,0:T(8,128)(2,1)S(1)}, bf16[64,128]{1,0:T(8,128)(2,1)S(1)}, u32[]{:S(2)}, u32[]{:S(2)}) %collective-permute-start.4) | collective-permute-done | bytes 16416 | tf_op jit(solution)/shard_map/ppermute | solution.py:489
  91.0 4.0 %collective-permute-done.5.up = bf16[64,128]{1,0:T(8,128)(2,1)S(1)} collective-permute-done((bf16[64,128]{1,0:T(8,128)(2,1)S(1)}, bf16[64,128]{1,0:T(8,128)(2,1)S(1)}, u32[]{:S(2)}, u32[]{:S(2)}) %collective-permute-start.5) | collective-permute-done | bytes 16416 | tf_op jit(solution)/shard_map/ppermute | solution.py:488
  95.0 1.7 shard_map.337
  96.8 5.9 %all-to-all-start.3 = ((bf16[32,32,128]{2,1,0:T(8,128)(2,1)}), bf16[32,32,128]{2,1,0:T(8,128)(2,1)S(1)}, u32[]{:S(2)}, u32[]{:S(2)}) async-start(bf16[32,32,128]{2,1,0:T(8,128)(2,1)} %get-tuple-element.48), calls=%async_computation.3 | async-start | bytes 524288 | tf_op jit(solution)/shard_map/all_to_all | solution.py:485
  102.7 1.9 copy.92
  104.6 1.2 copy.93
  105.8 8.1 %all-to-all-done.3.gathered = bf16[32,32,128]{2,1,0:T(8,128)(2,1)S(1)} async-done(((bf16[32,32,128]{2,1,0:T(8,128)(2,1)}), bf16[32,32,128]{2,1,0:T(8,128)(2,1)S(1)}, u32[]{:S(2)}, u32[]{:S(2)}) %all-to-all-start.3) | async-done | bytes 262176 | tf_op jit(solution)/shard_map/all_to_all | solution.py:485
  113.9 0.8 pick.19
  114.7 1.3 collective-permute-start.6
  116.0 1.5 collective-permute-start.7
  117.5 0.8 copy-done.17
  119.7 1.2 collective-permute-done.6.down
  120.9 4.0 %collective-permute-done.7.up = bf16[128,128]{1,0:T(8,128)(2,1)S(1)} collective-permute-done((bf16[128,128]{1,0:T(8,128)(2,1)S(1)}, bf16[128,128]{1,0:T(8,128)(2,1)S(1)}, u32[]{:S(2)}, u32[]{:S(2)}) %collective-permute-start.7) | collective-permute-done | bytes 32800 | tf_op jit(solution)/shard_map/ppermute | solution.py:488
  124.9 1.4 shard_map.338
  126.3 0.8 copy-done.4
  127.9 5.8 %all-to-all-start.4 = ((bf16[32,64,128]{2,1,0:T(8,128)(2,1)}), bf16[32,64,128]{2,1,0:T(8,128)(2,1)S(1)}, u32[]{:S(2)}, u32[]{:S(2)}) async-start(bf16[32,64,128]{2,1,0:T(8,128)(2,1)} %copy-done.4), calls=%async_computation.4 | async-start | bytes 1048576 | tf_op jit(solution)/shard_map/all_to_all | solution.py:485
  133.7 1.2 reshape.63
  134.9 1.1 copy.94
  136.1 14.1 %all-to-all-done.4.gathered = bf16[32,64,128]{2,1,0:T(8,128)(2,1)S(1)} async-done(((bf16[32,64,128]{2,1,0:T(8,128)(2,1)}), bf16[32,64,128]{2,1,0:T(8,128)(2,1)S(1)}, u32[]{:S(2)}, u32[]{:S(2)}) %all-to-all-start.4) | async-done | bytes 524320 | tf_op jit(solution)/shard_map/all_to_all | solution.py:485
  150.2 1.0 pick.21
  151.2 1.3 collective-permute-start.8
  152.5 1.3 collective-permute-start.9
  153.8 1.0 copy-done.13
  155.6 0.8 pick.20.own
  156.5 1.5 collective-permute-done.8.down
  158.0 3.8 %collective-permute-done.9.up = bf16[256,128]{1,0:T(8,128)(2,1)S(1)} collective-permute-done((bf16[256,128]{1,0:T(8,128)(2,1)S(1)}, bf16[256,128]{1,0:T(8,128)(2,1)S(1)}, u32[]{:S(2)}, u32[]{:S(2)}) %collective-permute-start.9) | collective-permute-done | bytes 65568 | tf_op jit(solution)/shard_map/ppermute | solution.py:488
  161.8 2.7 %shard_map.339 = (bf16[96,4096]{1,0:T(8,128)(2,1)S(1)}, bf16[32,64,128]{2,1,0:T(8,128)(2,1)}) custom-call(f32[64,1024]{1,0:T(8,128)S(1)} %main_conv.10.base, bf16[256,128]{1,0:T(8,128)(2,1)S(1)} %pick.20.own, bf16[256,128]{1,0:T(8,128)(2,1)S(1)} %collective-permute-done.8.down, bf16[256,128]{1,0:T(8,128)(2,1)S(1)} %collective-permute-done.9.up, ...), custom_call_target="tpu_custom_call" | custom-call | tf_op jit(solution)/shard_map/pallas_call | solution.py:262
  164.5 0.9 copy-done.10
  165.4 6.6 %all-to-all-start.5 = ((bf16[32,64,128]{2,1,0:T(8,128)(2,1)}), bf16[32,64,128]{2,1,0:T(8,128)(2,1)S(1)}, u32[]{:S(2)}, u32[]{:S(2)}) async-start(bf16[32,64,128]{2,1,0:T(8,128)(2,1)} %get-tuple-element.60), calls=%async_computation.5 | async-start | bytes 1048576 | tf_op jit(solution)/shard_map/all_to_all | solution.py:485
  172.3 16.2 %all-to-all-done.5.gathered = bf16[32,64,128]{2,1,0:T(8,128)(2,1)S(1)} async-done(((bf16[32,64,128]{2,1,0:T(8,128)(2,1)}), bf16[32,64,128]{2,1,0:T(8,128)(2,1)S(1)}, u32[]{:S(2)}, u32[]{:S(2)}) %all-to-all-start.5) | async-done | bytes 524320 | tf_op jit(solution)/shard_map/all_to_all | solution.py:485
  188.5 0.9 pick.23
  189.5 1.3 collective-permute-start.10
  190.8 1.3 collective-permute-start.11
  192.1 1.4 main_conv.11.base
  194.3 1.8 collective-permute-done.10.down
  196.1 3.8 %collective-permute-done.11.up = bf16[224,128]{1,0:T(8,128)(2,1)S(1)} collective-permute-done((bf16[224,128]{1,0:T(8,128)(2,1)S(1)}, bf16[224,128]{1,0:T(8,128)(2,1)S(1)}, u32[]{:S(2)}, u32[]{:S(2)}) %collective-permute-start.11) | collective-permute-done | bytes 57376 | tf_op jit(solution)/shard_map/ppermute | solution.py:488
  199.9 1.5 shard_map.340
  (122 shorter events, 14.7 us)
Async XLA Ops:
  0.0 18.4 %copy-start.30 = (s32[128]{0:T(128)S(1)}, s32[128]{0:T(128)}, u32[]{:S(2)}) copy-start(s32[128]{0:T(128)} %constant.192.clone) | copy-start | bytes 1540
  0.0 1.0 copy-start
  1.0 0.7 copy-start.8
  3.2 21.3 %all-to-all-start = ((bf16[32,32,128]{2,1,0:T(8,128)(2,1)}), bf16[32,32,128]{2,1,0:T(8,128)(2,1)S(1)}, u32[]{:S(2)}, u32[]{:S(2)}) async-start(bf16[32,32,128]{2,1,0:T(8,128)(2,1)} %get-tuple-element.35), calls=%async_computation | async-start | bytes 524288 | tf_op jit(solution)/shard_map/all_to_all | solution.py:485
  17.3 1.4 copy-start.21
  17.3 1.4 copy-start.22
  17.3 1.4 copy-start.23
  17.3 1.4 copy-start.40
  17.3 1.4 copy-start.41
  17.3 1.4 copy-start.42
  17.3 1.4 copy-start.43
  17.4 1.4 copy-start.44
  17.4 2.0 copy-start.39
  17.4 2.1 %copy-start.25 = (s32[512]{0:T(512)S(1)}, s32[512]{0:T(512)}, u32[]{:S(2)}) copy-start(s32[512]{0:T(512)} %constant.198.clone) | copy-start | bytes 6148
  17.4 2.3 %copy-start.24 = (bf16[32,288]{1,0:T(8,128)(2,1)S(1)}, bf16[32,288]{1,0:T(8,128)(2,1)}, u32[]{:S(2)}) copy-start(bf16[32,288]{1,0:T(8,128)(2,1)} %param.38) | copy-start | bytes 55300
  18.4 1.6 copy-start.27
  18.4 1.7 copy-start.38
  25.9 6.3 %collective-permute-start = (bf16[96,128]{1,0:T(8,128)(2,1)}, bf16[96,128]{1,0:T(8,128)(2,1)}, u32[]{:S(2)}, u32[]{:S(2)}) collective-permute-start(bf16[96,128]{1,0:T(8,128)(2,1)} %get-tuple-element.36), channel_id=1, source_target_pairs={{0,32},{3,35},{4,36},{7,39},{24,56},{27,59},{28,60},{31,63},{2,33}... | collective-permute-start | bytes 73736 | tf_op jit(solution)/shard_map/ppermute | solution.py:489
  27.2 9.1 %collective-permute-start.1 = (bf16[96,128]{1,0:T(8,128)(2,1)}, bf16[96,128]{1,0:T(8,128)(2,1)}, u32[]{:S(2)}, u32[]{:S(2)}) collective-permute-start(bf16[96,128]{1,0:T(8,128)(2,1)} %get-tuple-element.37), channel_id=1, source_target_pairs={{26,224},{27,225},{18,226},{19,227},{24,232},{0,240},{2,248},{3,24... | collective-permute-start | bytes 73736 | tf_op jit(solution)/shard_map/ppermute | solution.py:488
  28.5 2.3 %copy-start.9 = (f32[2,32]{1,0:T(2,128)S(1)}, f32[2,32]{1,0:T(2,128)}, u32[]{:S(2)}) copy-start(f32[2,32]{1,0:T(2,128)} %film_ref.1) | copy-start | bytes 772
  28.5 2.3 %copy-start.31 = (f32[2,192]{1,0:T(2,128)S(1)}, f32[2,192]{1,0:T(2,128)}, u32[]{:S(2)}) copy-start(f32[2,192]{1,0:T(2,128)} %param.45) | copy-start | bytes 4612
  28.5 2.3 %copy-start.33 = (f32[2,32]{1,0:T(2,128)S(1)}, f32[2,32]{1,0:T(2,128)}, u32[]{:S(2)}) copy-start(f32[2,32]{1,0:T(2,128)} %param.39) | copy-start | bytes 772
  28.5 2.3 %copy-start.34 = (f32[2,64]{1,0:T(2,128)S(1)}, f32[2,64]{1,0:T(2,128)}, u32[]{:S(2)}) copy-start(f32[2,64]{1,0:T(2,128)} %param.41) | copy-start | bytes 1540
  28.5 2.2 %copy-start.35 = (f32[2,128]{1,0:T(2,128)S(1)}, f32[2,128]{1,0:T(2,128)}, u32[]{:S(2)}) copy-start(f32[2,128]{1,0:T(2,128)} %param.43) | copy-start | bytes 3076
  28.5 2.2 %copy-start.36 = (f32[2,96]{1,0:T(2,128)S(1)}, f32[2,96]{1,0:T(2,128)}, u32[]{:S(2)}) copy-start(f32[2,96]{1,0:T(2,128)} %param.47) | copy-start | bytes 2308
  28.5 7.7 %copy-start.1 = (bf16[32,1,4096]{2,0,1:T(8,128)(2,1)S(1)}, bf16[32,1,4096]{2,0,1:T(8,128)(2,1)}, u32[]{:S(2)}) copy-start(bf16[32,1,4096]{2,0,1:T(8,128)(2,1)} %param.36) | copy-start | bytes 786436
  29.9 0.8 copy-start.2
  36.3 1.0 copy-start.3
  39.3 0.7 copy-start.5
  40.0 0.6 copy-start.14
  40.6 19.9 %copy-start.15 = (bf16[32,1024]{1,0:T(8,128)(2,1)S(1)}, bf16[32,1024]{1,0:T(8,128)(2,1)}, u32[]{:S(2)}) copy-start(bf16[32,1024]{1,0:T(8,128)(2,1)} %copy-done.14) | copy-start | bytes 196612
  40.6 16.5 %all-to-all-start.1 = ((bf16[32,16,128]{2,1,0:T(8,128)(2,1)}), bf16[32,16,128]{2,1,0:T(8,128)(2,1)S(1)}, u32[]{:S(2)}, u32[]{:S(2)}) async-start(bf16[32,16,128]{2,1,0:T(8,128)(2,1)} %copy-done.5), calls=%async_computation.1 | async-start | bytes 262144 | tf_op jit(solution)/shard_map/all_to_all | solution.py:485
  57.9 6.0 %collective-permute-start.2 = (bf16[64,128]{1,0:T(8,128)(2,1)S(1)}, bf16[64,128]{1,0:T(8,128)(2,1)S(1)}, u32[]{:S(2)}, u32[]{:S(2)}) collective-permute-start(bf16[64,128]{1,0:T(8,128)(2,1)S(1)} %get-tuple-element.40), channel_id=1, source_target_pairs={{0,32},{3,35},{4,36},{7,39},{24,56},{27,59},{28,60},{31,63},{2,33}... | collective-permute-start | bytes 49160 | tf_op jit(solution)/shard_map/ppermute | solution.py:489
  59.2 8.7 %collective-permute-start.3 = (bf16[64,128]{1,0:T(8,128)(2,1)S(1)}, bf16[64,128]{1,0:T(8,128)(2,1)S(1)}, u32[]{:S(2)}, u32[]{:S(2)}) collective-permute-start(bf16[64,128]{1,0:T(8,128)(2,1)S(1)} %get-tuple-element.41), channel_id=1, source_target_pairs={{26,224},{27,225},{18,226},{19,227},{24,232},{0,240},{2,248},{3,24... | collective-permute-start | bytes 49160 | tf_op jit(solution)/shard_map/ppermute | solution.py:488
  61.3 14.3 %copy-start.19 = (bf16[128,576]{0,1:T(8,128)(2,1)S(1)}, bf16[128,576]{0,1:T(8,128)(2,1)}, u32[]{:S(2)}) copy-start(bf16[128,576]{0,1:T(8,128)(2,1)} %param.42) | copy-start | bytes 442372
  62.1 13.7 %copy-start.37 = (s32[128]{0:T(128)S(1)}, s32[128]{0:T(128)}, u32[]{:S(2)}) copy-start(s32[128]{0:T(128)} %constant.196.clone) | copy-start | bytes 1540
  69.8 5.8 %copy-start.6 = (bf16[64,1024]{1,0:T(8,128)(2,1)}, bf16[64,1024]{1,0:T(8,128)(2,1)S(1)}, u32[]{:S(2)}) copy-start(bf16[64,1024]{1,0:T(8,128)(2,1)S(1)} %get-tuple-element.51.skip) | copy-start | bytes 393220
  69.8 14.4 %all-to-all-start.2 = ((bf16[32,16,128]{2,1,0:T(8,128)(2,1)}), bf16[32,16,128]{2,1,0:T(8,128)(2,1)S(1)}, u32[]{:S(2)}, u32[]{:S(2)}) async-start(bf16[32,16,128]{2,1,0:T(8,128)(2,1)} %get-tuple-element.43), calls=%async_computation.2 | async-start | bytes 262144 | tf_op jit(solution)/shard_map/all_to_all | solution.py:485
  85.0 6.0 %collective-permute-start.4 = (bf16[64,128]{1,0:T(8,128)(2,1)S(1)}, bf16[64,128]{1,0:T(8,128)(2,1)S(1)}, u32[]{:S(2)}, u32[]{:S(2)}) collective-permute-start(bf16[64,128]{1,0:T(8,128)(2,1)S(1)} %get-tuple-element.44), channel_id=1, source_target_pairs={{0,32},{3,35},{4,36},{7,39},{24,56},{27,59},{28,60},{31,63},{2,33}... | collective-permute-start | bytes 49160 | tf_op jit(solution)/shard_map/ppermute | solution.py:489
  86.3 8.7 %collective-permute-start.5 = (bf16[64,128]{1,0:T(8,128)(2,1)S(1)}, bf16[64,128]{1,0:T(8,128)(2,1)S(1)}, u32[]{:S(2)}, u32[]{:S(2)}) collective-permute-start(bf16[64,128]{1,0:T(8,128)(2,1)S(1)} %get-tuple-element.45), channel_id=1, source_target_pairs={{26,224},{27,225},{18,226},{19,227},{24,232},{0,240},{2,248},{3,24... | collective-permute-start | bytes 49160 | tf_op jit(solution)/shard_map/ppermute | solution.py:488
  96.8 18.0 %copy-start.16 = (bf16[128,256]{1,0:T(8,128)(2,1)}, bf16[128,256]{1,0:T(8,128)(2,1)S(1)}, u32[]{:S(2)}) copy-start(bf16[128,256]{1,0:T(8,128)(2,1)S(1)} %get-tuple-element.46.a_ref) | copy-start | bytes 196612
  96.8 9.0 %copy-start.28 = (s32[512]{0:T(512)S(1)}, s32[512]{0:T(512)}, u32[]{:S(2)}) copy-start(s32[512]{0:T(512)} %constant.199.clone) | copy-start | bytes 6148
  96.8 17.1 %all-to-all-start.3 = ((bf16[32,32,128]{2,1,0:T(8,128)(2,1)}), bf16[32,32,128]{2,1,0:T(8,128)(2,1)S(1)}, u32[]{:S(2)}, u32[]{:S(2)}) async-start(bf16[32,32,128]{2,1,0:T(8,128)(2,1)} %get-tuple-element.48), calls=%async_computation.3 | async-start | bytes 524288 | tf_op jit(solution)/shard_map/all_to_all | solution.py:485
  114.7 6.1 %collective-permute-start.6 = (bf16[128,128]{1,0:T(8,128)(2,1)S(1)}, bf16[128,128]{1,0:T(8,128)(2,1)S(1)}, u32[]{:S(2)}, u32[]{:S(2)}) collective-permute-start(bf16[128,128]{1,0:T(8,128)(2,1)S(1)} %get-tuple-element.49), channel_id=1, source_target_pairs={{0,32},{3,35},{4,36},{7,39},{24,56},{27,59},{28,60},{31,63},{2,33}... | collective-permute-start | bytes 98312 | tf_op jit(solution)/shard_map/ppermute | solution.py:489
  116.0 8.9 %collective-permute-start.7 = (bf16[128,128]{1,0:T(8,128)(2,1)S(1)}, bf16[128,128]{1,0:T(8,128)(2,1)S(1)}, u32[]{:S(2)}, u32[]{:S(2)}) collective-permute-start(bf16[128,128]{1,0:T(8,128)(2,1)S(1)} %get-tuple-element.50), channel_id=1, source_target_pairs={{26,224},{27,225},{18,226},{19,227},{24,232},{0,240},{2,248},{3,24... | collective-permute-start | bytes 98312 | tf_op jit(solution)/shard_map/ppermute | solution.py:488
  117.5 0.8 copy-start.17
  118.4 6.6 %copy-start.7 = (bf16[64,1024]{1,0:T(8,128)(2,1)S(1)}, bf16[64,1024]{1,0:T(8,128)(2,1)}, u32[]{:S(2)}) copy-start(bf16[64,1024]{1,0:T(8,128)(2,1)} %copy-done.6) | copy-start | bytes 393220
  126.3 0.8 copy-start.4
  127.2 0.8 copy-start.12
  127.9 5.8 %copy-start.18 = (bf16[64,1728]{1,0:T(8,128)(2,1)S(1)}, bf16[64,1728]{1,0:T(8,128)(2,1)}, u32[]{:S(2)}) copy-start(bf16[64,1728]{1,0:T(8,128)(2,1)} %param.46) | copy-start | bytes 663556
  127.9 22.3 %all-to-all-start.4 = ((bf16[32,64,128]{2,1,0:T(8,128)(2,1)}), bf16[32,64,128]{2,1,0:T(8,128)(2,1)S(1)}, u32[]{:S(2)}, u32[]{:S(2)}) async-start(bf16[32,64,128]{2,1,0:T(8,128)(2,1)} %copy-done.4), calls=%async_computation.4 | async-start | bytes 1048576 | tf_op jit(solution)/shard_map/all_to_all | solution.py:485
  133.7 2.4 %copy-start.32 = (s32[256]{0:T(256)S(1)}, s32[256]{0:T(256)}, u32[]{:S(2)}) copy-start(s32[256]{0:T(256)} %constant.200.clone) | copy-start | bytes 3076
  133.7 2.4 %copy-start.26 = (s32[512]{0:T(512)S(1)}, s32[512]{0:T(512)}, u32[]{:S(2)}) copy-start(s32[512]{0:T(512)} %constant.198.clone) | copy-start | bytes 6148
  151.2 6.8 %collective-permute-start.8 = (bf16[256,128]{1,0:T(8,128)(2,1)S(1)}, bf16[256,128]{1,0:T(8,128)(2,1)S(1)}, u32[]{:S(2)}, u32[]{:S(2)}) collective-permute-start(bf16[256,128]{1,0:T(8,128)(2,1)S(1)} %get-tuple-element.55), channel_id=1, source_target_pairs={{0,32},{3,35},{4,36},{7,39},{24,56},{27,59},{28,60},{31,63},{2,33}... | collective-permute-start | bytes 196616 | tf_op jit(solution)/shard_map/ppermute | solution.py:489
  152.5 9.2 %collective-permute-start.9 = (bf16[256,128]{1,0:T(8,128)(2,1)S(1)}, bf16[256,128]{1,0:T(8,128)(2,1)S(1)}, u32[]{:S(2)}, u32[]{:S(2)}) collective-permute-start(bf16[256,128]{1,0:T(8,128)(2,1)S(1)} %get-tuple-element.56), channel_id=1, source_target_pairs={{26,224},{27,225},{18,226},{19,227},{24,232},{0,240},{2,248},{3,24... | collective-permute-start | bytes 196616 | tf_op jit(solution)/shard_map/ppermute | solution.py:488
  153.8 1.0 copy-start.13
  164.5 0.9 copy-start.10
  165.4 6.7 %copy-start.20 = (bf16[32,864]{1,0:T(8,128)(2,1)S(1)}, bf16[32,864]{1,0:T(8,128)(2,1)}, u32[]{:S(2)}) copy-start(bf16[32,864]{1,0:T(8,128)(2,1)} %param.48) | copy-start | bytes 165892
  165.4 6.8 %copy-start.29 = (s32[384]{0:T(512)S(1)}, s32[384]{0:T(512)}, u32[]{:S(2)}) copy-start(s32[384]{0:T(512)} %constant.201.clone) | copy-start | bytes 4612
  165.4 26.6 %copy-start.11 = (bf16[96,4096]{1,0:T(8,128)(2,1)S(1)}, bf16[96,4096]{1,0:T(8,128)(2,1)}, u32[]{:S(2)}) copy-start(bf16[96,4096]{1,0:T(8,128)(2,1)} %copy-done.10) | copy-start | bytes 2359300
  165.4 23.1 %all-to-all-start.5 = ((bf16[32,64,128]{2,1,0:T(8,128)(2,1)}), bf16[32,64,128]{2,1,0:T(8,128)(2,1)S(1)}, u32[]{:S(2)}, u32[]{:S(2)}) async-start(bf16[32,64,128]{2,1,0:T(8,128)(2,1)} %get-tuple-element.60), calls=%async_computation.5 | async-start | bytes 1048576 | tf_op jit(solution)/shard_map/all_to_all | solution.py:485
  189.5 6.6 %collective-permute-start.10 = (bf16[224,128]{1,0:T(8,128)(2,1)S(1)}, bf16[224,128]{1,0:T(8,128)(2,1)S(1)}, u32[]{:S(2)}, u32[]{:S(2)}) collective-permute-start(bf16[224,128]{1,0:T(8,128)(2,1)S(1)} %get-tuple-element.61), channel_id=1, source_target_pairs={{0,32},{3,35},{4,36},{7,39},{24,56},{27,59},{28,60},{31,63},{2,33}... | collective-permute-start | bytes 172040 | tf_op jit(solution)/shard_map/ppermute | solution.py:489
  190.8 9.1 %collective-permute-start.11 = (bf16[224,128]{1,0:T(8,128)(2,1)S(1)}, bf16[224,128]{1,0:T(8,128)(2,1)S(1)}, u32[]{:S(2)}, u32[]{:S(2)}) collective-permute-start(bf16[224,128]{1,0:T(8,128)(2,1)S(1)} %get-tuple-element.62), channel_id=1, source_target_pairs={{26,224},{27,225},{18,226},{19,227},{24,232},{0,240},{2,248},{3,24... | collective-permute-start | bytes 172040 | tf_op jit(solution)/shard_map/ppermute | solution.py:488

commit v2 on v1

--- a/solution.py
+++ b/solution.py
@@ -268,16 +268,9 @@
 
 
 def start_kernel(x_ref, film_ref, a_ref, slots, stage):
-    square = [lax.broadcasted_iota(jnp.int32, (32, 32), dim) for dim in (0, 1)]
-    columns = [
-        jnp.sum(jnp.where(square[0] == square[1], film_ref[k : k + 1, :], 0.0), axis=1, keepdims=True) for k in (0, 1)
-    ]
-    a = activate(x_ref[...].astype(F32), jnp.concatenate(columns, axis=1))
+    a = activate(x_ref[...].astype(F32), columns_of(film_ref[...]))
     a_ref[...] = a
-    cell = lax.broadcasted_iota(jnp.int32, (4096, 128), 0)
-    lane = lanes_of(128)
-    wanted = jnp.where(lane < 64, lane * 64, (lane - 64) * 64 + 63)
-    put_slots(stage, 0, frame_64(a, jnp.where(cell == wanted, 1.0, 0.0).astype(BF16)), 64)
+    put_slots(stage, 0, frame_64(a, ones_at((4096, 128), 1, side_cell)), 64)
     send_slots(stage, slots)
 
 
@@ -343,37 +336,81 @@
     out_ref[...] = (skip[...].astype(F32) + total).astype(BF16)
 
 
-def one_hot(targets, width):
-    return (jnp.asarray(targets, jnp.int32)[:, None] == lax.broadcasted_iota(jnp.int32, (1, width), 1)).astype(BF16)
-
-
-def border_targets(length, width):
+def border_cell(k, length):
     cells = length * length
-    k = np.arange(length)
-    targets = np.full(width, -1)
-    edges = [k, cells - length + k, k * length, k * length + length - 1]
-    targets[: 4 * length] = np.concatenate(edges)
-    targets[4 * length : 4 * length + 4] = [0, length - 1, cells - length, cells - 1]
-    return targets
-
-
-def chunk_targets(length):
-    lane = np.arange(512)
+    part, place = k // length, k % length
+    cell = jnp.where(part == 0, place, jnp.where(part == 1, cells - length + place, -1))
+    cell = jnp.where(part == 2, place * length, jnp.where(part == 3, place * length + length - 1, cell))
+    end = 4 * length
+    cell = jnp.where(k == end, 0, jnp.where(k == end + 1, length - 1, cell))
+    return jnp.where(k == end + 2, cells - length, jnp.where(k == end + 3, cells - 1, cell))
+
+
+def chunk_lane(lane, length):
     return (lane // length // 2) * (length // 2) + (lane % length) // 2
 
 
-def double_targets(length, width):
-    targets = np.full(width, -1)
-    lane = np.arange(4 * length)
-    targets[: 4 * length] = (lane // length) * (length // 2) + (lane % length) // 2
-    targets[4 * length : 4 * length + 4] = 2 * length + np.arange(4)
-    return targets
-
-
-def tap_rows(weight):
-    out_channels = weight.shape[0]
-    channels = weight.shape[1] // 9
-    return weight.reshape(out_channels, 9, channels).transpose(1, 0, 2).reshape(9 * out_channels, channels)
+def double_lane(lane, length):
+    end = 4 * length
+    half = (lane // length) * (length // 2) + (lane % length) // 2
+    return jnp.where(lane < end, half, jnp.where(lane < end + 4, lane - 2 * length, -1))
+
+
+def side_cell(k):
+    return jnp.where(k < 64, k * 64, (k - 64) * 64 + 63)
+
+
+def corner_lane(k):
+    return jnp.where(k == 0, 0, jnp.where(k == 1, 63, jnp.where(k == 2, 64, jnp.where(k == 3, 127, -1))))
+
+
+def ones_at(shape, axis, function, value=1.0):
+    own = [1, 1]
+    own[axis] = shape[axis]
+    wanted = function(lax.broadcasted_iota(jnp.int32, tuple(own), axis))
+    other = lax.broadcasted_iota(jnp.int32, shape, 1 - axis)
+    return jnp.where(other == wanted, value, 0.0).astype(BF16)
+
+
+MATRICES = {
+    "we": ((128, 4096), 0, side_cell, 1.0),
+    "wet": ((4096, 128), 1, side_cell, 1.0),
+    "cm": ((128, 128), 0, corner_lane, 1.0),
+    "c64": ((512, 128), 0, lambda k: chunk_lane(k, 64), 0.25),
+    "x32t": ((1024, 128), 1, lambda k: border_cell(k, 32), 1.0),
+    "x32": ((256, 1024), 0, lambda k: border_cell(k, 32), 1.0),
+    "c32": ((512, 128), 0, lambda k: chunk_lane(k, 32), 0.25),
+    "x16t": ((256, 128), 1, lambda k: jnp.where(k < 64, border_cell(k, 16), -1), 1.0),
+    "x16": ((128, 256), 0, lambda k: border_cell(k, 16), 1.0),
+    "r32": ((128, 512), 1, lambda k: chunk_lane(k, 32), 1.0),
+    "r64": ((128, 512), 1, lambda k: chunk_lane(k, 64), 1.0),
+    "double32": ((128, 256), 1, lambda k: double_lane(k, 32), 1.0),
+    "double64": ((256, 384), 1, lambda k: double_lane(k, 64), 1.0),
+}
+
+
+def matrices_kernel(*outs):
+    for out, (shape, axis, function, value) in zip(outs, MATRICES.values()):
+        out[...] = ones_at(shape, axis, function, value)
+
+
+def columns_of(film):
+    channels = film.shape[1]
+    square = [lax.broadcasted_iota(jnp.int32, (channels, channels), dim) for dim in (0, 1)]
+    same = square[0] == square[1]
+    columns = [jnp.sum(jnp.where(same, film[k : k + 1, :], 0.0), axis=1, keepdims=True) for k in (0, 1)]
+    return jnp.concatenate(columns, axis=1)
+
+
+def prepare_kernel(*refs):
+    films, weights, film_out, outs = refs[:6], refs[6:12], refs[12], refs[13:]
+    for film, (first, last) in zip(films, FILM_ROWS.values()):
+        film_out[first:last, :] = columns_of(film[...])
+    for weight, out in zip(weights, outs):
+        out_channels = weight.shape[0]
+        channels = weight.shape[1] // 9
+        for t in range(9):
+            out[t * out_channels : (t + 1) * out_channels, :] = weight[:, t * channels : (t + 1) * channels]
 
 
 NEAR_RELAY = {p: p for p in (0, 3, 4, 7, 24, 27, 28, 31)}
@@ -459,25 +496,13 @@
     link_turn,
 ):
     x = features[:, 0, :]
-    film = jnp.concatenate([film_first, film_second, film_third, film_fourth, film_fifth, film_sixth], axis=1).T
     codes = link_codes(link_patch, link_shift, link_turn)
-    w1, w2, w3, w4, w5, w6 = [
-        tap_rows(w) for w in (weight_first, weight_second, weight_third, weight_fourth, weight_fifth, weight_sixth)
-    ]
-    k = np.arange(64)
-    we = one_hot(np.concatenate([k * 64, k * 64 + 63]), 4096)
-    wet = we.T
-    cm = one_hot(np.concatenate([[0, 63, 64, 127], np.full(124, -1)]), 128)
-    x32 = one_hot(border_targets(32, 256), 1024)
-    x32t = one_hot(border_targets(32, 256)[:128], 1024).T
-    x16 = one_hot(border_targets(16, 128), 256)
-    x16t = one_hot(np.where(np.arange(128) < 64, border_targets(16, 128), -1), 256).T
-    r64 = one_hot(chunk_targets(64), 128).T
-    r32 = one_hot(chunk_targets(32), 128).T
-    c64 = one_hot(chunk_targets(64), 128) * jnp.asarray(0.25, BF16)
-    c32 = one_hot(chunk_targets(32), 128) * jnp.asarray(0.25, BF16)
-    double32 = one_hot(double_targets(32, 256), 128).T
-    double64 = one_hot(double_targets(64, 384), 256).T
+    films = (film_first, film_second, film_third, film_fourth, film_fifth, film_sixth)
+    weights = (weight_first, weight_second, weight_third, weight_fourth, weight_fifth, weight_sixth)
+    rows = [((9 * w.shape[0], w.shape[1] // 9), BF16) for w in weights]
+    film, w1, w2, w3, w4, w5, w6 = call(prepare_kernel, [((544, 2), F32)] + rows, *films, *weights)
+    made = call(matrices_kernel, [(entry[0], BF16) for entry in MATRICES.values()])
+    we, wet, cm, c64, x32t, x32, c32, x16t, x16, r32, r64, double32, double64 = made
     near_moves = face_moves(0)
     far_moves = face_moves(1)
 

time: 203 us -> 191 us (0.941)
  the two profiles are of different devices: /device:TPU:1 before, /device:TPU:6 now
where the time goes in v2:
time: 191 us
  blocking collectives  77.8 us (41%)
  starting transfers between devices  50.5 us (26%)
  waiting for transfers between devices  28.8 us (15%)
  Pallas kernels  26.4 us (14%)
  between operations  3.18 us (2%)
  local copies, waits for them, and re-layouts  2.86 us (1%)
    all_to_all x5, blocking collectives, exchange(): lax.all_to_all(slots, 'patch', split_axis=0, concat_axis=0, tiled=True)  77.8 us
    ppermute x6, starting transfers between devices, exchange(): from_far = lax.ppermute(for_far, ('face', 'patch'), far_moves)  29.1 us
    ppermute x6, waiting for transfers between devices, exchange(): from_far = lax.ppermute(for_far, ('face', 'patch'), far_moves)  23.3 us
    ppermute x6, starting transfers between devices, exchange(): from_near = lax.ppermute(for_near, ('face', 'patch'), near_moves)  12.4 us
    pallas_call x9, Pallas kernels, call(): pl.pallas_call(kernel, out_shape=tuple((jax.ShapeDtypeStruct(s, t) for s,...  11.4 us
    pallas_call x12, Pallas kernels, pick(): pl.pallas_call(functools.partial(pick_kernel, specs=specs), out_shape=(sh...  9.77 us
    all_to_all x1, starting transfers between devices, exchange(): lax.all_to_all(slots, 'patch', split_axis=0, concat_axis=0, tiled=True)  9.07 us
    all_to_all x1, waiting for transfers between devices, exchange(): lax.all_to_all(slots, 'patch', split_axis=0, concat_axis=0, tiled=True)  5.49 us
  transfers between devices with their start and end apart: 13, of which 7 were waited for; matrix products, arithmetic and copies ran while one was open for 1% of the time, Pallas kernels for 6%

profile of v2, /device:TPU:6, one launch (start us, length us, event | category | flops | bytes accessed | tf_op | source)
XLA Modules:
  0.0 190.6 jit_solution(14936932705883661691)
XLA Ops:
  0.0 0.7 copy-done.7
  0.7 0.9 copy-done
  1.6 1.6 shard_map.226
  3.2 9.1 %all-to-all-start = ((bf16[32,32,128]{2,1,0:T(8,128)(2,1)}), bf16[32,32,128]{2,1,0:T(8,128)(2,1)S(1)}, u32[]{:S(2)}, u32[]{:S(2)}) async-start(bf16[32,32,128]{2,1,0:T(8,128)(2,1)} %get-tuple-element.56), calls=%async_computation | async-start | bytes 524288 | tf_op jit(solution)/shard_map/all_to_all | solution.py:510
  12.3 0.7 fusion.19
  15.8 0.1 fusion.4
  16.0 0.1 reshape.6
  16.1 0.2 fusion.12
  16.3 0.1 copy.34
  16.4 0.1 copy.35
  16.4 0.1 slice.8.code_ref
  16.5 0.2 copy.32.refs_8_
  16.8 0.2 copy-done.3
  16.9 0.5 copy-done.4
  17.4 0.4 shard_map.227
  17.8 5.5 %all-to-all-done.gathered = bf16[32,32,128]{2,1,0:T(8,128)(2,1)S(1)} async-done(((bf16[32,32,128]{2,1,0:T(8,128)(2,1)}), bf16[32,32,128]{2,1,0:T(8,128)(2,1)S(1)}, u32[]{:S(2)}, u32[]{:S(2)}) %all-to-all-start) | async-done | bytes 262176 | tf_op jit(solution)/shard_map/all_to_all | solution.py:510
  23.3 0.8 pick.13
  24.1 2.7 %collective-permute-start = (bf16[96,128]{1,0:T(8,128)(2,1)S(1)}, bf16[96,128]{1,0:T(8,128)(2,1)S(1)}, u32[]{:S(2)}, u32[]{:S(2)}) collective-permute-start(bf16[96,128]{1,0:T(8,128)(2,1)S(1)} %get-tuple-element.57), channel_id=1, source_target_pairs={{0,32},{3,35},{4,36},{7,39},{24,56},{27,59},{28,60},{31,63},{2,33}... | collective-permute-start | bytes 73736 | tf_op jit(solution)/shard_map/ppermute | solution.py:514
  26.9 3.5 %collective-permute-start.1 = (bf16[96,128]{1,0:T(8,128)(2,1)S(1)}, bf16[96,128]{1,0:T(8,128)(2,1)S(1)}, u32[]{:S(2)}, u32[]{:S(2)}) collective-permute-start(bf16[96,128]{1,0:T(8,128)(2,1)S(1)} %get-tuple-element.58), channel_id=1, source_target_pairs={{26,224},{27,225},{18,226},{19,227},{24,232},{0,240},{2,248},{3,24... | collective-permute-start | bytes 73736 | tf_op jit(solution)/shard_map/ppermute | solution.py:513
  30.4 1.4 main_conv.6.base
  31.7 0.8 shard_map.228
  32.6 0.7 pick.12.own
  33.3 3.5 %collective-permute-done.1.up = bf16[96,128]{1,0:T(8,128)(2,1)S(1)} collective-permute-done((bf16[96,128]{1,0:T(8,128)(2,1)S(1)}, bf16[96,128]{1,0:T(8,128)(2,1)S(1)}, u32[]{:S(2)}, u32[]{:S(2)}) %collective-permute-start.1) | collective-permute-done | bytes 24608 | tf_op jit(solution)/shard_map/ppermute | solution.py:513
  36.8 1.3 shard_map.229
  38.1 12.4 %all_to_all.30.gathered = bf16[32,16,128]{2,1,0:T(8,128)(2,1)S(1)} all-to-all(bf16[32,16,128]{2,1,0:T(8,128)(2,1)S(1)} %get-tuple-element.67), channel_id=1, replica_groups=mesh['face'=8,'patch'=32] {'patch'}, dimensions={0} | all-to-all | bytes 262144 | tf_op jit(solution)/shard_map/all_to_all | solution.py:510
  50.4 0.8 pick.15
  51.2 1.9 %collective-permute-start.2 = (bf16[64,128]{1,0:T(8,128)(2,1)S(1)}, bf16[64,128]{1,0:T(8,128)(2,1)S(1)}, u32[]{:S(2)}, u32[]{:S(2)}) collective-permute-start(bf16[64,128]{1,0:T(8,128)(2,1)S(1)} %get-tuple-element.68), channel_id=1, source_target_pairs={{0,32},{3,35},{4,36},{7,39},{24,56},{27,59},{28,60},{31,63},{2,33}... | collective-permute-start | bytes 49160 | tf_op jit(solution)/shard_map/ppermute | solution.py:514
  53.2 4.8 %collective-permute-start.3 = (bf16[64,128]{1,0:T(8,128)(2,1)S(1)}, bf16[64,128]{1,0:T(8,128)(2,1)S(1)}, u32[]{:S(2)}, u32[]{:S(2)}) collective-permute-start(bf16[64,128]{1,0:T(8,128)(2,1)S(1)} %get-tuple-element.69), channel_id=1, source_target_pairs={{26,224},{27,225},{18,226},{19,227},{24,232},{0,240},{2,248},{3,24... | collective-permute-start | bytes 49160 | tf_op jit(solution)/shard_map/ppermute | solution.py:513
  58.0 0.8 main_conv.7.base
  58.7 0.7 pick.14.own
  59.5 3.7 %collective-permute-done.3.up = bf16[64,128]{1,0:T(8,128)(2,1)S(1)} collective-permute-done((bf16[64,128]{1,0:T(8,128)(2,1)S(1)}, bf16[64,128]{1,0:T(8,128)(2,1)S(1)}, u32[]{:S(2)}, u32[]{:S(2)}) %collective-permute-start.3) | collective-permute-done | bytes 16416 | tf_op jit(solution)/shard_map/ppermute | solution.py:513
  63.2 1.2 shard_map.230
  64.4 11.9 %all_to_all.31.gathered = bf16[32,16,128]{2,1,0:T(8,128)(2,1)S(1)} all-to-all(bf16[32,16,128]{2,1,0:T(8,128)(2,1)S(1)} %get-tuple-element.75), channel_id=1, replica_groups=mesh['face'=8,'patch'=32] {'patch'}, dimensions={0} | all-to-all | bytes 262144 | tf_op jit(solution)/shard_map/all_to_all | solution.py:510
  76.3 0.8 pick.17
  77.1 1.9 %collective-permute-start.4 = (bf16[64,128]{1,0:T(8,128)(2,1)S(1)}, bf16[64,128]{1,0:T(8,128)(2,1)S(1)}, u32[]{:S(2)}, u32[]{:S(2)}) collective-permute-start(bf16[64,128]{1,0:T(8,128)(2,1)S(1)} %get-tuple-element.76), channel_id=1, source_target_pairs={{0,32},{3,35},{4,36},{7,39},{24,56},{27,59},{28,60},{31,63},{2,33}... | collective-permute-start | bytes 49160 | tf_op jit(solution)/shard_map/ppermute | solution.py:514
  79.1 4.8 %collective-permute-start.5 = (bf16[64,128]{1,0:T(8,128)(2,1)S(1)}, bf16[64,128]{1,0:T(8,128)(2,1)S(1)}, u32[]{:S(2)}, u32[]{:S(2)}) collective-permute-start(bf16[64,128]{1,0:T(8,128)(2,1)S(1)} %get-tuple-element.77), channel_id=1, source_target_pairs={{26,224},{27,225},{18,226},{19,227},{24,232},{0,240},{2,248},{3,24... | collective-permute-start | bytes 49160 | tf_op jit(solution)/shard_map/ppermute | solution.py:513
  83.9 0.5 main_conv.8.base
  84.4 0.8 pick.16.own
  85.2 3.9 %collective-permute-done.5.up = bf16[64,128]{1,0:T(8,128)(2,1)S(1)} collective-permute-done((bf16[64,128]{1,0:T(8,128)(2,1)S(1)}, bf16[64,128]{1,0:T(8,128)(2,1)S(1)}, u32[]{:S(2)}, u32[]{:S(2)}) %collective-permute-start.5) | collective-permute-done | bytes 16416 | tf_op jit(solution)/shard_map/ppermute | solution.py:513
  89.1 1.1 shard_map.231
  90.2 14.4 %all_to_all.32.gathered = bf16[32,32,128]{2,1,0:T(8,128)(2,1)S(1)} all-to-all(bf16[32,32,128]{2,1,0:T(8,128)(2,1)S(1)} %get-tuple-element.82), channel_id=1, replica_groups=mesh['face'=8,'patch'=32] {'patch'}, dimensions={0} | all-to-all | bytes 524288 | tf_op jit(solution)/shard_map/all_to_all | solution.py:510
  104.6 0.8 pick.19
  105.4 1.9 %collective-permute-start.6 = (bf16[128,128]{1,0:T(8,128)(2,1)S(1)}, bf16[128,128]{1,0:T(8,128)(2,1)S(1)}, u32[]{:S(2)}, u32[]{:S(2)}) collective-permute-start(bf16[128,128]{1,0:T(8,128)(2,1)S(1)} %get-tuple-element.83), channel_id=1, source_target_pairs={{0,32},{3,35},{4,36},{7,39},{24,56},{27,59},{28,60},{31,63},{2,33}... | collective-permute-start | bytes 98312 | tf_op jit(solution)/shard_map/ppermute | solution.py:514
  107.3 5.1 %collective-permute-start.7 = (bf16[128,128]{1,0:T(8,128)(2,1)S(1)}, bf16[128,128]{1,0:T(8,128)(2,1)S(1)}, u32[]{:S(2)}, u32[]{:S(2)}) collective-permute-start(bf16[128,128]{1,0:T(8,128)(2,1)S(1)} %get-tuple-element.84), channel_id=1, source_target_pairs={{26,224},{27,225},{18,226},{19,227},{24,232},{0,240},{2,248},{3,24... | collective-permute-start | bytes 98312 | tf_op jit(solution)/shard_map/ppermute | solution.py:513
  112.5 0.5 main_conv.9.base
  113.0 0.8 pick.18.own
  113.8 3.7 %collective-permute-done.7.up = bf16[128,128]{1,0:T(8,128)(2,1)S(1)} collective-permute-done((bf16[128,128]{1,0:T(8,128)(2,1)S(1)}, bf16[128,128]{1,0:T(8,128)(2,1)S(1)}, u32[]{:S(2)}, u32[]{:S(2)}) %collective-permute-start.7) | collective-permute-done | bytes 32800 | tf_op jit(solution)/shard_map/ppermute | solution.py:513
  117.5 1.4 shard_map.232
  118.9 19.5 %all_to_all.33.gathered = bf16[32,64,128]{2,1,0:T(8,128)(2,1)S(1)} all-to-all(bf16[32,64,128]{2,1,0:T(8,128)(2,1)S(1)} %get-tuple-element.90), channel_id=1, replica_groups=mesh['face'=8,'patch'=32] {'patch'}, dimensions={0} | all-to-all | bytes 1048576 | tf_op jit(solution)/shard_map/all_to_all | solution.py:510
  138.4 1.0 pick.21
  139.3 1.9 %collective-permute-start.8 = (bf16[256,128]{1,0:T(8,128)(2,1)S(1)}, bf16[256,128]{1,0:T(8,128)(2,1)S(1)}, u32[]{:S(2)}, u32[]{:S(2)}) collective-permute-start(bf16[256,128]{1,0:T(8,128)(2,1)S(1)} %get-tuple-element.91), channel_id=1, source_target_pairs={{0,32},{3,35},{4,36},{7,39},{24,56},{27,59},{28,60},{31,63},{2,33}... | collective-permute-start | bytes 196616 | tf_op jit(solution)/shard_map/ppermute | solution.py:514
  141.3 5.5 %collective-permute-start.9 = (bf16[256,128]{1,0:T(8,128)(2,1)S(1)}, bf16[256,128]{1,0:T(8,128)(2,1)S(1)}, u32[]{:S(2)}, u32[]{:S(2)}) collective-permute-start(bf16[256,128]{1,0:T(8,128)(2,1)S(1)} %get-tuple-element.92), channel_id=1, source_target_pairs={{26,224},{27,225},{18,226},{19,227},{24,232},{0,240},{2,248},{3,24... | collective-permute-start | bytes 196616 | tf_op jit(solution)/shard_map/ppermute | solution.py:513
  146.7 0.8 main_conv.10.base
  147.5 0.8 pick.20.own
  148.4 4.6 %collective-permute-done.9.up = bf16[256,128]{1,0:T(8,128)(2,1)S(1)} collective-permute-done((bf16[256,128]{1,0:T(8,128)(2,1)S(1)}, bf16[256,128]{1,0:T(8,128)(2,1)S(1)}, u32[]{:S(2)}, u32[]{:S(2)}) %collective-permute-start.9) | collective-permute-done | bytes 65568 | tf_op jit(solution)/shard_map/ppermute | solution.py:513
  153.0 2.0 %shard_map.233 = (bf16[96,4096]{1,0:T(8,128)(2,1)S(1)}, bf16[32,64,128]{2,1,0:T(8,128)(2,1)S(1)}) custom-call(f32[64,1024]{1,0:T(8,128)S(1)} %main_conv.10.base, bf16[256,128]{1,0:T(8,128)(2,1)S(1)} %pick.20.own, bf16[256,128]{1,0:T(8,128)(2,1)S(1)} %collective-permute-done.8.down, bf16[256,128]{1,0:T(8,128)(2,1)S(1)} %collective-permute-done.9.up, ...), custom_call_target="tpu_custom_call" | custom-call | tf_op jit(solution)/shard_map/pallas_call | solution.py:262
  155.1 19.7 %all_to_all.34.gathered = bf16[32,64,128]{2,1,0:T(8,128)(2,1)S(1)} all-to-all(bf16[32,64,128]{2,1,0:T(8,128)(2,1)S(1)} %get-tuple-element.99), channel_id=1, replica_groups=mesh['face'=8,'patch'=32] {'patch'}, dimensions={0} | all-to-all | bytes 1048576 | tf_op jit(solution)/shard_map/all_to_all | solution.py:510
  174.8 0.9 pick.23
  175.7 1.9 %collective-permute-start.10 = (bf16[224,128]{1,0:T(8,128)(2,1)S(1)}, bf16[224,128]{1,0:T(8,128)(2,1)S(1)}, u32[]{:S(2)}, u32[]{:S(2)}) collective-permute-start(bf16[224,128]{1,0:T(8,128)(2,1)S(1)} %get-tuple-element.100), channel_id=1, source_target_pairs={{0,32},{3,35},{4,36},{7,39},{24,56},{27,59},{28,60},{31,63},{2,33}... | collective-permute-start | bytes 172040 | tf_op jit(solution)/shard_map/ppermute | solution.py:514
  177.6 5.5 %collective-permute-start.11 = (bf16[224,128]{1,0:T(8,128)(2,1)S(1)}, bf16[224,128]{1,0:T(8,128)(2,1)S(1)}, u32[]{:S(2)}, u32[]{:S(2)}) collective-permute-start(bf16[224,128]{1,0:T(8,128)(2,1)S(1)} %get-tuple-element.101), channel_id=1, source_target_pairs={{26,224},{27,225},{18,226},{19,227},{24,232},{0,240},{2,248},{3,24... | collective-permute-start | bytes 172040 | tf_op jit(solution)/shard_map/ppermute | solution.py:513
  183.1 1.4 main_conv.11.base
  184.5 0.8 pick.22.own
  185.3 3.8 %collective-permute-done.11.up = bf16[224,128]{1,0:T(8,128)(2,1)S(1)} collective-permute-done((bf16[224,128]{1,0:T(8,128)(2,1)S(1)}, bf16[224,128]{1,0:T(8,128)(2,1)S(1)}, u32[]{:S(2)}, u32[]{:S(2)}) %collective-permute-start.11) | collective-permute-done | bytes 57376 | tf_op jit(solution)/shard_map/ppermute | solution.py:513
  189.1 1.5 shard_map.234
  (52 shorter events, 0.2 us)
Async XLA Ops:
  0.0 0.7 copy-start.7
  0.7 0.9 copy-start
  3.2 9.1 %copy-start.22 = (s32[32]{0:T(128)S(1)}, s32[32]{0:T(128)}, u32[]{:S(2)}) copy-start(s32[32]{0:T(128)} %constant.166.clone) | copy-start | bytes 388
  3.2 9.1 %copy-start.23 = (s32[32]{0:T(128)S(1)}, s32[32]{0:T(128)}, u32[]{:S(2)}) copy-start(s32[32]{0:T(128)} %constant.165.clone) | copy-start | bytes 388
  3.2 12.6 %copy-start.16 = (s32[8,32,8]{1,2,0:T(8,128)S(1)}, s32[8,32,8]{1,2,0:T(8,128)}, u32[]{:S(2)}) copy-start(s32[8,32,8]{1,2,0:T(8,128)} %param.39) | copy-start | bytes 24580
  3.2 13.3 %copy-start.13 = (bf16[128,576]{0,1:T(8,128)(2,1)S(1)}, bf16[128,576]{0,1:T(8,128)(2,1)}, u32[]{:S(2)}) copy-start(bf16[128,576]{0,1:T(8,128)(2,1)} %param.30) | copy-start | bytes 442372
  3.2 20.1 %all-to-all-start = ((bf16[32,32,128]{2,1,0:T(8,128)(2,1)}), bf16[32,32,128]{2,1,0:T(8,128)(2,1)S(1)}, u32[]{:S(2)}, u32[]{:S(2)}) async-start(bf16[32,32,128]{2,1,0:T(8,128)(2,1)} %get-tuple-element.56), calls=%async_computation | async-start | bytes 524288 | tf_op jit(solution)/shard_map/all_to_all | solution.py:510
  12.3 3.5 %copy-start.15 = (s32[8,32,8]{1,2,0:T(8,128)S(1)}, s32[8,32,8]{1,2,0:T(8,128)}, u32[]{:S(2)}) copy-start(s32[8,32,8]{1,2,0:T(8,128)} %param.37) | copy-start | bytes 24580
  13.0 2.8 %copy-start.19 = (s32[8]{0:T(128)S(1)}, s32[8]{0:T(128)}, u32[]{:S(2)}) copy-start(s32[8]{0:T(128)} %constant.162.clone) | copy-start | bytes 100
  13.0 2.8 %copy-start.20 = (s32[8]{0:T(128)S(1)}, s32[8]{0:T(128)}, u32[]{:S(2)}) copy-start(s32[8]{0:T(128)} %constant.161.clone) | copy-start | bytes 100
  13.0 2.8 %copy-start.21 = (s32[8]{0:T(128)S(1)}, s32[8]{0:T(128)}, u32[]{:S(2)}) copy-start(s32[8]{0:T(128)} %constant.160.clone) | copy-start | bytes 100
  13.0 2.8 %copy-start.14 = (s32[8,32,8]{1,2,0:T(8,128)S(1)}, s32[8,32,8]{1,2,0:T(8,128)}, u32[]{:S(2)}) copy-start(s32[8,32,8]{1,2,0:T(8,128)} %param.38) | copy-start | bytes 24580
  13.0 2.8 %copy-start.18 = (s32[8]{0:T(128)S(1)}, s32[8]{0:T(128)}, u32[]{:S(2)}) copy-start(s32[8]{0:T(128)} %constant.163.clone) | copy-start | bytes 100
  13.0 3.7 %copy-start.6 = (bf16[32,288]{1,0:T(8,128)(2,1)S(1)}, bf16[32,288]{1,0:T(8,128)(2,1)}, u32[]{:S(2)}) copy-start(bf16[32,288]{1,0:T(8,128)(2,1)} %refs_6_.1) | copy-start | bytes 55300
  13.0 3.7 %copy-start.8 = (f32[2,192]{1,0:T(2,128)S(1)}, f32[2,192]{1,0:T(2,128)}, u32[]{:S(2)}) copy-start(f32[2,192]{1,0:T(2,128)} %refs_4_.1) | copy-start | bytes 4612
  13.0 3.7 %copy-start.9 = (f32[2,32]{1,0:T(2,128)S(1)}, f32[2,32]{1,0:T(2,128)}, u32[]{:S(2)}) copy-start(f32[2,32]{1,0:T(2,128)} %refs_1_.1) | copy-start | bytes 772
  13.1 3.7 %copy-start.10 = (f32[2,64]{1,0:T(2,128)S(1)}, f32[2,64]{1,0:T(2,128)}, u32[]{:S(2)}) copy-start(f32[2,64]{1,0:T(2,128)} %refs_2_.1) | copy-start | bytes 1540
  13.1 3.7 %copy-start.11 = (f32[2,128]{1,0:T(2,128)S(1)}, f32[2,128]{1,0:T(2,128)}, u32[]{:S(2)}) copy-start(f32[2,128]{1,0:T(2,128)} %refs_3_.1) | copy-start | bytes 3076
  13.1 3.7 %copy-start.12 = (f32[2,96]{1,0:T(2,128)S(1)}, f32[2,96]{1,0:T(2,128)}, u32[]{:S(2)}) copy-start(f32[2,96]{1,0:T(2,128)} %refs_5_.1) | copy-start | bytes 2308
  13.1 2.7 %copy-start.17 = (pred[8]{0:T(512)(128)(4,1)S(1)}, pred[8]{0:T(512)(128)(4,1)}, u32[]{:S(2)}) copy-start(pred[8]{0:T(512)(128)(4,1)} %constant.164.clone) | copy-start | bytes 28
  14.3 2.4 %copy-start.5 = (bf16[64,288]{1,0:T(8,128)(2,1)S(1)}, bf16[64,288]{1,0:T(8,128)(2,1)}, u32[]{:S(2)}) copy-start(bf16[64,288]{1,0:T(8,128)(2,1)} %refs_7_.1) | copy-start | bytes 110596
  15.8 1.0 copy-start.2
  16.0 1.0 copy-start.3
  16.5 0.9 copy-start.4
  24.1 9.2 %collective-permute-start = (bf16[96,128]{1,0:T(8,128)(2,1)S(1)}, bf16[96,128]{1,0:T(8,128)(2,1)S(1)}, u32[]{:S(2)}, u32[]{:S(2)}) collective-permute-start(bf16[96,128]{1,0:T(8,128)(2,1)S(1)} %get-tuple-element.57), channel_id=1, source_target_pairs={{0,32},{3,35},{4,36},{7,39},{24,56},{27,59},{28,60},{31,63},{2,33}... | collective-permute-start | bytes 73736 | tf_op jit(solution)/shard_map/ppermute | solution.py:514
  26.9 9.9 %collective-permute-start.1 = (bf16[96,128]{1,0:T(8,128)(2,1)S(1)}, bf16[96,128]{1,0:T(8,128)(2,1)S(1)}, u32[]{:S(2)}, u32[]{:S(2)}) collective-permute-start(bf16[96,128]{1,0:T(8,128)(2,1)S(1)} %get-tuple-element.58), channel_id=1, source_target_pairs={{26,224},{27,225},{18,226},{19,227},{24,232},{0,240},{2,248},{3,24... | collective-permute-start | bytes 73736 | tf_op jit(solution)/shard_map/ppermute | solution.py:513
  31.7 5.1 %copy-start.1 = (bf16[32,1,4096]{2,0,1:T(8,128)(2,1)S(1)}, bf16[32,1,4096]{2,0,1:T(8,128)(2,1)}, u32[]{:S(2)}) copy-start(bf16[32,1,4096]{2,0,1:T(8,128)(2,1)} %param.24) | copy-start | bytes 786436
  51.2 8.2 %collective-permute-start.2 = (bf16[64,128]{1,0:T(8,128)(2,1)S(1)}, bf16[64,128]{1,0:T(8,128)(2,1)S(1)}, u32[]{:S(2)}, u32[]{:S(2)}) collective-permute-start(bf16[64,128]{1,0:T(8,128)(2,1)S(1)} %get-tuple-element.68), channel_id=1, source_target_pairs={{0,32},{3,35},{4,36},{7,39},{24,56},{27,59},{28,60},{31,63},{2,33}... | collective-permute-start | bytes 49160 | tf_op jit(solution)/shard_map/ppermute | solution.py:514
  53.2 10.0 %collective-permute-start.3 = (bf16[64,128]{1,0:T(8,128)(2,1)S(1)}, bf16[64,128]{1,0:T(8,128)(2,1)S(1)}, u32[]{:S(2)}, u32[]{:S(2)}) collective-permute-start(bf16[64,128]{1,0:T(8,128)(2,1)S(1)} %get-tuple-element.69), channel_id=1, source_target_pairs={{26,224},{27,225},{18,226},{19,227},{24,232},{0,240},{2,248},{3,24... | collective-permute-start | bytes 49160 | tf_op jit(solution)/shard_map/ppermute | solution.py:513
  77.1 8.0 %collective-permute-start.4 = (bf16[64,128]{1,0:T(8,128)(2,1)S(1)}, bf16[64,128]{1,0:T(8,128)(2,1)S(1)}, u32[]{:S(2)}, u32[]{:S(2)}) collective-permute-start(bf16[64,128]{1,0:T(8,128)(2,1)S(1)} %get-tuple-element.76), channel_id=1, source_target_pairs={{0,32},{3,35},{4,36},{7,39},{24,56},{27,59},{28,60},{31,63},{2,33}... | collective-permute-start | bytes 49160 | tf_op jit(solution)/shard_map/ppermute | solution.py:514
  79.1 10.0 %collective-permute-start.5 = (bf16[64,128]{1,0:T(8,128)(2,1)S(1)}, bf16[64,128]{1,0:T(8,128)(2,1)S(1)}, u32[]{:S(2)}, u32[]{:S(2)}) collective-permute-start(bf16[64,128]{1,0:T(8,128)(2,1)S(1)} %get-tuple-element.77), channel_id=1, source_target_pairs={{26,224},{27,225},{18,226},{19,227},{24,232},{0,240},{2,248},{3,24... | collective-permute-start | bytes 49160 | tf_op jit(solution)/shard_map/ppermute | solution.py:513
  105.4 8.4 %collective-permute-start.6 = (bf16[128,128]{1,0:T(8,128)(2,1)S(1)}, bf16[128,128]{1,0:T(8,128)(2,1)S(1)}, u32[]{:S(2)}, u32[]{:S(2)}) collective-permute-start(bf16[128,128]{1,0:T(8,128)(2,1)S(1)} %get-tuple-element.83), channel_id=1, source_target_pairs={{0,32},{3,35},{4,36},{7,39},{24,56},{27,59},{28,60},{31,63},{2,33}... | collective-permute-start | bytes 98312 | tf_op jit(solution)/shard_map/ppermute | solution.py:514
  107.3 10.1 %collective-permute-start.7 = (bf16[128,128]{1,0:T(8,128)(2,1)S(1)}, bf16[128,128]{1,0:T(8,128)(2,1)S(1)}, u32[]{:S(2)}, u32[]{:S(2)}) collective-permute-start(bf16[128,128]{1,0:T(8,128)(2,1)S(1)} %get-tuple-element.84), channel_id=1, source_target_pairs={{26,224},{27,225},{18,226},{19,227},{24,232},{0,240},{2,248},{3,24... | collective-permute-start | bytes 98312 | tf_op jit(solution)/shard_map/ppermute | solution.py:513
  139.3 9.0 %collective-permute-start.8 = (bf16[256,128]{1,0:T(8,128)(2,1)S(1)}, bf16[256,128]{1,0:T(8,128)(2,1)S(1)}, u32[]{:S(2)}, u32[]{:S(2)}) collective-permute-start(bf16[256,128]{1,0:T(8,128)(2,1)S(1)} %get-tuple-element.91), channel_id=1, source_target_pairs={{0,32},{3,35},{4,36},{7,39},{24,56},{27,59},{28,60},{31,63},{2,33}... | collective-permute-start | bytes 196616 | tf_op jit(solution)/shard_map/ppermute | solution.py:514
  141.3 11.8 %collective-permute-start.9 = (bf16[256,128]{1,0:T(8,128)(2,1)S(1)}, bf16[256,128]{1,0:T(8,128)(2,1)S(1)}, u32[]{:S(2)}, u32[]{:S(2)}) collective-permute-start(bf16[256,128]{1,0:T(8,128)(2,1)S(1)} %get-tuple-element.92), channel_id=1, source_target_pairs={{26,224},{27,225},{18,226},{19,227},{24,232},{0,240},{2,248},{3,24... | collective-permute-start | bytes 196616 | tf_op jit(solution)/shard_map/ppermute | solution.py:513
  175.7 9.6 %collective-permute-start.10 = (bf16[224,128]{1,0:T(8,128)(2,1)S(1)}, bf16[224,128]{1,0:T(8,128)(2,1)S(1)}, u32[]{:S(2)}, u32[]{:S(2)}) collective-permute-start(bf16[224,128]{1,0:T(8,128)(2,1)S(1)} %get-tuple-element.100), channel_id=1, source_target_pairs={{0,32},{3,35},{4,36},{7,39},{24,56},{27,59},{28,60},{31,63},{2,33}... | collective-permute-start | bytes 172040 | tf_op jit(solution)/shard_map/ppermute | solution.py:514
  177.6 11.5 %collective-permute-start.11 = (bf16[224,128]{1,0:T(8,128)(2,1)S(1)}, bf16[224,128]{1,0:T(8,128)(2,1)S(1)}, u32[]{:S(2)}, u32[]{:S(2)}) collective-permute-start(bf16[224,128]{1,0:T(8,128)(2,1)S(1)} %get-tuple-element.101), channel_id=1, source_target_pairs={{26,224},{27,225},{18,226},{19,227},{24,232},{0,240},{2,248},{3,24... | collective-permute-start | bytes 172040 | tf_op jit(solution)/shard_map/ppermute | solution.py:513

commit v3 on v2

--- a/solution.py
+++ b/solution.py
@@ -413,10 +413,17 @@
             out[t * out_channels : (t + 1) * out_channels, :] = weight[:, t * channels : (t + 1) * channels]
 
 
-NEAR_RELAY = {p: p for p in (0, 3, 4, 7, 24, 27, 28, 31)}
-NEAR_RELAY |= {1: 2, 2: 10, 8: 11, 6: 5, 5: 13, 15: 12, 25: 26, 26: 18, 16: 19, 30: 29, 29: 21, 23: 20}
-FAR_RELAY = {0: 26, 1: 27, 2: 18, 3: 19, 8: 24, 16: 0, 24: 2, 25: 3, 26: 10, 27: 11}
-FAR_RELAY |= {7: 29, 6: 28, 5: 21, 4: 20, 15: 31, 23: 7, 31: 5, 30: 4, 29: 13, 28: 12}
+def swaps(left):
+    pairs = {}
+    for one, other in left:
+        for a, b in ((one, other), (other, one)):
+            pairs[a] = b
+            pairs[a // 8 * 8 + 7 - a % 8] = b // 8 * 8 + 7 - b % 8
+    return pairs
+
+
+NEAR_RELAY = {p: p for p in range(32)} | swaps([(1, 11), (8, 10), (16, 18), (25, 19)])
+FAR_RELAY = swaps([(0, 24), (2, 26), (3, 27), (1, 19), (25, 11), (8, 18), (16, 10), (9, 17)])
 
 
 def other_face(face, kind):

time: 191 us -> 176 us (0.921)
  the two profiles are of different devices: /device:TPU:6 before, /device:TPU:39 now
where the time goes in v3:
time: 176 us; the launch traced here: 173 us
  blocking collectives  86.5 us (49%)
  starting transfers between devices  34.3 us (19%)
  Pallas kernels  26.4 us (15%)
  waiting for transfers between devices  18.8 us (11%)
  between operations  3.13 us (2%)
  local copies, waits for them, and re-layouts  2.86 us (2%)
    all_to_all x5, blocking collectives, exchange(): lax.all_to_all(slots, 'patch', split_axis=0, concat_axis=0, tiled=True)  86.5 us
    ppermute x6, starting transfers between devices, exchange(): from_far = lax.ppermute(for_far, ('face', 'patch'), far_moves)  24 us
    ppermute x6, waiting for transfers between devices, exchange(): from_far = lax.ppermute(for_far, ('face', 'patch'), far_moves)  14.2 us
    pallas_call x9, Pallas kernels, call(): pl.pallas_call(kernel, out_shape=tuple((jax.ShapeDtypeStruct(s, t) for s,...  11.3 us
    pallas_call x12, Pallas kernels, pick(): pl.pallas_call(functools.partial(pick_kernel, specs=specs), out_shape=(sh...  9.77 us
    all_to_all x1, starting transfers between devices, exchange(): lax.all_to_all(slots, 'patch', split_axis=0, concat_axis=0, tiled=True)  9.22 us
    pallas_call x6, Pallas kernels, main_conv(): pl.pallas_call(functools.partial(main_kernel, length=length), out_shape=j...  5.31 us
    all_to_all x1, waiting for transfers between devices, exchange(): lax.all_to_all(slots, 'patch', split_axis=0, concat_axis=0, tiled=True)  4.6 us
  transfers between devices with their start and end apart: 13, of which 7 were waited for; matrix products, arithmetic and copies ran while one was open for 1% of the time, Pallas kernels for 6%

profile of v3, /device:TPU:39, one launch (start us, length us, event | category | flops | bytes accessed | tf_op | source)
XLA Modules:
  0.0 173.0 jit_solution(11002197155212271491)
XLA Ops:
  0.0 0.7 copy-done.7
  0.7 0.9 copy-done
  1.6 1.6 shard_map.226
  3.2 9.2 %all-to-all-start = ((bf16[32,32,128]{2,1,0:T(8,128)(2,1)}), bf16[32,32,128]{2,1,0:T(8,128)(2,1)S(1)}, u32[]{:S(2)}, u32[]{:S(2)}) async-start(bf16[32,32,128]{2,1,0:T(8,128)(2,1)} %get-tuple-element.56), calls=%async_computation | async-start | bytes 524288 | tf_op jit(solution)/shard_map/all_to_all | solution.py:517
  12.5 0.7 fusion.19
  16.0 0.1 fusion.4
  16.2 0.1 reshape.6
  16.2 0.2 fusion.12
  16.4 0.1 copy.34
  16.5 0.1 copy.35
  16.6 0.1 slice.8.code_ref
  16.7 0.2 copy.32.refs_8_
  16.9 0.2 copy-done.3
  17.1 0.5 copy-done.4
  17.6 0.4 shard_map.227
  18.0 4.6 %all-to-all-done.gathered = bf16[32,32,128]{2,1,0:T(8,128)(2,1)S(1)} async-done(((bf16[32,32,128]{2,1,0:T(8,128)(2,1)}), bf16[32,32,128]{2,1,0:T(8,128)(2,1)S(1)}, u32[]{:S(2)}, u32[]{:S(2)}) %all-to-all-start) | async-done | bytes 262176 | tf_op jit(solution)/shard_map/all_to_all | solution.py:517
  22.6 0.8 pick.13
  23.4 0.6 collective-permute-start
  24.0 3.9 %collective-permute-start.1 = (bf16[96,128]{1,0:T(8,128)(2,1)S(1)}, bf16[96,128]{1,0:T(8,128)(2,1)S(1)}, u32[]{:S(2)}, u32[]{:S(2)}) collective-permute-start(bf16[96,128]{1,0:T(8,128)(2,1)S(1)} %get-tuple-element.58), channel_id=1, source_target_pairs={{24,224},{31,231},{0,248},{7,255},{26,226},{29,229},{2,250},{5,253... | collective-permute-start | bytes 73736 | tf_op jit(solution)/shard_map/ppermute | solution.py:520
  27.9 1.3 main_conv.6.base
  29.3 0.8 shard_map.228
  30.1 0.7 pick.12.own
  30.9 1.1 collective-permute-done.1.up
  31.9 1.3 shard_map.229
  33.2 14.0 %all_to_all.30.gathered = bf16[32,16,128]{2,1,0:T(8,128)(2,1)S(1)} all-to-all(bf16[32,16,128]{2,1,0:T(8,128)(2,1)S(1)} %get-tuple-element.67), channel_id=1, replica_groups=mesh['face'=8,'patch'=32] {'patch'}, dimensions={0} | all-to-all | bytes 262144 | tf_op jit(solution)/shard_map/all_to_all | solution.py:517
  47.2 0.8 pick.15
  48.0 0.1 collective-permute-start.2
  48.1 4.1 %collective-permute-start.3 = (bf16[64,128]{1,0:T(8,128)(2,1)S(1)}, bf16[64,128]{1,0:T(8,128)(2,1)S(1)}, u32[]{:S(2)}, u32[]{:S(2)}) collective-permute-start(bf16[64,128]{1,0:T(8,128)(2,1)S(1)} %get-tuple-element.69), channel_id=1, source_target_pairs={{24,224},{31,231},{0,248},{7,255},{26,226},{29,229},{2,250},{5,253... | collective-permute-start | bytes 49160 | tf_op jit(solution)/shard_map/ppermute | solution.py:520
  52.2 0.8 main_conv.7.base
  52.9 0.7 pick.14.own
  53.7 2.2 %collective-permute-done.3.up = bf16[64,128]{1,0:T(8,128)(2,1)S(1)} collective-permute-done((bf16[64,128]{1,0:T(8,128)(2,1)S(1)}, bf16[64,128]{1,0:T(8,128)(2,1)S(1)}, u32[]{:S(2)}, u32[]{:S(2)}) %collective-permute-start.3) | collective-permute-done | bytes 16416 | tf_op jit(solution)/shard_map/ppermute | solution.py:520
  55.9 1.2 shard_map.230
  57.1 13.2 %all_to_all.31.gathered = bf16[32,16,128]{2,1,0:T(8,128)(2,1)S(1)} all-to-all(bf16[32,16,128]{2,1,0:T(8,128)(2,1)S(1)} %get-tuple-element.75), channel_id=1, replica_groups=mesh['face'=8,'patch'=32] {'patch'}, dimensions={0} | all-to-all | bytes 262144 | tf_op jit(solution)/shard_map/all_to_all | solution.py:517
  70.4 0.8 pick.17
  71.2 0.1 collective-permute-start.4
  71.3 4.3 %collective-permute-start.5 = (bf16[64,128]{1,0:T(8,128)(2,1)S(1)}, bf16[64,128]{1,0:T(8,128)(2,1)S(1)}, u32[]{:S(2)}, u32[]{:S(2)}) collective-permute-start(bf16[64,128]{1,0:T(8,128)(2,1)S(1)} %get-tuple-element.77), channel_id=1, source_target_pairs={{24,224},{31,231},{0,248},{7,255},{26,226},{29,229},{2,250},{5,253... | collective-permute-start | bytes 49160 | tf_op jit(solution)/shard_map/ppermute | solution.py:520
  75.6 0.5 main_conv.8.base
  76.1 0.8 pick.16.own
  76.9 2.5 %collective-permute-done.5.up = bf16[64,128]{1,0:T(8,128)(2,1)S(1)} collective-permute-done((bf16[64,128]{1,0:T(8,128)(2,1)S(1)}, bf16[64,128]{1,0:T(8,128)(2,1)S(1)}, u32[]{:S(2)}, u32[]{:S(2)}) %collective-permute-start.5) | collective-permute-done | bytes 16416 | tf_op jit(solution)/shard_map/ppermute | solution.py:520
  79.4 1.1 shard_map.231
  80.5 16.2 %all_to_all.32.gathered = bf16[32,32,128]{2,1,0:T(8,128)(2,1)S(1)} all-to-all(bf16[32,32,128]{2,1,0:T(8,128)(2,1)S(1)} %get-tuple-element.82), channel_id=1, replica_groups=mesh['face'=8,'patch'=32] {'patch'}, dimensions={0} | all-to-all | bytes 524288 | tf_op jit(solution)/shard_map/all_to_all | solution.py:517
  96.7 0.8 pick.19
  97.5 0.1 collective-permute-start.6
  97.6 4.0 %collective-permute-start.7 = (bf16[128,128]{1,0:T(8,128)(2,1)S(1)}, bf16[128,128]{1,0:T(8,128)(2,1)S(1)}, u32[]{:S(2)}, u32[]{:S(2)}) collective-permute-start(bf16[128,128]{1,0:T(8,128)(2,1)S(1)} %get-tuple-element.84), channel_id=1, source_target_pairs={{24,224},{31,231},{0,248},{7,255},{26,226},{29,229},{2,250},{5,253... | collective-permute-start | bytes 98312 | tf_op jit(solution)/shard_map/ppermute | solution.py:520
  101.6 0.5 main_conv.9.base
  102.1 0.8 pick.18.own
  102.9 2.7 %collective-permute-done.7.up = bf16[128,128]{1,0:T(8,128)(2,1)S(1)} collective-permute-done((bf16[128,128]{1,0:T(8,128)(2,1)S(1)}, bf16[128,128]{1,0:T(8,128)(2,1)S(1)}, u32[]{:S(2)}, u32[]{:S(2)}) %collective-permute-start.7) | collective-permute-done | bytes 32800 | tf_op jit(solution)/shard_map/ppermute | solution.py:520
  105.6 1.4 shard_map.232
  107.0 21.2 %all_to_all.33.gathered = bf16[32,64,128]{2,1,0:T(8,128)(2,1)S(1)} all-to-all(bf16[32,64,128]{2,1,0:T(8,128)(2,1)S(1)} %get-tuple-element.90), channel_id=1, replica_groups=mesh['face'=8,'patch'=32] {'patch'}, dimensions={0} | all-to-all | bytes 1048576 | tf_op jit(solution)/shard_map/all_to_all | solution.py:517
  128.2 1.0 pick.21
  129.2 0.1 collective-permute-start.8
  129.3 3.9 %collective-permute-start.9 = (bf16[256,128]{1,0:T(8,128)(2,1)S(1)}, bf16[256,128]{1,0:T(8,128)(2,1)S(1)}, u32[]{:S(2)}, u32[]{:S(2)}) collective-permute-start(bf16[256,128]{1,0:T(8,128)(2,1)S(1)} %get-tuple-element.92), channel_id=1, source_target_pairs={{24,224},{31,231},{0,248},{7,255},{26,226},{29,229},{2,250},{5,253... | collective-permute-start | bytes 196616 | tf_op jit(solution)/shard_map/ppermute | solution.py:520
  133.2 0.8 main_conv.10.base
  134.0 0.8 pick.20.own
  134.8 2.9 %collective-permute-done.9.up = bf16[256,128]{1,0:T(8,128)(2,1)S(1)} collective-permute-done((bf16[256,128]{1,0:T(8,128)(2,1)S(1)}, bf16[256,128]{1,0:T(8,128)(2,1)S(1)}, u32[]{:S(2)}, u32[]{:S(2)}) %collective-permute-start.9) | collective-permute-done | bytes 65568 | tf_op jit(solution)/shard_map/ppermute | solution.py:520
  137.7 2.0 %shard_map.233 = (bf16[96,4096]{1,0:T(8,128)(2,1)S(1)}, bf16[32,64,128]{2,1,0:T(8,128)(2,1)S(1)}) custom-call(f32[64,1024]{1,0:T(8,128)S(1)} %main_conv.10.base, bf16[256,128]{1,0:T(8,128)(2,1)S(1)} %pick.20.own, bf16[256,128]{1,0:T(8,128)(2,1)S(1)} %collective-permute-done.8.down, bf16[256,128]{1,0:T(8,128)(2,1)S(1)} %collective-permute-done.9.up, ...), custom_call_target="tpu_custom_call" | custom-call | tf_op jit(solution)/shard_map/pallas_call | solution.py:262
  139.8 21.9 %all_to_all.34.gathered = bf16[32,64,128]{2,1,0:T(8,128)(2,1)S(1)} all-to-all(bf16[32,64,128]{2,1,0:T(8,128)(2,1)S(1)} %get-tuple-element.99), channel_id=1, replica_groups=mesh['face'=8,'patch'=32] {'patch'}, dimensions={0} | all-to-all | bytes 1048576 | tf_op jit(solution)/shard_map/all_to_all | solution.py:517
  161.6 0.9 pick.23
  162.6 0.1 collective-permute-start.10
  162.7 3.9 %collective-permute-start.11 = (bf16[224,128]{1,0:T(8,128)(2,1)S(1)}, bf16[224,128]{1,0:T(8,128)(2,1)S(1)}, u32[]{:S(2)}, u32[]{:S(2)}) collective-permute-start(bf16[224,128]{1,0:T(8,128)(2,1)S(1)} %get-tuple-element.101), channel_id=1, source_target_pairs={{24,224},{31,231},{0,248},{7,255},{26,226},{29,229},{2,250},{5,253... | collective-permute-start | bytes 172040 | tf_op jit(solution)/shard_map/ppermute | solution.py:520
  166.6 1.4 main_conv.11.base
  168.0 0.8 pick.22.own
  168.8 2.8 %collective-permute-done.11.up = bf16[224,128]{1,0:T(8,128)(2,1)S(1)} collective-permute-done((bf16[224,128]{1,0:T(8,128)(2,1)S(1)}, bf16[224,128]{1,0:T(8,128)(2,1)S(1)}, u32[]{:S(2)}, u32[]{:S(2)}) %collective-permute-start.11) | collective-permute-done | bytes 57376 | tf_op jit(solution)/shard_map/ppermute | solution.py:520
  171.5 1.5 shard_map.234
  (52 shorter events, 0.2 us)
Async XLA Ops:
  0.0 0.7 copy-start.7
  0.7 0.9 copy-start
  3.2 9.3 %copy-start.22 = (s32[32]{0:T(128)S(1)}, s32[32]{0:T(128)}, u32[]{:S(2)}) copy-start(s32[32]{0:T(128)} %constant.166.clone) | copy-start | bytes 388
  3.2 9.3 %copy-start.23 = (s32[32]{0:T(128)S(1)}, s32[32]{0:T(128)}, u32[]{:S(2)}) copy-start(s32[32]{0:T(128)} %constant.165.clone) | copy-start | bytes 388
  3.2 12.7 %copy-start.16 = (s32[8,32,8]{1,2,0:T(8,128)S(1)}, s32[8,32,8]{1,2,0:T(8,128)}, u32[]{:S(2)}) copy-start(s32[8,32,8]{1,2,0:T(8,128)} %param.39) | copy-start | bytes 24580
  3.2 13.5 %copy-start.13 = (bf16[128,576]{0,1:T(8,128)(2,1)S(1)}, bf16[128,576]{0,1:T(8,128)(2,1)}, u32[]{:S(2)}) copy-start(bf16[128,576]{0,1:T(8,128)(2,1)} %param.30) | copy-start | bytes 442372
  3.2 19.4 %all-to-all-start = ((bf16[32,32,128]{2,1,0:T(8,128)(2,1)}), bf16[32,32,128]{2,1,0:T(8,128)(2,1)S(1)}, u32[]{:S(2)}, u32[]{:S(2)}) async-start(bf16[32,32,128]{2,1,0:T(8,128)(2,1)} %get-tuple-element.56), calls=%async_computation | async-start | bytes 524288 | tf_op jit(solution)/shard_map/all_to_all | solution.py:517
  12.4 3.5 %copy-start.15 = (s32[8,32,8]{1,2,0:T(8,128)S(1)}, s32[8,32,8]{1,2,0:T(8,128)}, u32[]{:S(2)}) copy-start(s32[8,32,8]{1,2,0:T(8,128)} %param.37) | copy-start | bytes 24580
  13.2 2.8 %copy-start.19 = (s32[8]{0:T(128)S(1)}, s32[8]{0:T(128)}, u32[]{:S(2)}) copy-start(s32[8]{0:T(128)} %constant.162.clone) | copy-start | bytes 100
  13.2 2.8 %copy-start.20 = (s32[8]{0:T(128)S(1)}, s32[8]{0:T(128)}, u32[]{:S(2)}) copy-start(s32[8]{0:T(128)} %constant.161.clone) | copy-start | bytes 100
  13.2 2.8 %copy-start.21 = (s32[8]{0:T(128)S(1)}, s32[8]{0:T(128)}, u32[]{:S(2)}) copy-start(s32[8]{0:T(128)} %constant.160.clone) | copy-start | bytes 100
  13.2 2.8 %copy-start.14 = (s32[8,32,8]{1,2,0:T(8,128)S(1)}, s32[8,32,8]{1,2,0:T(8,128)}, u32[]{:S(2)}) copy-start(s32[8,32,8]{1,2,0:T(8,128)} %param.38) | copy-start | bytes 24580
  13.2 2.8 %copy-start.18 = (s32[8]{0:T(128)S(1)}, s32[8]{0:T(128)}, u32[]{:S(2)}) copy-start(s32[8]{0:T(128)} %constant.163.clone) | copy-start | bytes 100
  13.2 3.7 %copy-start.6 = (bf16[32,288]{1,0:T(8,128)(2,1)S(1)}, bf16[32,288]{1,0:T(8,128)(2,1)}, u32[]{:S(2)}) copy-start(bf16[32,288]{1,0:T(8,128)(2,1)} %refs_6_.1) | copy-start | bytes 55300
  13.2 3.7 %copy-start.8 = (f32[2,192]{1,0:T(2,128)S(1)}, f32[2,192]{1,0:T(2,128)}, u32[]{:S(2)}) copy-start(f32[2,192]{1,0:T(2,128)} %refs_4_.1) | copy-start | bytes 4612
  13.2 3.7 %copy-start.9 = (f32[2,32]{1,0:T(2,128)S(1)}, f32[2,32]{1,0:T(2,128)}, u32[]{:S(2)}) copy-start(f32[2,32]{1,0:T(2,128)} %refs_1_.1) | copy-start | bytes 772
  13.2 3.7 %copy-start.10 = (f32[2,64]{1,0:T(2,128)S(1)}, f32[2,64]{1,0:T(2,128)}, u32[]{:S(2)}) copy-start(f32[2,64]{1,0:T(2,128)} %refs_2_.1) | copy-start | bytes 1540
  13.2 3.7 %copy-start.11 = (f32[2,128]{1,0:T(2,128)S(1)}, f32[2,128]{1,0:T(2,128)}, u32[]{:S(2)}) copy-start(f32[2,128]{1,0:T(2,128)} %refs_3_.1) | copy-start | bytes 3076
  13.2 3.7 %copy-start.12 = (f32[2,96]{1,0:T(2,128)S(1)}, f32[2,96]{1,0:T(2,128)}, u32[]{:S(2)}) copy-start(f32[2,96]{1,0:T(2,128)} %refs_5_.1) | copy-start | bytes 2308
  13.3 2.7 %copy-start.17 = (pred[8]{0:T(512)(128)(4,1)S(1)}, pred[8]{0:T(512)(128)(4,1)}, u32[]{:S(2)}) copy-start(pred[8]{0:T(512)(128)(4,1)} %constant.164.clone) | copy-start | bytes 28
  14.5 2.4 %copy-start.5 = (bf16[64,288]{1,0:T(8,128)(2,1)S(1)}, bf16[64,288]{1,0:T(8,128)(2,1)}, u32[]{:S(2)}) copy-start(bf16[64,288]{1,0:T(8,128)(2,1)} %refs_7_.1) | copy-start | bytes 110596
  16.0 1.0 copy-start.2
  16.1 1.0 copy-start.3
  16.7 0.9 copy-start.4
  23.4 7.5 %collective-permute-start = (bf16[96,128]{1,0:T(8,128)(2,1)S(1)}, bf16[96,128]{1,0:T(8,128)(2,1)S(1)}, u32[]{:S(2)}, u32[]{:S(2)}) collective-permute-start(bf16[96,128]{1,0:T(8,128)(2,1)S(1)} %get-tuple-element.57), channel_id=1, source_target_pairs={{0,32},{11,33},{2,34},{3,35},{4,36},{5,37},{12,38},{7,39},{10,40},... | collective-permute-start | bytes 73736 | tf_op jit(solution)/shard_map/ppermute | solution.py:521
  24.0 7.9 %collective-permute-start.1 = (bf16[96,128]{1,0:T(8,128)(2,1)S(1)}, bf16[96,128]{1,0:T(8,128)(2,1)S(1)}, u32[]{:S(2)}, u32[]{:S(2)}) collective-permute-start(bf16[96,128]{1,0:T(8,128)(2,1)S(1)} %get-tuple-element.58), channel_id=1, source_target_pairs={{24,224},{31,231},{0,248},{7,255},{26,226},{29,229},{2,250},{5,253... | collective-permute-start | bytes 73736 | tf_op jit(solution)/shard_map/ppermute | solution.py:520
  29.2 2.7 %copy-start.1 = (bf16[32,1,4096]{2,0,1:T(8,128)(2,1)S(1)}, bf16[32,1,4096]{2,0,1:T(8,128)(2,1)}, u32[]{:S(2)}) copy-start(bf16[32,1,4096]{2,0,1:T(8,128)(2,1)} %param.24) | copy-start | bytes 786436
  48.0 5.7 %collective-permute-start.2 = (bf16[64,128]{1,0:T(8,128)(2,1)S(1)}, bf16[64,128]{1,0:T(8,128)(2,1)S(1)}, u32[]{:S(2)}, u32[]{:S(2)}) collective-permute-start(bf16[64,128]{1,0:T(8,128)(2,1)S(1)} %get-tuple-element.68), channel_id=1, source_target_pairs={{0,32},{11,33},{2,34},{3,35},{4,36},{5,37},{12,38},{7,39},{10,40},... | collective-permute-start | bytes 49160 | tf_op jit(solution)/shard_map/ppermute | solution.py:521
  48.1 7.8 %collective-permute-start.3 = (bf16[64,128]{1,0:T(8,128)(2,1)S(1)}, bf16[64,128]{1,0:T(8,128)(2,1)S(1)}, u32[]{:S(2)}, u32[]{:S(2)}) collective-permute-start(bf16[64,128]{1,0:T(8,128)(2,1)S(1)} %get-tuple-element.69), channel_id=1, source_target_pairs={{24,224},{31,231},{0,248},{7,255},{26,226},{29,229},{2,250},{5,253... | collective-permute-start | bytes 49160 | tf_op jit(solution)/shard_map/ppermute | solution.py:520
  71.2 5.7 %collective-permute-start.4 = (bf16[64,128]{1,0:T(8,128)(2,1)S(1)}, bf16[64,128]{1,0:T(8,128)(2,1)S(1)}, u32[]{:S(2)}, u32[]{:S(2)}) collective-permute-start(bf16[64,128]{1,0:T(8,128)(2,1)S(1)} %get-tuple-element.76), channel_id=1, source_target_pairs={{0,32},{11,33},{2,34},{3,35},{4,36},{5,37},{12,38},{7,39},{10,40},... | collective-permute-start | bytes 49160 | tf_op jit(solution)/shard_map/ppermute | solution.py:521
  71.3 8.1 %collective-permute-start.5 = (bf16[64,128]{1,0:T(8,128)(2,1)S(1)}, bf16[64,128]{1,0:T(8,128)(2,1)S(1)}, u32[]{:S(2)}, u32[]{:S(2)}) collective-permute-start(bf16[64,128]{1,0:T(8,128)(2,1)S(1)} %get-tuple-element.77), channel_id=1, source_target_pairs={{24,224},{31,231},{0,248},{7,255},{26,226},{29,229},{2,250},{5,253... | collective-permute-start | bytes 49160 | tf_op jit(solution)/shard_map/ppermute | solution.py:520
  97.5 5.4 %collective-permute-start.6 = (bf16[128,128]{1,0:T(8,128)(2,1)S(1)}, bf16[128,128]{1,0:T(8,128)(2,1)S(1)}, u32[]{:S(2)}, u32[]{:S(2)}) collective-permute-start(bf16[128,128]{1,0:T(8,128)(2,1)S(1)} %get-tuple-element.83), channel_id=1, source_target_pairs={{0,32},{11,33},{2,34},{3,35},{4,36},{5,37},{12,38},{7,39},{10,40},... | collective-permute-start | bytes 98312 | tf_op jit(solution)/shard_map/ppermute | solution.py:521
  97.6 8.0 %collective-permute-start.7 = (bf16[128,128]{1,0:T(8,128)(2,1)S(1)}, bf16[128,128]{1,0:T(8,128)(2,1)S(1)}, u32[]{:S(2)}, u32[]{:S(2)}) collective-permute-start(bf16[128,128]{1,0:T(8,128)(2,1)S(1)} %get-tuple-element.84), channel_id=1, source_target_pairs={{24,224},{31,231},{0,248},{7,255},{26,226},{29,229},{2,250},{5,253... | collective-permute-start | bytes 98312 | tf_op jit(solution)/shard_map/ppermute | solution.py:520
  129.2 5.6 %collective-permute-start.8 = (bf16[256,128]{1,0:T(8,128)(2,1)S(1)}, bf16[256,128]{1,0:T(8,128)(2,1)S(1)}, u32[]{:S(2)}, u32[]{:S(2)}) collective-permute-start(bf16[256,128]{1,0:T(8,128)(2,1)S(1)} %get-tuple-element.91), channel_id=1, source_target_pairs={{0,32},{11,33},{2,34},{3,35},{4,36},{5,37},{12,38},{7,39},{10,40},... | collective-permute-start | bytes 196616 | tf_op jit(solution)/shard_map/ppermute | solution.py:521
  129.3 8.4 %collective-permute-start.9 = (bf16[256,128]{1,0:T(8,128)(2,1)S(1)}, bf16[256,128]{1,0:T(8,128)(2,1)S(1)}, u32[]{:S(2)}, u32[]{:S(2)}) collective-permute-start(bf16[256,128]{1,0:T(8,128)(2,1)S(1)} %get-tuple-element.92), channel_id=1, source_target_pairs={{24,224},{31,231},{0,248},{7,255},{26,226},{29,229},{2,250},{5,253... | collective-permute-start | bytes 196616 | tf_op jit(solution)/shard_map/ppermute | solution.py:520
  162.6 6.2 %collective-permute-start.10 = (bf16[224,128]{1,0:T(8,128)(2,1)S(1)}, bf16[224,128]{1,0:T(8,128)(2,1)S(1)}, u32[]{:S(2)}, u32[]{:S(2)}) collective-permute-start(bf16[224,128]{1,0:T(8,128)(2,1)S(1)} %get-tuple-element.100), channel_id=1, source_target_pairs={{0,32},{11,33},{2,34},{3,35},{4,36},{5,37},{12,38},{7,39},{10,40},... | collective-permute-start | bytes 172040 | tf_op jit(solution)/shard_map/ppermute | solution.py:521
  162.7 8.9 %collective-permute-start.11 = (bf16[224,128]{1,0:T(8,128)(2,1)S(1)}, bf16[224,128]{1,0:T(8,128)(2,1)S(1)}, u32[]{:S(2)}, u32[]{:S(2)}) collective-permute-start(bf16[224,128]{1,0:T(8,128)(2,1)S(1)} %get-tuple-element.101), channel_id=1, source_target_pairs={{24,224},{31,231},{0,248},{7,255},{26,226},{29,229},{2,250},{5,253... | collective-permute-start | bytes 172040 | tf_op jit(solution)/shard_map/ppermute | solution.py:520

commit v4 on v3

--- a/solution.py
+++ b/solution.py
@@ -258,13 +258,13 @@
     )(codes, gathered)
 
 
-def call(kernel, shapes, *args, stage=0):
+def call(kernel, shapes, *args, name, stage=0):
     return pl.pallas_call(
         kernel,
         out_shape=tuple(jax.ShapeDtypeStruct(s, t) for s, t in shapes),
         scratch_shapes=[pltpu.VMEM((4, stage, 128), BF16)] if stage else [],
         compiler_params=LIMIT,
-    )(*[in_vmem(x) for x in args])
+    )(*(args if name == "start" else [in_vmem(x) for x in args]))
 
 
 def start_kernel(x_ref, film_ref, a_ref, slots, stage):
@@ -507,8 +507,10 @@
     films = (film_first, film_second, film_third, film_fourth, film_fifth, film_sixth)
     weights = (weight_first, weight_second, weight_third, weight_fourth, weight_fifth, weight_sixth)
     rows = [((9 * w.shape[0], w.shape[1] // 9), BF16) for w in weights]
-    film, w1, w2, w3, w4, w5, w6 = call(prepare_kernel, [((544, 2), F32)] + rows, *films, *weights)
-    made = call(matrices_kernel, [(entry[0], BF16) for entry in MATRICES.values()])
+    film, w1, w2, w3, w4, w5, w6 = call(
+        prepare_kernel, [((544, 2), F32)] + rows, *films, *weights, name="prepare"
+    )
+    made = call(matrices_kernel, [(entry[0], BF16) for entry in MATRICES.values()], name="matrices")
     we, wet, cm, c64, x32t, x32, c32, x16t, x16, r32, r64, double32, double64 = made
     near_moves = face_moves(0)
     far_moves = face_moves(1)
@@ -522,13 +524,16 @@
         (own,) = pick(codes[:8], gathered, specs, 1)
         return own, from_near, from_far
 
-    a1, f1 = call(start_kernel, [((32, 4096), BF16), ((32, 32, 128), BF16)], x, film_first, stage=32)
+    a1, f1 = call(
+        start_kernel, [((32, 4096), BF16), ((32, 32, 128), BF16)], x, film_first, name="start", stage=32
+    )
     h = exchange(f1, ((32, 64),))
     base = main_conv(a1, w1, 64)
     skip_fine, a2, f2, fine_frame = call(
         finish_1,
         [((32, 4096), BF16), ((32, 1024), BF16), ((32, 16, 128), BF16), ((32, 256), BF16)],
         base, x, *h, w1, we, cm, wet, c64, x32t, film,
+        name="finish_1",
         stage=16,
     )
     h = exchange(f2, ((32, 32),))
@@ -537,6 +542,7 @@
         finish_2,
         [((64, 1024), BF16), ((64, 256), BF16), ((32, 16, 128), BF16), ((64, 128), BF16)],
         base, *h, w2, x32, c32, x32t, x16t, film,
+        name="finish_2",
         stage=16,
     )
     h = exchange(f3, ((64, 16),))
@@ -545,6 +551,7 @@
         finish_3,
         [((128, 256), F32), ((128, 256), BF16), ((32, 32, 128), BF16)],
         base, *h, w3, x16, x16t, film,
+        name="finish_3",
         stage=32,
     )
     h = exchange(f4, ((128, 16),))
@@ -553,6 +560,7 @@
         finish_4,
         [((192, 1024), BF16), ((32, 64, 128), BF16)],
         base, third, *h, w4, x16, x16t, r32, skip_middle, middle_frame, film,
+        name="finish_4",
         stage=64,
     )
     h = exchange(f5, ((128, 16), (64, 32)))
@@ -561,6 +569,7 @@
         finish_5,
         [((96, 4096), BF16), ((32, 64, 128), BF16)],
         base, *h, w5, x32, x32t, double32, r64, skip_fine, fine_frame, film,
+        name="finish_5",
         stage=64,
     )
     h = exchange(f6, ((64, 32), (32, 64)))
@@ -569,6 +578,7 @@
         finish_6,
         [((32, 4096), BF16)],
         base, *h, w6, we, cm, double64, skip_fine, film,
+        name="finish_6",
     )
     return result[:, None, :]
 

time: 176 us -> 176 us (level)
  no operation moved by 1% of the time
where the time goes in v4:
time: 176 us; the launch traced here: 173 us
  blocking collectives  86.5 us (49%)
  starting transfers between devices  34.3 us (19%)
  Pallas kernels  26.4 us (15%)
  waiting for transfers between devices  18.8 us (11%)
  between operations  3.13 us (2%)
  local copies, waits for them, and re-layouts  2.86 us (2%)
    all_to_all x5, blocking collectives, exchange(): lax.all_to_all(slots, 'patch', split_axis=0, concat_axis=0, tiled=True)  86.5 us
    ppermute x6, starting transfers between devices, exchange(): from_far = lax.ppermute(for_far, ('face', 'patch'), far_moves)  24 us
    ppermute x6, waiting for transfers between devices, exchange(): from_far = lax.ppermute(for_far, ('face', 'patch'), far_moves)  14.2 us
    pallas_call x9, Pallas kernels, call(): pl.pallas_call(kernel, out_shape=tuple((jax.ShapeDtypeStruct(s, t) for s,...  11.3 us
    pallas_call x12, Pallas kernels, pick(): pl.pallas_call(functools.partial(pick_kernel, specs=specs), out_shape=(sh...  9.77 us
    all_to_all x1, starting transfers between devices, exchange(): lax.all_to_all(slots, 'patch', split_axis=0, concat_axis=0, tiled=True)  9.22 us
    pallas_call x6, Pallas kernels, main_conv(): pl.pallas_call(functools.partial(main_kernel, length=length), out_shape=j...  5.31 us
    all_to_all x1, waiting for transfers between devices, exchange(): lax.all_to_all(slots, 'patch', split_axis=0, concat_axis=0, tiled=True)  4.6 us
  transfers between devices with their start and end apart: 13, of which 7 were waited for; matrix products, arithmetic and copies ran while one was open for 1% of the time, Pallas kernels for 6%

profile of v4, /device:TPU:39, one launch (start us, length us, event | category | flops | bytes accessed | tf_op | source)
XLA Modules:
  0.0 173.0 jit_solution(11002197155212271491)
XLA Ops:
  0.0 0.7 copy-done.7
  0.7 0.9 copy-done
  1.6 1.6 shard_map.226
  3.2 9.2 %all-to-all-start = ((bf16[32,32,128]{2,1,0:T(8,128)(2,1)}), bf16[32,32,128]{2,1,0:T(8,128)(2,1)S(1)}, u32[]{:S(2)}, u32[]{:S(2)}) async-start(bf16[32,32,128]{2,1,0:T(8,128)(2,1)} %get-tuple-element.56), calls=%async_computation | async-start | bytes 524288 | tf_op jit(solution)/shard_map/all_to_all | solution.py:519
  12.5 0.7 fusion.19
  16.0 0.1 fusion.4
  16.2 0.1 reshape.6
  16.2 0.2 fusion.12
  16.4 0.1 copy.34
  16.5 0.1 copy.35
  16.6 0.1 slice.8.code_ref
  16.7 0.2 copy.32.refs_8_
  16.9 0.2 copy-done.3
  17.1 0.5 copy-done.4
  17.6 0.4 shard_map.227
  18.0 4.6 %all-to-all-done.gathered = bf16[32,32,128]{2,1,0:T(8,128)(2,1)S(1)} async-done(((bf16[32,32,128]{2,1,0:T(8,128)(2,1)}), bf16[32,32,128]{2,1,0:T(8,128)(2,1)S(1)}, u32[]{:S(2)}, u32[]{:S(2)}) %all-to-all-start) | async-done | bytes 262176 | tf_op jit(solution)/shard_map/all_to_all | solution.py:519
  22.6 0.8 pick.13
  23.4 0.6 collective-permute-start
  24.0 3.9 %collective-permute-start.1 = (bf16[96,128]{1,0:T(8,128)(2,1)S(1)}, bf16[96,128]{1,0:T(8,128)(2,1)S(1)}, u32[]{:S(2)}, u32[]{:S(2)}) collective-permute-start(bf16[96,128]{1,0:T(8,128)(2,1)S(1)} %get-tuple-element.58), channel_id=1, source_target_pairs={{24,224},{31,231},{0,248},{7,255},{26,226},{29,229},{2,250},{5,253... | collective-permute-start | bytes 73736 | tf_op jit(solution)/shard_map/ppermute | solution.py:522
  27.9 1.3 main_conv.6.base
  29.3 0.8 shard_map.228
  30.1 0.7 pick.12.own
  30.9 1.1 collective-permute-done.1.up
  31.9 1.3 shard_map.229
  33.2 14.0 %all_to_all.30.gathered = bf16[32,16,128]{2,1,0:T(8,128)(2,1)S(1)} all-to-all(bf16[32,16,128]{2,1,0:T(8,128)(2,1)S(1)} %get-tuple-element.67), channel_id=1, replica_groups=mesh['face'=8,'patch'=32] {'patch'}, dimensions={0} | all-to-all | bytes 262144 | tf_op jit(solution)/shard_map/all_to_all | solution.py:519
  47.2 0.8 pick.15
  48.0 0.1 collective-permute-start.2
  48.1 4.1 %collective-permute-start.3 = (bf16[64,128]{1,0:T(8,128)(2,1)S(1)}, bf16[64,128]{1,0:T(8,128)(2,1)S(1)}, u32[]{:S(2)}, u32[]{:S(2)}) collective-permute-start(bf16[64,128]{1,0:T(8,128)(2,1)S(1)} %get-tuple-element.69), channel_id=1, source_target_pairs={{24,224},{31,231},{0,248},{7,255},{26,226},{29,229},{2,250},{5,253... | collective-permute-start | bytes 49160 | tf_op jit(solution)/shard_map/ppermute | solution.py:522
  52.2 0.8 main_conv.7.base
  52.9 0.7 pick.14.own
  53.7 2.2 %collective-permute-done.3.up = bf16[64,128]{1,0:T(8,128)(2,1)S(1)} collective-permute-done((bf16[64,128]{1,0:T(8,128)(2,1)S(1)}, bf16[64,128]{1,0:T(8,128)(2,1)S(1)}, u32[]{:S(2)}, u32[]{:S(2)}) %collective-permute-start.3) | collective-permute-done | bytes 16416 | tf_op jit(solution)/shard_map/ppermute | solution.py:522
  55.9 1.2 shard_map.230
  57.1 13.2 %all_to_all.31.gathered = bf16[32,16,128]{2,1,0:T(8,128)(2,1)S(1)} all-to-all(bf16[32,16,128]{2,1,0:T(8,128)(2,1)S(1)} %get-tuple-element.75), channel_id=1, replica_groups=mesh['face'=8,'patch'=32] {'patch'}, dimensions={0} | all-to-all | bytes 262144 | tf_op jit(solution)/shard_map/all_to_all | solution.py:519
  70.4 0.8 pick.17
  71.2 0.1 collective-permute-start.4
  71.3 4.3 %collective-permute-start.5 = (bf16[64,128]{1,0:T(8,128)(2,1)S(1)}, bf16[64,128]{1,0:T(8,128)(2,1)S(1)}, u32[]{:S(2)}, u32[]{:S(2)}) collective-permute-start(bf16[64,128]{1,0:T(8,128)(2,1)S(1)} %get-tuple-element.77), channel_id=1, source_target_pairs={{24,224},{31,231},{0,248},{7,255},{26,226},{29,229},{2,250},{5,253... | collective-permute-start | bytes 49160 | tf_op jit(solution)/shard_map/ppermute | solution.py:522
  75.6 0.5 main_conv.8.base
  76.1 0.8 pick.16.own
  76.9 2.5 %collective-permute-done.5.up = bf16[64,128]{1,0:T(8,128)(2,1)S(1)} collective-permute-done((bf16[64,128]{1,0:T(8,128)(2,1)S(1)}, bf16[64,128]{1,0:T(8,128)(2,1)S(1)}, u32[]{:S(2)}, u32[]{:S(2)}) %collective-permute-start.5) | collective-permute-done | bytes 16416 | tf_op jit(solution)/shard_map/ppermute | solution.py:522
  79.4 1.1 shard_map.231
  80.5 16.2 %all_to_all.32.gathered = bf16[32,32,128]{2,1,0:T(8,128)(2,1)S(1)} all-to-all(bf16[32,32,128]{2,1,0:T(8,128)(2,1)S(1)} %get-tuple-element.82), channel_id=1, replica_groups=mesh['face'=8,'patch'=32] {'patch'}, dimensions={0} | all-to-all | bytes 524288 | tf_op jit(solution)/shard_map/all_to_all | solution.py:519
  96.7 0.8 pick.19
  97.5 0.1 collective-permute-start.6
  97.6 4.0 %collective-permute-start.7 = (bf16[128,128]{1,0:T(8,128)(2,1)S(1)}, bf16[128,128]{1,0:T(8,128)(2,1)S(1)}, u32[]{:S(2)}, u32[]{:S(2)}) collective-permute-start(bf16[128,128]{1,0:T(8,128)(2,1)S(1)} %get-tuple-element.84), channel_id=1, source_target_pairs={{24,224},{31,231},{0,248},{7,255},{26,226},{29,229},{2,250},{5,253... | collective-permute-start | bytes 98312 | tf_op jit(solution)/shard_map/ppermute | solution.py:522
  101.6 0.5 main_conv.9.base
  102.1 0.8 pick.18.own
  102.9 2.7 %collective-permute-done.7.up = bf16[128,128]{1,0:T(8,128)(2,1)S(1)} collective-permute-done((bf16[128,128]{1,0:T(8,128)(2,1)S(1)}, bf16[128,128]{1,0:T(8,128)(2,1)S(1)}, u32[]{:S(2)}, u32[]{:S(2)}) %collective-permute-start.7) | collective-permute-done | bytes 32800 | tf_op jit(solution)/shard_map/ppermute | solution.py:522
  105.6 1.4 shard_map.232
  107.0 21.2 %all_to_all.33.gathered = bf16[32,64,128]{2,1,0:T(8,128)(2,1)S(1)} all-to-all(bf16[32,64,128]{2,1,0:T(8,128)(2,1)S(1)} %get-tuple-element.90), channel_id=1, replica_groups=mesh['face'=8,'patch'=32] {'patch'}, dimensions={0} | all-to-all | bytes 1048576 | tf_op jit(solution)/shard_map/all_to_all | solution.py:519
  128.2 1.0 pick.21
  129.2 0.1 collective-permute-start.8
  129.3 3.9 %collective-permute-start.9 = (bf16[256,128]{1,0:T(8,128)(2,1)S(1)}, bf16[256,128]{1,0:T(8,128)(2,1)S(1)}, u32[]{:S(2)}, u32[]{:S(2)}) collective-permute-start(bf16[256,128]{1,0:T(8,128)(2,1)S(1)} %get-tuple-element.92), channel_id=1, source_target_pairs={{24,224},{31,231},{0,248},{7,255},{26,226},{29,229},{2,250},{5,253... | collective-permute-start | bytes 196616 | tf_op jit(solution)/shard_map/ppermute | solution.py:522
  133.2 0.8 main_conv.10.base
  134.0 0.8 pick.20.own
  134.8 2.9 %collective-permute-done.9.up = bf16[256,128]{1,0:T(8,128)(2,1)S(1)} collective-permute-done((bf16[256,128]{1,0:T(8,128)(2,1)S(1)}, bf16[256,128]{1,0:T(8,128)(2,1)S(1)}, u32[]{:S(2)}, u32[]{:S(2)}) %collective-permute-start.9) | collective-permute-done | bytes 65568 | tf_op jit(solution)/shard_map/ppermute | solution.py:522
  137.7 2.0 %shard_map.233 = (bf16[96,4096]{1,0:T(8,128)(2,1)S(1)}, bf16[32,64,128]{2,1,0:T(8,128)(2,1)S(1)}) custom-call(f32[64,1024]{1,0:T(8,128)S(1)} %main_conv.10.base, bf16[256,128]{1,0:T(8,128)(2,1)S(1)} %pick.20.own, bf16[256,128]{1,0:T(8,128)(2,1)S(1)} %collective-permute-done.8.down, bf16[256,128]{1,0:T(8,128)(2,1)S(1)} %collective-permute-done.9.up, ...), custom_call_target="tpu_custom_call" | custom-call | tf_op jit(solution)/shard_map/pallas_call | solution.py:262
  139.8 21.9 %all_to_all.34.gathered = bf16[32,64,128]{2,1,0:T(8,128)(2,1)S(1)} all-to-all(bf16[32,64,128]{2,1,0:T(8,128)(2,1)S(1)} %get-tuple-element.99), channel_id=1, replica_groups=mesh['face'=8,'patch'=32] {'patch'}, dimensions={0} | all-to-all | bytes 1048576 | tf_op jit(solution)/shard_map/all_to_all | solution.py:519
  161.6 0.9 pick.23
  162.6 0.1 collective-permute-start.10
  162.7 3.9 %collective-permute-start.11 = (bf16[224,128]{1,0:T(8,128)(2,1)S(1)}, bf16[224,128]{1,0:T(8,128)(2,1)S(1)}, u32[]{:S(2)}, u32[]{:S(2)}) collective-permute-start(bf16[224,128]{1,0:T(8,128)(2,1)S(1)} %get-tuple-element.101), channel_id=1, source_target_pairs={{24,224},{31,231},{0,248},{7,255},{26,226},{29,229},{2,250},{5,253... | collective-permute-start | bytes 172040 | tf_op jit(solution)/shard_map/ppermute | solution.py:522
  166.6 1.4 main_conv.11.base
  168.0 0.8 pick.22.own
  168.8 2.8 %collective-permute-done.11.up = bf16[224,128]{1,0:T(8,128)(2,1)S(1)} collective-permute-done((bf16[224,128]{1,0:T(8,128)(2,1)S(1)}, bf16[224,128]{1,0:T(8,128)(2,1)S(1)}, u32[]{:S(2)}, u32[]{:S(2)}) %collective-permute-start.11) | collective-permute-done | bytes 57376 | tf_op jit(solution)/shard_map/ppermute | solution.py:522
  171.5 1.5 shard_map.234
  (52 shorter events, 0.2 us)
Async XLA Ops:
  0.0 0.7 copy-start.7
  0.7 0.9 copy-start
  3.2 9.3 %copy-start.22 = (s32[32]{0:T(128)S(1)}, s32[32]{0:T(128)}, u32[]{:S(2)}) copy-start(s32[32]{0:T(128)} %constant.166.clone) | copy-start | bytes 388
  3.2 9.3 %copy-start.23 = (s32[32]{0:T(128)S(1)}, s32[32]{0:T(128)}, u32[]{:S(2)}) copy-start(s32[32]{0:T(128)} %constant.165.clone) | copy-start | bytes 388
  3.2 12.7 %copy-start.16 = (s32[8,32,8]{1,2,0:T(8,128)S(1)}, s32[8,32,8]{1,2,0:T(8,128)}, u32[]{:S(2)}) copy-start(s32[8,32,8]{1,2,0:T(8,128)} %param.39) | copy-start | bytes 24580
  3.2 13.5 %copy-start.13 = (bf16[128,576]{0,1:T(8,128)(2,1)S(1)}, bf16[128,576]{0,1:T(8,128)(2,1)}, u32[]{:S(2)}) copy-start(bf16[128,576]{0,1:T(8,128)(2,1)} %param.30) | copy-start | bytes 442372
  3.2 19.4 %all-to-all-start = ((bf16[32,32,128]{2,1,0:T(8,128)(2,1)}), bf16[32,32,128]{2,1,0:T(8,128)(2,1)S(1)}, u32[]{:S(2)}, u32[]{:S(2)}) async-start(bf16[32,32,128]{2,1,0:T(8,128)(2,1)} %get-tuple-element.56), calls=%async_computation | async-start | bytes 524288 | tf_op jit(solution)/shard_map/all_to_all | solution.py:519
  12.4 3.5 %copy-start.15 = (s32[8,32,8]{1,2,0:T(8,128)S(1)}, s32[8,32,8]{1,2,0:T(8,128)}, u32[]{:S(2)}) copy-start(s32[8,32,8]{1,2,0:T(8,128)} %param.37) | copy-start | bytes 24580
  13.2 2.8 %copy-start.19 = (s32[8]{0:T(128)S(1)}, s32[8]{0:T(128)}, u32[]{:S(2)}) copy-start(s32[8]{0:T(128)} %constant.162.clone) | copy-start | bytes 100
  13.2 2.8 %copy-start.20 = (s32[8]{0:T(128)S(1)}, s32[8]{0:T(128)}, u32[]{:S(2)}) copy-start(s32[8]{0:T(128)} %constant.161.clone) | copy-start | bytes 100
  13.2 2.8 %copy-start.21 = (s32[8]{0:T(128)S(1)}, s32[8]{0:T(128)}, u32[]{:S(2)}) copy-start(s32[8]{0:T(128)} %constant.160.clone) | copy-start | bytes 100
  13.2 2.8 %copy-start.14 = (s32[8,32,8]{1,2,0:T(8,128)S(1)}, s32[8,32,8]{1,2,0:T(8,128)}, u32[]{:S(2)}) copy-start(s32[8,32,8]{1,2,0:T(8,128)} %param.38) | copy-start | bytes 24580
  13.2 2.8 %copy-start.18 = (s32[8]{0:T(128)S(1)}, s32[8]{0:T(128)}, u32[]{:S(2)}) copy-start(s32[8]{0:T(128)} %constant.163.clone) | copy-start | bytes 100
  13.2 3.7 %copy-start.6 = (bf16[32,288]{1,0:T(8,128)(2,1)S(1)}, bf16[32,288]{1,0:T(8,128)(2,1)}, u32[]{:S(2)}) copy-start(bf16[32,288]{1,0:T(8,128)(2,1)} %refs_6_.1) | copy-start | bytes 55300
  13.2 3.7 %copy-start.8 = (f32[2,192]{1,0:T(2,128)S(1)}, f32[2,192]{1,0:T(2,128)}, u32[]{:S(2)}) copy-start(f32[2,192]{1,0:T(2,128)} %refs_4_.1) | copy-start | bytes 4612
  13.2 3.7 %copy-start.9 = (f32[2,32]{1,0:T(2,128)S(1)}, f32[2,32]{1,0:T(2,128)}, u32[]{:S(2)}) copy-start(f32[2,32]{1,0:T(2,128)} %refs_1_.1) | copy-start | bytes 772
  13.2 3.7 %copy-start.10 = (f32[2,64]{1,0:T(2,128)S(1)}, f32[2,64]{1,0:T(2,128)}, u32[]{:S(2)}) copy-start(f32[2,64]{1,0:T(2,128)} %refs_2_.1) | copy-start | bytes 1540
  13.2 3.7 %copy-start.11 = (f32[2,128]{1,0:T(2,128)S(1)}, f32[2,128]{1,0:T(2,128)}, u32[]{:S(2)}) copy-start(f32[2,128]{1,0:T(2,128)} %refs_3_.1) | copy-start | bytes 3076
  13.2 3.7 %copy-start.12 = (f32[2,96]{1,0:T(2,128)S(1)}, f32[2,96]{1,0:T(2,128)}, u32[]{:S(2)}) copy-start(f32[2,96]{1,0:T(2,128)} %refs_5_.1) | copy-start | bytes 2308
  13.3 2.7 %copy-start.17 = (pred[8]{0:T(512)(128)(4,1)S(1)}, pred[8]{0:T(512)(128)(4,1)}, u32[]{:S(2)}) copy-start(pred[8]{0:T(512)(128)(4,1)} %constant.164.clone) | copy-start | bytes 28
  14.5 2.4 %copy-start.5 = (bf16[64,288]{1,0:T(8,128)(2,1)S(1)}, bf16[64,288]{1,0:T(8,128)(2,1)}, u32[]{:S(2)}) copy-start(bf16[64,288]{1,0:T(8,128)(2,1)} %refs_7_.1) | copy-start | bytes 110596
  16.0 1.0 copy-start.2
  16.1 1.0 copy-start.3
  16.7 0.9 copy-start.4
  23.4 7.5 %collective-permute-start = (bf16[96,128]{1,0:T(8,128)(2,1)S(1)}, bf16[96,128]{1,0:T(8,128)(2,1)S(1)}, u32[]{:S(2)}, u32[]{:S(2)}) collective-permute-start(bf16[96,128]{1,0:T(8,128)(2,1)S(1)} %get-tuple-element.57), channel_id=1, source_target_pairs={{0,32},{11,33},{2,34},{3,35},{4,36},{5,37},{12,38},{7,39},{10,40},... | collective-permute-start | bytes 73736 | tf_op jit(solution)/shard_map/ppermute | solution.py:523
  24.0 7.9 %collective-permute-start.1 = (bf16[96,128]{1,0:T(8,128)(2,1)S(1)}, bf16[96,128]{1,0:T(8,128)(2,1)S(1)}, u32[]{:S(2)}, u32[]{:S(2)}) collective-permute-start(bf16[96,128]{1,0:T(8,128)(2,1)S(1)} %get-tuple-element.58), channel_id=1, source_target_pairs={{24,224},{31,231},{0,248},{7,255},{26,226},{29,229},{2,250},{5,253... | collective-permute-start | bytes 73736 | tf_op jit(solution)/shard_map/ppermute | solution.py:522
  29.2 2.7 %copy-start.1 = (bf16[32,1,4096]{2,0,1:T(8,128)(2,1)S(1)}, bf16[32,1,4096]{2,0,1:T(8,128)(2,1)}, u32[]{:S(2)}) copy-start(bf16[32,1,4096]{2,0,1:T(8,128)(2,1)} %param.24) | copy-start | bytes 786436
  48.0 5.7 %collective-permute-start.2 = (bf16[64,128]{1,0:T(8,128)(2,1)S(1)}, bf16[64,128]{1,0:T(8,128)(2,1)S(1)}, u32[]{:S(2)}, u32[]{:S(2)}) collective-permute-start(bf16[64,128]{1,0:T(8,128)(2,1)S(1)} %get-tuple-element.68), channel_id=1, source_target_pairs={{0,32},{11,33},{2,34},{3,35},{4,36},{5,37},{12,38},{7,39},{10,40},... | collective-permute-start | bytes 49160 | tf_op jit(solution)/shard_map/ppermute | solution.py:523
  48.1 7.8 %collective-permute-start.3 = (bf16[64,128]{1,0:T(8,128)(2,1)S(1)}, bf16[64,128]{1,0:T(8,128)(2,1)S(1)}, u32[]{:S(2)}, u32[]{:S(2)}) collective-permute-start(bf16[64,128]{1,0:T(8,128)(2,1)S(1)} %get-tuple-element.69), channel_id=1, source_target_pairs={{24,224},{31,231},{0,248},{7,255},{26,226},{29,229},{2,250},{5,253... | collective-permute-start | bytes 49160 | tf_op jit(solution)/shard_map/ppermute | solution.py:522
  71.2 5.7 %collective-permute-start.4 = (bf16[64,128]{1,0:T(8,128)(2,1)S(1)}, bf16[64,128]{1,0:T(8,128)(2,1)S(1)}, u32[]{:S(2)}, u32[]{:S(2)}) collective-permute-start(bf16[64,128]{1,0:T(8,128)(2,1)S(1)} %get-tuple-element.76), channel_id=1, source_target_pairs={{0,32},{11,33},{2,34},{3,35},{4,36},{5,37},{12,38},{7,39},{10,40},... | collective-permute-start | bytes 49160 | tf_op jit(solution)/shard_map/ppermute | solution.py:523
  71.3 8.1 %collective-permute-start.5 = (bf16[64,128]{1,0:T(8,128)(2,1)S(1)}, bf16[64,128]{1,0:T(8,128)(2,1)S(1)}, u32[]{:S(2)}, u32[]{:S(2)}) collective-permute-start(bf16[64,128]{1,0:T(8,128)(2,1)S(1)} %get-tuple-element.77), channel_id=1, source_target_pairs={{24,224},{31,231},{0,248},{7,255},{26,226},{29,229},{2,250},{5,253... | collective-permute-start | bytes 49160 | tf_op jit(solution)/shard_map/ppermute | solution.py:522
  97.5 5.4 %collective-permute-start.6 = (bf16[128,128]{1,0:T(8,128)(2,1)S(1)}, bf16[128,128]{1,0:T(8,128)(2,1)S(1)}, u32[]{:S(2)}, u32[]{:S(2)}) collective-permute-start(bf16[128,128]{1,0:T(8,128)(2,1)S(1)} %get-tuple-element.83), channel_id=1, source_target_pairs={{0,32},{11,33},{2,34},{3,35},{4,36},{5,37},{12,38},{7,39},{10,40},... | collective-permute-start | bytes 98312 | tf_op jit(solution)/shard_map/ppermute | solution.py:523
  97.6 8.0 %collective-permute-start.7 = (bf16[128,128]{1,0:T(8,128)(2,1)S(1)}, bf16[128,128]{1,0:T(8,128)(2,1)S(1)}, u32[]{:S(2)}, u32[]{:S(2)}) collective-permute-start(bf16[128,128]{1,0:T(8,128)(2,1)S(1)} %get-tuple-element.84), channel_id=1, source_target_pairs={{24,224},{31,231},{0,248},{7,255},{26,226},{29,229},{2,250},{5,253... | collective-permute-start | bytes 98312 | tf_op jit(solution)/shard_map/ppermute | solution.py:522
  129.2 5.6 %collective-permute-start.8 = (bf16[256,128]{1,0:T(8,128)(2,1)S(1)}, bf16[256,128]{1,0:T(8,128)(2,1)S(1)}, u32[]{:S(2)}, u32[]{:S(2)}) collective-permute-start(bf16[256,128]{1,0:T(8,128)(2,1)S(1)} %get-tuple-element.91), channel_id=1, source_target_pairs={{0,32},{11,33},{2,34},{3,35},{4,36},{5,37},{12,38},{7,39},{10,40},... | collective-permute-start | bytes 196616 | tf_op jit(solution)/shard_map/ppermute | solution.py:523
  129.3 8.4 %collective-permute-start.9 = (bf16[256,128]{1,0:T(8,128)(2,1)S(1)}, bf16[256,128]{1,0:T(8,128)(2,1)S(1)}, u32[]{:S(2)}, u32[]{:S(2)}) collective-permute-start(bf16[256,128]{1,0:T(8,128)(2,1)S(1)} %get-tuple-element.92), channel_id=1, source_target_pairs={{24,224},{31,231},{0,248},{7,255},{26,226},{29,229},{2,250},{5,253... | collective-permute-start | bytes 196616 | tf_op jit(solution)/shard_map/ppermute | solution.py:522
  162.6 6.2 %collective-permute-start.10 = (bf16[224,128]{1,0:T(8,128)(2,1)S(1)}, bf16[224,128]{1,0:T(8,128)(2,1)S(1)}, u32[]{:S(2)}, u32[]{:S(2)}) collective-permute-start(bf16[224,128]{1,0:T(8,128)(2,1)S(1)} %get-tuple-element.100), channel_id=1, source_target_pairs={{0,32},{11,33},{2,34},{3,35},{4,36},{5,37},{12,38},{7,39},{10,40},... | collective-permute-start | bytes 172040 | tf_op jit(solution)/shard_map/ppermute | solution.py:523
  162.7 8.9 %collective-permute-start.11 = (bf16[224,128]{1,0:T(8,128)(2,1)S(1)}, bf16[224,128]{1,0:T(8,128)(2,1)S(1)}, u32[]{:S(2)}, u32[]{:S(2)}) collective-permute-start(bf16[224,128]{1,0:T(8,128)(2,1)S(1)} %get-tuple-element.101), channel_id=1, source_target_pairs={{24,224},{31,231},{0,248},{7,255},{26,226},{29,229},{2,250},{5,253... | collective-permute-start | bytes 172040 | tf_op jit(solution)/shard_map/ppermute | solution.py:522
